TPU v7x, 32 devices: a whole 2x2x4 slice. The times are simulated.
32 devices in a mesh: group: 4 (over y, core), peer: 8 (over z, x).
Axes of the slice: x: 2, y: 2, z: 4, core: 2. Of those that a mesh axis runs over, the one named last changes fastest.
Arguments:
- states: float32 [41, 1048576], P(None, ('group', 'peer')), may hold values from -6 to 6
- block_part: int32 [8192], P(('group', 'peer')), may hold values from 0 to 31, as said below
- tile_perm: int32 [8192, 128], P(('group', 'peer')), may hold values from 0 to 127, each once within a row
- half_volt: float32 [40], replicated, may hold values from -4 to 4
- steepness: float32 [40], replicated, may hold values from 0.5 to 4
- gate_rate: float32 [40], replicated, may hold values from 0.1 to 1
- conductance: float32 [40], replicated, may hold values from 0.005 to 0.08
- reversal: float32 [40], replicated, may hold values from -6 to 6
Outputs:
- regrouped: float32 [41, 1048576], P(None, ('group', 'peer'))
Inputs may be any that keep to these rules, and one draw needn't show every extreme that they name: `block_part`: every partition holds exactly 256 blocks. Within each slab of 256 consecutive global blocks no partition holds more than 16 blocks; every slab has exactly 16 blocks of some partition, and every partition has exactly 16 blocks in some slab.
All inputs are finite; a program needn't handle non-finite values.
Results may differ from a plain program's by a relative error of at most 0.0001.
Values sent between devices are 32-bit elements; how exact they have to be, the bound alone decides.
No kernel may reach another device: no remote copies, remote signals or barrier semaphores. Data moves between devices by JAX's collectives and lax.ppermute only.
A program may use at most 192 MiB of HBM per device.

v0:
```python
import functools

import jax
import jax.numpy as jnp
from jax import lax
from jax.experimental import pallas as pl
from jax.experimental.pallas import tpu as pltpu
from jax.sharding import PartitionSpec as P


time_step = 0.25
sublanes = 8
both = ("group", "peer")
smem_full = pl.BlockSpec(memory_space=pltpu.SMEM)
vmem_full = pl.BlockSpec(memory_space=pltpu.VMEM)
any_full = pl.BlockSpec(memory_space=pl.ANY)


def round_up(value, step):
    return -(-value // step) * step


class Plan:
    def __init__(self, rows, blocks, width):
        self.rows, self.blocks, self.width = rows, blocks, width
        self.peers = lax.axis_size("peer")
        self.devices = lax.axis_size("group") * self.peers
        self.near = self.peers // 2
        self.mates = self.devices // 2
        most = 2 * blocks // self.devices
        self.slots = max(most // 2, 1)
        self.over = most - self.slots
        self.full = rows // sublanes * sublanes
        self.extra = rows - self.full
        self.direct_rows = round_up(rows * self.slots, sublanes)
        self.relay_rows = round_up(rows * 2 * self.over, sublanes)
        self.worst = self.mates * self.over

    def half(self, device):
        return (device % self.peers) // self.near

    def mate(self, device):
        return device // self.peers * self.near + device % self.near

    def device(self, mate, half):
        return mate // self.near * self.peers + half * self.near + mate % self.near

    def partner(self, device):
        flip = 1 - 2 * self.half(device)
        return device + flip * self.near

    def me(self):
        return lax.axis_index("group") * self.peers + lax.axis_index("peer")


def advance_kernel(params_ref, states_ref, out_ref, *, step):
    rows = states_ref.shape[0]
    row = lax.broadcasted_iota(jnp.int32, (rows, step), 0)

    def one(i, carry):
        cols = pl.ds(pl.multiple_of(i * step, step), step)
        vals = states_ref[:, cols]
        voltage = vals[0:1]
        relax = 1.5 + 0.5 * jnp.tanh(0.5 * voltage)
        steady = 0.5 + 0.5 * jnp.tanh((voltage - params_ref[0]) * params_ref[1])
        damping = jnp.exp(params_ref[2] * relax)
        gates = steady + (vals - steady) * damping
        current = jnp.sum(
            params_ref[3] * gates * (voltage - params_ref[4]), axis=0, keepdims=True
        )
        out_ref[:, cols] = jnp.where(row == 0, voltage - time_step * current, gates)
        return carry

    lax.fori_loop(0, states_ref.shape[1] // step, one, 0)


def advance(states, half_volt, steepness, gate_rate, conductance, reversal):
    rows, nodes = states.shape
    step = 128
    params = jnp.stack([half_volt, 0.5 * steepness, -gate_rate, conductance, reversal])
    params = jnp.pad(params, ((0, 0), (1, 0)))
    params = jnp.broadcast_to(params[:, :, None], params.shape + (step,))
    block = fitting(nodes, 4096)
    return pl.pallas_call(
        functools.partial(advance_kernel, step=step),
        grid=(nodes // block,),
        in_specs=[
            pl.BlockSpec(params.shape, lambda i: (0, 0, 0)),
            pl.BlockSpec((rows, block), lambda i: (0, i)),
        ],
        out_specs=pl.BlockSpec((rows, block), lambda i: (0, i)),
        out_shape=jax.ShapeDtypeStruct(states.shape, states.dtype),
        cost_estimate=pl.CostEstimate(
            flops=40 * rows * nodes,
            bytes_accessed=8 * rows * nodes,
            transcendentals=3 * rows * nodes,
        ),
        name="advance",
    )(params, states)


def fitting(total, most):
    size = min(total, most)
    while total % size:
        size -= 128
    return size


def put_block(plan, adv_ref, block, put, base, tail):
    cols = pl.ds(pl.multiple_of(block * plan.width, plan.width), plan.width)
    put(base, plan.full, adv_ref[0 : plan.full, cols])
    for e in range(plan.extra):
        put(tail(e), 1, adv_ref[plan.full + e : plan.full + e + 1, cols])


def cross_kernel(table_ref, adv_ref, cross_ref, *, plan, room):
    me = plan.me()
    mine = plan.half(me)

    def one(s, carry):
        start, at = carry
        count = table_ref[s * plan.devices + me]
        far = (plan.half(s) != mine).astype(jnp.int32)
        more = jnp.maximum(count - plan.slots, 0) * far

        def spill(k, carry):
            slot = jnp.minimum(at + k, room - 1)

            def put(base, size, vals):
                if size == plan.full:
                    base = pl.multiple_of(base, sublanes)
                cross_ref[pl.ds(base, size), :] = vals

            put_block(
                plan,
                adv_ref,
                start + plan.slots + k,
                put,
                slot * plan.full,
                lambda e: room * plan.full + e * room + slot,
            )
            return carry

        lax.fori_loop(0, more, spill, 0)
        return start + count, at + more

    lax.fori_loop(0, plan.devices, one, (0, 0))


def pack_cross(plan, table, adv, room):
    rows = round_up(room * plan.rows, sublanes)
    return pl.pallas_call(
        functools.partial(cross_kernel, plan=plan, room=room),
        in_specs=[smem_full, vmem_full],
        out_specs=vmem_full,
        out_shape=jax.ShapeDtypeStruct((rows, plan.width), adv.dtype),
        name="pack_cross",
    )(table, adv)


def direct_kernel(table_ref, adv_ref, direct_ref, start_ref, *, plan):
    me = plan.me()
    per_step = direct_ref.shape[0]
    first = pl.program_id(0) * per_step

    @pl.when(first == 0)
    def _():
        start_ref[0] = 0

    start = start_ref[0]
    for d in range(per_step):

        def put(base, size, vals):
            direct_ref[d, base : base + size, :] = vals

        for k in range(plan.slots):
            put_block(
                plan,
                adv_ref,
                jnp.minimum(start + k, plan.blocks - 1),
                put,
                k * plan.full,
                lambda e: plan.slots * plan.full + e * plan.slots + k,
            )
        start = start + table_ref[(first + d) * plan.devices + me]
    start_ref[0] = start


def pack_direct(plan, table, adv):
    per_step = fitting_blocks(plan.devices, 4)
    return pl.pallas_call(
        functools.partial(direct_kernel, plan=plan),
        grid_spec=pltpu.PrefetchScalarGridSpec(
            num_scalar_prefetch=1,
            grid=(plan.devices // per_step,),
            in_specs=[pl.BlockSpec(adv.shape, lambda i, *_: (0, 0))],
            out_specs=pl.BlockSpec(
                (per_step, plan.direct_rows, plan.width), lambda i, *_: (i, 0, 0)
            ),
            scratch_shapes=[pltpu.SMEM((1,), jnp.int32)],
        ),
        out_shape=jax.ShapeDtypeStruct(
            (plan.devices, plan.direct_rows, plan.width), adv.dtype
        ),
        name="pack_direct",
    )(table, adv)


def relay_kernel(table_ref, adv_ref, cross_ref, *refs, plan, room):
    outs, (own_ref, far_ref) = refs[: plan.mates], refs[plan.mates :]
    me = plan.me()
    mine = plan.half(me)
    other = plan.partner(me)

    def scan(s, carry):
        start, at = carry
        own_ref[s] = start
        far_ref[s] = at
        near = (plan.half(s) == mine).astype(jnp.int32)
        more = jnp.maximum(table_ref[s * plan.devices + other] - plan.slots, 0)
        return start + table_ref[s * plan.devices + me], at + more * near

    lax.fori_loop(0, plan.devices, scan, (0, 0))
    here = plan.mate(me)
    slots = 2 * plan.over
    for d, out_ref in enumerate(outs):
        s = plan.device(here ^ d, mine)
        start = own_ref[s] + plan.slots
        at = far_ref[s]

        def put(base, size, vals):
            out_ref[base : base + size, :] = vals

        for k in range(plan.over):
            put_block(
                plan,
                adv_ref,
                jnp.minimum(start + k, plan.blocks - 1),
                put,
                k * plan.full,
                lambda e: slots * plan.full + e * slots + k,
            )
        for k in range(plan.over):
            slot = jnp.minimum(at + k, room - 1)
            to = plan.over + k
            out_ref[to * plan.full : (to + 1) * plan.full, :] = cross_ref[
                pl.ds(pl.multiple_of(slot * plan.full, plan.full), plan.full), :
            ]
            for e in range(plan.extra):
                row = slots * plan.full + e * slots + to
                out_ref[row : row + 1, :] = cross_ref[
                    pl.ds(room * plan.full + e * room + slot, 1), :
                ]


def relay(plan, table, adv, crossed, room):
    piece = jax.ShapeDtypeStruct((plan.relay_rows, plan.width), adv.dtype)
    return pl.pallas_call(
        functools.partial(relay_kernel, plan=plan, room=room),
        in_specs=[smem_full, vmem_full, vmem_full],
        out_specs=[vmem_full] * plan.mates,
        out_shape=[piece] * plan.mates,
        scratch_shapes=[
            pltpu.SMEM((plan.devices,), jnp.int32),
            pltpu.SMEM((plan.devices,), jnp.int32),
        ],
        name="relay",
    )(table, adv, crossed)


def permuted(vals, lanes):
    return jnp.take_along_axis(vals, lanes, axis=1, mode="promise_in_bounds")


def unpack_kernel(base_ref, tail_ref, step_ref, perm_ref, direct_ref, *refs, plan):
    pieces = refs[: plan.mates]
    out_ref, got_ref, last_ref, sem = refs[plan.mates :]
    per_step, width = perm_ref.shape
    first = pl.program_id(0) * per_step

    @pl.when(first == 0)
    def _():
        direct = plan.devices * plan.direct_rows
        copies = [
            pltpu.make_async_copy(direct_ref, got_ref.at[pl.ds(0, direct)], sem.at[0])
        ]
        for d, piece_ref in enumerate(pieces):
            rows = pl.ds(direct + d * plan.relay_rows, plan.relay_rows)
            copies.append(
                pltpu.make_async_copy(piece_ref, got_ref.at[rows], sem.at[1 + d])
            )
        for copy in copies:
            copy.start()
        for copy in copies:
            copy.wait()

    for i in range(per_step):
        base = pl.multiple_of(base_ref[first + i], sublanes)
        tail = tail_ref[first + i]
        stride = step_ref[first + i]
        lanes = jnp.broadcast_to(perm_ref[i : i + 1, :], (plan.full, width))
        vals = got_ref[pl.ds(base, plan.full), :]
        out_ref[0 : plan.full, i * width : (i + 1) * width] = permuted(vals, lanes)
        for e in range(plan.extra):
            last_ref[e, i : i + 1, :] = got_ref[pl.ds(tail + e * stride, 1), :]
    for e in range(plan.extra):
        last = permuted(last_ref[e], perm_ref[...])
        for i in range(per_step):
            cols = slice(i * width, (i + 1) * width)
            out_ref[plan.full + e : plan.full + e + 1, cols] = last[i : i + 1, :]


def unpack(plan, places, perm, direct, pieces):
    per_step = fitting_blocks(plan.blocks, 16)
    total = plan.devices * plan.direct_rows + plan.mates * plan.relay_rows
    return pl.pallas_call(
        functools.partial(unpack_kernel, plan=plan),
        grid_spec=pltpu.PrefetchScalarGridSpec(
            num_scalar_prefetch=3,
            grid=(plan.blocks // per_step,),
            in_specs=[pl.BlockSpec((per_step, plan.width), lambda i, *_: (i, 0))]
            + [any_full] * (1 + plan.mates),
            out_specs=pl.BlockSpec((plan.rows, per_step * plan.width), lambda i, *_: (0, i)),
            scratch_shapes=[
                pltpu.VMEM((total, plan.width), direct.dtype),
                pltpu.VMEM((max(plan.extra, 1), per_step, plan.width), direct.dtype),
                pltpu.SemaphoreType.DMA((1 + plan.mates,)),
            ],
        ),
        out_shape=jax.ShapeDtypeStruct((plan.rows, plan.blocks * plan.width), direct.dtype),
        name="unpack",
    )(*places, perm, direct, *pieces)


def fitting_blocks(total, most):
    size = min(total, most)
    while total % size:
        size -= 1
    return size


def find_places(plan, block_part, me):
    same = block_part[:, None] == block_part[None, :]
    position = jnp.arange(plan.blocks, dtype=jnp.int32)
    ahead = position[None, :] < position[:, None]
    rank = jnp.sum((same & ahead).astype(jnp.int32), axis=1, dtype=jnp.int32)
    direct = rank < plan.slots
    home = plan.half(block_part) == plan.half(me)
    piece = plan.mate(block_part) ^ plan.mate(me)
    origin = plan.devices * plan.direct_rows + piece * plan.relay_rows
    slot = rank - plan.slots + jnp.where(home, 0, plan.over)
    slots = 2 * plan.over
    base = jnp.where(
        direct, block_part * plan.direct_rows + rank * plan.full, origin + slot * plan.full
    )
    tail = jnp.where(
        direct,
        block_part * plan.direct_rows + plan.slots * plan.full + rank,
        origin + slots * plan.full + slot,
    )
    return base, tail, jnp.where(direct, plan.slots, slots)


def exchange(plan, room, table, adv, places, tile_perm):
    over = range(plan.devices)
    cross = pack_cross(plan, table, adv, room)
    crossed = lax.ppermute(cross, both, [(i, plan.partner(i)) for i in over])
    direct = pack_direct(plan, table, adv)
    arrived = lax.all_to_all(direct, both, split_axis=0, concat_axis=0, tiled=True)
    pieces = list(relay(plan, table, adv, crossed, room))
    for d in range(1, plan.mates):
        pairs = [(i, plan.device(plan.mate(i) ^ d, plan.half(i))) for i in over]
        pieces[d] = lax.ppermute(pieces[d], both, pairs)
    flat = arrived.reshape(plan.devices * plan.direct_rows, plan.width)
    return unpack(plan, places, tile_perm, flat, pieces)


def on_device(
    states, block_part, tile_perm, half_volt, steepness, gate_rate, conductance, reversal
):
    blocks, width = tile_perm.shape
    plan = Plan(states.shape[0], blocks, width)
    devices = plan.devices
    me = plan.me()
    ids = jnp.arange(devices, dtype=jnp.int32)
    onehot = (block_part[:, None] == ids[None, :]).astype(jnp.int32)
    counts = jnp.sum(onehot, axis=0, dtype=jnp.int32)
    told = jnp.broadcast_to(counts[None, :], (devices, devices))
    table = lax.all_to_all(told, both, split_axis=0, concat_axis=0, tiled=True)
    adv = advance(states, half_volt, steepness, gate_rate, conductance, reversal)
    far = plan.half(ids)[:, None] != plan.half(ids)[None, :]
    spilled = jnp.sum(jnp.where(far, jnp.maximum(table - plan.slots, 0), 0), axis=0)
    spilled = jnp.max(spilled)
    places = find_places(plan, block_part, me)
    rooms = [plan.worst * 3 // 8, plan.worst // 2, plan.worst]
    rooms = [round_up(room, sublanes) for room in rooms]
    choice = sum((spilled > room).astype(jnp.int32) for room in rooms[:-1])
    return lax.switch(
        choice,
        [functools.partial(exchange, plan, room) for room in rooms],
        table.reshape(-1),
        adv,
        places,
        tile_perm,
    )


def solution(mesh):
    return jax.shard_map(
        on_device,
        mesh=mesh,
        in_specs=(
            P(None, both),
            P(both),
            P(both, None),
            P(),
            P(),
            P(),
            P(),
            P(),
        ),
        out_specs=P(None, both),
        check_vma=False,
    )
```

profile of v0, /device:TPU:25, one launch (start us, length us, event | category | flops | bytes accessed | tf_op | source)
XLA Modules:
  0.0 320.2 jit_solution(12575743254306539355)
XLA Ops:
  1.4 6.2 %all-to-all-start.3 = ((s32[32,1,32]{2,1,0:T(1,128)}), s32[32,1,32]{2,1,0:T(1,128)S(1)}, u32[]{:S(2)}, u32[]{:S(2)}) async-start(s32[32,1,32]{2,1,0:T(1,128)} %broadcast_in_dim.11), calls=%async_computation.3 | async-start | bytes 32768 | tf_op jit(solution)/shard_map/all_to_all | solution.py:389
  12.1 13.1 %advance.1 = f32[41,32768]{1,0:T(8,128)} custom-call(f32[5,41,128]{2,1,0:T(8,128)} %broadcast_in_dim.12.params_ref, f32[41,32768]{1,0:T(8,128)} %states_ref.1), custom_call_target="tpu_custom_call" | custom-call | flops 53739520 | bytes 10747904 | tf_op jit(solution)/shard_map/advance/pallas_call | solution.py:84
  27.3 292.9 %conditional.1 = (f32[41,32768]{1,0:T(8,128)}) conditional(s32[]{:T(128)} %clamp.3, (s32[32,1,32]{2,1,0:T(1,128)S(1)}, f32[41,32768]{1,0:T(8,128)}, s32[256]{0:T(256)S(1)}, s32[256]{0:T(256)S(1)}, (), /*index=5*/s32[256,128]{1,0:T(8,128)S(1)}, s32[256]{0:T(256)S(1)}, s32[256]{0:T(256)S(1)}, (), (), /*index=10*/s32[256]{0:T(256)S(1)}, (), ...), branch_computations={%region_4.5_spmd, %region_5.6_spmd, %region_6.7_spmd} | conditional | flops 10516 | bytes 71256496 | solution.py:398
  29.2 7.5 %pack_direct.4 = f32[32,328,128]{2,1,0:T(8,128)} custom-call(s32[1024]{0:T(1024)} %reshape.76.table_ref, f32[41,32768]{1,0:T(8,128)} %get-tuple-element.72.adv_ref), custom_call_target="tpu_custom_call" | custom-call | tf_op jit(solution)/shard_map/cond/branch_1_fun/pack_direct/pallas_call | solution.py:191
  36.8 5.9 %all-to-all-start.1 = ((f32[32,328,128]{2,1,0:T(8,128)}), f32[32,328,128]{2,1,0:T(8,128)}, u32[]{:S(2)}, u32[]{:S(2)}) async-start(f32[32,328,128]{2,1,0:T(8,128)} %pack_direct.4), calls=%async_computation.1 | async-start | bytes 10747904 | tf_op jit(solution)/shard_map/cond/branch_1_fun/all_to_all | solution.py:369
  42.6 5.1 %pack_cross.4 = f32[2624,128]{1,0:T(8,128)} custom-call(s32[1024]{0:T(1024)} %reshape.76.table_ref, f32[41,32768]{1,0:T(8,128)} %get-tuple-element.72.adv_ref), custom_call_target="tpu_custom_call" | custom-call | tf_op jit(solution)/shard_map/cond/branch_1_fun/pack_cross/pallas_call | solution.py:152
  47.9 170.0 %collective-permute-done.16.cross_ref = f32[2624,128]{1,0:T(8,128)S(1)} collective-permute-done((f32[2624,128]{1,0:T(8,128)}, f32[2624,128]{1,0:T(8,128)S(1)}, u32[]{:S(2)}, u32[]{:S(2)}) %collective-permute-start.16) | collective-permute-done | bytes 1343520 | tf_op jit(solution)/shard_map/cond/branch_1_fun/ppermute | solution.py:367
  219.0 6.7 %relay.4 = (f32[656,128]{1,0:T(8,128)}, f32[656,128]{1,0:T(8,128)}, f32[656,128]{1,0:T(8,128)}, f32[656,128]{1,0:T(8,128)}, f32[656,128]{1,0:T(8,128)}, /*index=...) custom-call(s32[1024]{0:T(1024)} %reshape.76.table_ref, ...), custom_call_target="tpu_custom_call" | custom-call | tf_op jit(solution)/shard_map/cond/branch_1_fun/relay/pallas_call | solution.py:258
  226.3 2.0 collective-permute-start.19
  228.3 1.3 collective-permute-start.20
  230.1 4.8 %collective-permute-done.17.refs_1_ = f32[656,128]{1,0:T(8,128)S(1)} collective-permute-done((f32[656,128]{1,0:T(8,128)}, f32[656,128]{1,0:T(8,128)S(1)}, u32[]{:S(2)}, u32[]{:S(2)}) %collective-permute-start.17) | collective-permute-done | bytes 335904 | tf_op jit(solution)/shard_map/cond/branch_1_fun/ppermute | solution.py:373
  234.9 1.3 collective-permute-start.22
  236.2 2.0 collective-permute-start.23
  238.2 4.9 %collective-permute-done.19.refs_3_ = f32[656,128]{1,0:T(8,128)S(1)} collective-permute-done((f32[656,128]{1,0:T(8,128)}, f32[656,128]{1,0:T(8,128)S(1)}, u32[]{:S(2)}, u32[]{:S(2)}) %collective-permute-start.19) | collective-permute-done | bytes 335904 | tf_op jit(solution)/shard_map/cond/branch_1_fun/ppermute | solution.py:373
  244.9 7.1 %collective-permute-done.21.refs_5_ = f32[656,128]{1,0:T(8,128)S(1)} collective-permute-done((f32[656,128]{1,0:T(8,128)}, f32[656,128]{1,0:T(8,128)S(1)}, u32[]{:S(2)}, u32[]{:S(2)}) %collective-permute-start.21) | collective-permute-done | bytes 335904 | tf_op jit(solution)/shard_map/cond/branch_1_fun/ppermute | solution.py:373
  252.6 2.7 collective-permute-start.27
  255.3 4.6 %collective-permute-done.23.refs_7_ = f32[656,128]{1,0:T(8,128)S(1)} collective-permute-done((f32[656,128]{1,0:T(8,128)}, f32[656,128]{1,0:T(8,128)S(1)}, u32[]{:S(2)}, u32[]{:S(2)}) %collective-permute-start.23) | collective-permute-done | bytes 335904 | tf_op jit(solution)/shard_map/cond/branch_1_fun/ppermute | solution.py:373
  259.9 2.1 collective-permute-start.29
  262.0 6.5 %collective-permute-done.25.refs_9_ = f32[656,128]{1,0:T(8,128)S(1)} collective-permute-done((f32[656,128]{1,0:T(8,128)}, f32[656,128]{1,0:T(8,128)S(1)}, u32[]{:S(2)}, u32[]{:S(2)}) %collective-permute-start.25) | collective-permute-done | bytes 335904 | tf_op jit(solution)/shard_map/cond/branch_1_fun/ppermute | solution.py:373
  268.4 2.5 collective-permute-start.30
  271.0 2.3 collective-permute-start.31
  274.4 2.9 collective-permute-done.27.refs_11_
  277.4 29.9 %collective-permute-done.28.refs_12_ = f32[656,128]{1,0:T(8,128)} collective-permute-done((f32[656,128]{1,0:T(8,128)}, f32[656,128]{1,0:T(8,128)}, u32[]{:S(2)}, u32[]{:S(2)}) %collective-permute-start.28) | collective-permute-done | bytes 335904 | tf_op jit(solution)/shard_map/cond/branch_1_fun/ppermute | solution.py:373
  307.4 12.8 %unpack.4 = f32[41,32768]{1,0:T(8,128)} custom-call(s32[256]{0:T(256)} %fusion.15.base_ref, s32[256]{0:T(256)} %get-tuple-element.536.tail_ref, s32[256]{0:T(256)} %get-tuple-element.534.step_ref, s32[256,128]{1,0:T(8,128)S(1)} %get-tuple-element.173.perm_ref, f32[10496,128]{1,0:T(8,128)} %bitcast.1.direct_ref, f32[656,128]{1,0:T(8,128)} %get-tuple-element.73.refs_0_, ...), custom_call_target="tpu_custom_call" | custom-call | tf_op jit(solution)/shard_map/cond/branch_1_fun/unpack/pallas_call | solution.py:316
  (69 shorter events, 14.5 us)
Async XLA Ops:
  1.4 23.8 %all-to-all-start.3 = ((s32[32,1,32]{2,1,0:T(1,128)}), s32[32,1,32]{2,1,0:T(1,128)S(1)}, u32[]{:S(2)}, u32[]{:S(2)}) async-start(s32[32,1,32]{2,1,0:T(1,128)} %broadcast_in_dim.11), calls=%async_computation.3 | async-start | bytes 32768 | tf_op jit(solution)/shard_map/all_to_all | solution.py:389
  36.8 270.5 %all-to-all-start.1 = ((f32[32,328,128]{2,1,0:T(8,128)}), f32[32,328,128]{2,1,0:T(8,128)}, u32[]{:S(2)}, u32[]{:S(2)}) async-start(f32[32,328,128]{2,1,0:T(8,128)} %pack_direct.4), calls=%async_computation.1 | async-start | bytes 10747904 | tf_op jit(solution)/shard_map/cond/branch_1_fun/all_to_all | solution.py:369
  47.7 170.1 %collective-permute-start.16 = (f32[2624,128]{1,0:T(8,128)}, f32[2624,128]{1,0:T(8,128)S(1)}, u32[]{:S(2)}, u32[]{:S(2)}) collective-permute-start(f32[2624,128]{1,0:T(8,128)} %pack_cross.4), channel_id=1, source_target_pairs={{0,4},{1,5},{2,6},{3,7},{4,0},{5,1},{6,2},{7,3},{8,12},{9,13},{10,... | collective-permute-start | bytes 4030472 | tf_op jit(solution)/shard_map/cond/branch_1_fun/ppermute | solution.py:367
  225.7 9.2 %collective-permute-start.17 = (f32[656,128]{1,0:T(8,128)}, f32[656,128]{1,0:T(8,128)S(1)}, u32[]{:S(2)}, u32[]{:S(2)}) collective-permute-start(f32[656,128]{1,0:T(8,128)} %get-tuple-element.74), channel_id=1, source_target_pairs={{0,1},{1,0},{2,3},{3,2},{4,5},{5,4},{6,7},{7,6},{8,9},{9,8},{10,11... | collective-permute-start | bytes 1007624 | tf_op jit(solution)/shard_map/cond/branch_1_fun/ppermute | solution.py:373
  226.3 9.9 %collective-permute-start.18 = (f32[656,128]{1,0:T(8,128)}, f32[656,128]{1,0:T(8,128)S(1)}, u32[]{:S(2)}, u32[]{:S(2)}) collective-permute-start(f32[656,128]{1,0:T(8,128)} %get-tuple-element.75), channel_id=1, source_target_pairs={{0,2},{1,3},{2,0},{3,1},{4,6},{5,7},{6,4},{7,5},{8,10},{9,11},{10,... | collective-permute-start | bytes 1007624 | tf_op jit(solution)/shard_map/cond/branch_1_fun/ppermute | solution.py:373
  226.3 16.7 %collective-permute-start.19 = (f32[656,128]{1,0:T(8,128)}, f32[656,128]{1,0:T(8,128)S(1)}, u32[]{:S(2)}, u32[]{:S(2)}) collective-permute-start(f32[656,128]{1,0:T(8,128)} %get-tuple-element.76), channel_id=1, source_target_pairs={{0,3},{1,2},{2,1},{3,0},{4,7},{5,6},{6,5},{7,4},{8,11},{9,10},{10,... | collective-permute-start | bytes 1007624 | tf_op jit(solution)/shard_map/cond/branch_1_fun/ppermute | solution.py:373
  228.3 15.9 %collective-permute-start.20 = (f32[656,128]{1,0:T(8,128)}, f32[656,128]{1,0:T(8,128)S(1)}, u32[]{:S(2)}, u32[]{:S(2)}) collective-permute-start(f32[656,128]{1,0:T(8,128)} %get-tuple-element.77), channel_id=1, source_target_pairs={{0,8},{1,9},{2,10},{3,11},{4,12},{5,13},{6,14},{7,15},{8,0},{9,1},... | collective-permute-start | bytes 1007624 | tf_op jit(solution)/shard_map/cond/branch_1_fun/ppermute | solution.py:373
  229.6 22.3 %collective-permute-start.21 = (f32[656,128]{1,0:T(8,128)}, f32[656,128]{1,0:T(8,128)S(1)}, u32[]{:S(2)}, u32[]{:S(2)}) collective-permute-start(f32[656,128]{1,0:T(8,128)} %get-tuple-element.78), channel_id=1, source_target_pairs={{0,9},{1,8},{2,11},{3,10},{4,13},{5,12},{6,15},{7,14},{8,1},{9,0},... | collective-permute-start | bytes 1007624 | tf_op jit(solution)/shard_map/cond/branch_1_fun/ppermute | solution.py:373
  234.9 72.4 %copy-start.5 = (f32[656,128]{1,0:T(8,128)}, f32[656,128]{1,0:T(8,128)S(1)}, u32[]{:S(2)}) copy-start(f32[656,128]{1,0:T(8,128)S(1)} %collective-permute-done.17.refs_1_) | copy-start | bytes 1007620 | tf_op jit(solution)/shard_map/cond
  234.9 17.7 %collective-permute-start.22 = (f32[656,128]{1,0:T(8,128)}, f32[656,128]{1,0:T(8,128)S(1)}, u32[]{:S(2)}, u32[]{:S(2)}) collective-permute-start(f32[656,128]{1,0:T(8,128)} %get-tuple-element.79), channel_id=1, source_target_pairs={{0,10},{1,11},{2,8},{3,9},{4,14},{5,15},{6,12},{7,13},{8,2},{9,3},... | collective-permute-start | bytes 1007624 | tf_op jit(solution)/shard_map/cond/branch_1_fun/ppermute | solution.py:373
  236.2 71.1 %copy-start.8 = (f32[656,128]{1,0:T(8,128)}, f32[656,128]{1,0:T(8,128)S(1)}, u32[]{:S(2)}) copy-start(f32[656,128]{1,0:T(8,128)S(1)} %collective-permute-done.18.refs_2_) | copy-start | bytes 1007620 | tf_op jit(solution)/shard_map/cond
  236.2 23.6 %collective-permute-start.23 = (f32[656,128]{1,0:T(8,128)}, f32[656,128]{1,0:T(8,128)S(1)}, u32[]{:S(2)}, u32[]{:S(2)}) collective-permute-start(f32[656,128]{1,0:T(8,128)} %get-tuple-element.80), channel_id=1, source_target_pairs={{0,11},{1,10},{2,9},{3,8},{4,15},{5,14},{6,13},{7,12},{8,3},{9,2},... | collective-permute-start | bytes 1007624 | tf_op jit(solution)/shard_map/cond/branch_1_fun/ppermute | solution.py:373
  243.0 64.3 %copy-start.11 = (f32[656,128]{1,0:T(8,128)}, f32[656,128]{1,0:T(8,128)S(1)}, u32[]{:S(2)}) copy-start(f32[656,128]{1,0:T(8,128)S(1)} %collective-permute-done.19.refs_3_) | copy-start | bytes 1007620 | tf_op jit(solution)/shard_map/cond
  243.0 16.8 %collective-permute-start.24 = (f32[656,128]{1,0:T(8,128)}, f32[656,128]{1,0:T(8,128)S(1)}, u32[]{:S(2)}, u32[]{:S(2)}) collective-permute-start(f32[656,128]{1,0:T(8,128)} %get-tuple-element.81), channel_id=1, source_target_pairs={{0,16},{1,17},{2,18},{3,19},{4,20},{5,21},{6,22},{7,23},{8,24},{9,... | collective-permute-start | bytes 1007624 | tf_op jit(solution)/shard_map/cond/branch_1_fun/ppermute | solution.py:373
  244.2 63.1 %copy-start.14 = (f32[656,128]{1,0:T(8,128)}, f32[656,128]{1,0:T(8,128)S(1)}, u32[]{:S(2)}) copy-start(f32[656,128]{1,0:T(8,128)S(1)} %collective-permute-done.20.refs_4_) | copy-start | bytes 1007620 | tf_op jit(solution)/shard_map/cond
  244.2 24.2 %collective-permute-start.25 = (f32[656,128]{1,0:T(8,128)}, f32[656,128]{1,0:T(8,128)S(1)}, u32[]{:S(2)}, u32[]{:S(2)}) collective-permute-start(f32[656,128]{1,0:T(8,128)} %get-tuple-element.82), channel_id=1, source_target_pairs={{0,17},{1,16},{2,19},{3,18},{4,21},{5,20},{6,23},{7,22},{8,25},{9,... | collective-permute-start | bytes 1007624 | tf_op jit(solution)/shard_map/cond/branch_1_fun/ppermute | solution.py:373
  252.0 55.3 %copy-start.17 = (f32[656,128]{1,0:T(8,128)}, f32[656,128]{1,0:T(8,128)S(1)}, u32[]{:S(2)}) copy-start(f32[656,128]{1,0:T(8,128)S(1)} %collective-permute-done.21.refs_5_) | copy-start | bytes 1007620 | tf_op jit(solution)/shard_map/cond
  252.0 19.0 %collective-permute-start.26 = (f32[656,128]{1,0:T(8,128)}, f32[656,128]{1,0:T(8,128)S(1)}, u32[]{:S(2)}, u32[]{:S(2)}) collective-permute-start(f32[656,128]{1,0:T(8,128)} %get-tuple-element.83), channel_id=1, source_target_pairs={{0,18},{1,19},{2,16},{3,17},{4,22},{5,23},{6,20},{7,21},{8,26},{9,... | collective-permute-start | bytes 1007624 | tf_op jit(solution)/shard_map/cond/branch_1_fun/ppermute | solution.py:373
  252.6 54.7 %copy-start.20 = (f32[656,128]{1,0:T(8,128)}, f32[656,128]{1,0:T(8,128)S(1)}, u32[]{:S(2)}) copy-start(f32[656,128]{1,0:T(8,128)S(1)} %collective-permute-done.22.refs_6_) | copy-start | bytes 1007620 | tf_op jit(solution)/shard_map/cond
  252.6 24.8 %collective-permute-start.27 = (f32[656,128]{1,0:T(8,128)}, f32[656,128]{1,0:T(8,128)}, u32[]{:S(2)}, u32[]{:S(2)}) collective-permute-start(f32[656,128]{1,0:T(8,128)} %get-tuple-element.84), channel_id=1, source_target_pairs={{0,19},{1,18},{2,17},{3,16},{4,23},{5,22},{6,21},{7,20},{8,27},{9,... | collective-permute-start | bytes 1007624 | tf_op jit(solution)/shard_map/cond/branch_1_fun/ppermute | solution.py:373
  259.9 47.4 %collective-permute-start.28 = (f32[656,128]{1,0:T(8,128)}, f32[656,128]{1,0:T(8,128)}, u32[]{:S(2)}, u32[]{:S(2)}) collective-permute-start(f32[656,128]{1,0:T(8,128)} %get-tuple-element.85), channel_id=1, source_target_pairs={{0,24},{1,25},{2,26},{3,27},{4,28},{5,29},{6,30},{7,31},{8,16},{9,... | collective-permute-start | bytes 1007624 | tf_op jit(solution)/shard_map/cond/branch_1_fun/ppermute | solution.py:373
  259.9 47.4 %collective-permute-start.29 = (f32[656,128]{1,0:T(8,128)}, f32[656,128]{1,0:T(8,128)}, u32[]{:S(2)}, u32[]{:S(2)}) collective-permute-start(f32[656,128]{1,0:T(8,128)} %get-tuple-element.86), channel_id=1, source_target_pairs={{0,25},{1,24},{2,27},{3,26},{4,29},{5,28},{6,31},{7,30},{8,17},{9,... | collective-permute-start | bytes 1007624 | tf_op jit(solution)/shard_map/cond/branch_1_fun/ppermute | solution.py:373
  268.4 38.8 %collective-permute-start.30 = (f32[656,128]{1,0:T(8,128)}, f32[656,128]{1,0:T(8,128)}, u32[]{:S(2)}, u32[]{:S(2)}) collective-permute-start(f32[656,128]{1,0:T(8,128)} %get-tuple-element.87), channel_id=1, source_target_pairs={{0,26},{1,27},{2,24},{3,25},{4,30},{5,31},{6,28},{7,29},{8,18},{9,... | collective-permute-start | bytes 1007624 | tf_op jit(solution)/shard_map/cond/branch_1_fun/ppermute | solution.py:373
  271.0 36.3 %collective-permute-start.31 = (f32[656,128]{1,0:T(8,128)}, f32[656,128]{1,0:T(8,128)}, u32[]{:S(2)}, u32[]{:S(2)}) collective-permute-start(f32[656,128]{1,0:T(8,128)} %get-tuple-element.88), channel_id=1, source_target_pairs={{0,27},{1,26},{2,25},{3,24},{4,31},{5,30},{6,29},{7,28},{8,19},{9,... | collective-permute-start | bytes 1007624 | tf_op jit(solution)/shard_map/cond/branch_1_fun/ppermute | solution.py:373
  (7 other events, 201.8 us)
where the time goes:
time: 324 us; the launch traced here: 320 us
  waiting for transfers between devices  231 us (71%)
  Pallas kernels  45.2 us (14%)
  starting transfers between devices  31.3 us (10%)
  other arithmetic  6.95 us (2%)
  local copies, waits for them, and re-layouts  4.48 us (1%)
    ppermute x1, waiting for transfers between devices, exchange(): crossed = lax.ppermute(cross, both, [(i, plan.partner(i)) for i in over])  170 us
    ppermute x15, waiting for transfers between devices, exchange(): pieces[d] = lax.ppermute(pieces[d], both, pairs)  60.7 us
    ppermute x15, starting transfers between devices, exchange(): pieces[d] = lax.ppermute(pieces[d], both, pairs)  19.1 us
    pallas_call x1, Pallas kernels, advance(): pl.pallas_call(functools.partial(advance_kernel, step=step), grid=(nodes...  13.1 us
    pallas_call x1, Pallas kernels, unpack(): pl.pallas_call(functools.partial(unpack_kernel, plan=plan), grid_spec=plt...  12.8 us
    pallas_call x1, Pallas kernels, pack_direct(): pl.pallas_call(functools.partial(direct_kernel, plan=plan), grid_spec=plt...  7.52 us
    pallas_call x1, Pallas kernels, relay(): pl.pallas_call(functools.partial(relay_kernel, plan=plan, room=room), in_...  6.71 us
  transfers between devices with their start and end apart: 18, of which 8 were waited for; matrix products, arithmetic and copies ran while one was open for 2% of the time, Pallas kernels for 8%

commit v1 on v0

v1 whole, which is shorter than its diff:
```python
import functools

import jax
import jax.numpy as jnp
from jax import lax
from jax.experimental import pallas as pl
from jax.experimental.pallas import tpu as pltpu
from jax.sharding import PartitionSpec as P


time_step = 0.25
sublanes = 8
both = ("group", "peer")
smem_full = pl.BlockSpec(memory_space=pltpu.SMEM)
vmem_full = pl.BlockSpec(memory_space=pltpu.VMEM)
any_full = pl.BlockSpec(memory_space=pl.ANY)


def round_up(value, step):
    return -(-value // step) * step


class Plan:
    def __init__(self, rows, blocks, width):
        self.rows, self.blocks, self.width = rows, blocks, width
        self.peers = lax.axis_size("peer")
        self.devices = lax.axis_size("group") * self.peers
        self.near = self.peers // 2
        self.mates = self.devices // 2
        most = 2 * blocks // self.devices
        self.slots = max(most // 2, 1)
        self.over = most - self.slots
        self.full = rows // sublanes * sublanes
        self.extra = rows - self.full
        self.direct_rows = round_up(rows * self.slots, sublanes)
        self.spill_rows = round_up(rows * self.over, sublanes)
        self.worst = self.mates * self.over

    def half(self, device):
        return (device % self.peers) // self.near

    def mate(self, device):
        return device // self.peers * self.near + device % self.near

    def device(self, mate, half):
        return mate // self.near * self.peers + half * self.near + mate % self.near

    def partner(self, device):
        flip = 1 - 2 * self.half(device)
        return device + flip * self.near

    def me(self):
        return lax.axis_index("group") * self.peers + lax.axis_index("peer")


def advanced(params_ref, vals, tail):
    full = vals.shape[0]
    voltage = vals[0:1]
    relax = 1.5 + 0.5 * jnp.tanh(0.5 * voltage)
    done, current = [], 0.0
    for part, rows in ((vals, slice(0, full)), (tail, slice(full, None))):
        if part is None:
            continue
        steady = 0.5 + 0.5 * jnp.tanh((voltage - params_ref[0, rows]) * params_ref[1, rows])
        damping = jnp.exp(params_ref[2, rows] * relax)
        gates = steady + (part - steady) * damping
        drive = params_ref[3, rows] * gates * (voltage - params_ref[4, rows])
        current = current + jnp.sum(drive, axis=0, keepdims=True)
        done.append(gates)
    row = lax.broadcasted_iota(jnp.int32, vals.shape, 0)
    done[0] = jnp.where(row == 0, voltage - time_step * current, done[0])
    return done


def advance_kernel(params_ref, states_ref, out_ref, *, width):
    rows = states_ref.shape[0]
    full = rows // sublanes * sublanes

    def one(i, carry):
        cols = pl.ds(pl.multiple_of(i * width, width), width)
        tail = states_ref[full:rows, cols] if rows > full else None
        done = advanced(params_ref, states_ref[0:full, cols], tail)
        out_ref[0:full, cols] = done[0]
        if rows > full:
            out_ref[full:rows, cols] = done[1]
        return carry

    lax.fori_loop(0, states_ref.shape[1] // width, one, 0)


def gate_params(half_volt, steepness, gate_rate, conductance, reversal, width):
    params = jnp.stack([half_volt, 0.5 * steepness, -gate_rate, conductance, reversal])
    params = jnp.pad(params, ((0, 0), (1, 0)))
    return jnp.broadcast_to(params[:, :, None], params.shape + (width,))


def advance(params, states):
    rows, nodes = states.shape
    width = params.shape[2]
    block = fitting(nodes, 4096)
    return pl.pallas_call(
        functools.partial(advance_kernel, width=width),
        grid=(nodes // block,),
        in_specs=[
            pl.BlockSpec(params.shape, lambda i: (0, 0, 0)),
            pl.BlockSpec((rows, block), lambda i: (0, i)),
        ],
        out_specs=pl.BlockSpec((rows, block), lambda i: (0, i)),
        out_shape=jax.ShapeDtypeStruct(states.shape, states.dtype),
        cost_estimate=pl.CostEstimate(
            flops=40 * rows * nodes,
            bytes_accessed=8 * rows * nodes,
            transcendentals=3 * rows * nodes,
        ),
        name="advance",
    )(params, states)


def fitting(total, most):
    size = min(total, most)
    while total % size:
        size -= 128
    return size


def put_block(plan, adv_ref, block, put, base, tail):
    cols = pl.ds(pl.multiple_of(block * plan.width, plan.width), plan.width)
    put(base, plan.full, adv_ref[0 : plan.full, cols])
    for e in range(plan.extra):
        put(tail(e), 1, adv_ref[plan.full + e : plan.full + e + 1, cols])


def cross_kernel(table_ref, adv_ref, cross_ref, *, plan, room):
    me = plan.me()
    mine = plan.half(me)

    def one(s, carry):
        start, at = carry
        count = table_ref[s, 0, me]
        far = (plan.half(s) != mine).astype(jnp.int32)
        more = jnp.maximum(count - plan.slots, 0) * far

        def spill(k, carry):
            slot = jnp.minimum(at + k, room - 1)

            def put(base, size, vals):
                if size == plan.full:
                    base = pl.multiple_of(base, sublanes)
                cross_ref[pl.ds(base, size), :] = vals

            put_block(
                plan,
                adv_ref,
                start + plan.slots + k,
                put,
                slot * plan.full,
                lambda e: room * plan.full + e * room + slot,
            )
            return carry

        lax.fori_loop(0, more, spill, 0)
        return start + count, at + more

    lax.fori_loop(0, plan.devices, one, (0, 0))


def pack_cross(plan, table, adv, room):
    rows = round_up(room * plan.rows, sublanes)
    return pl.pallas_call(
        functools.partial(cross_kernel, plan=plan, room=room),
        in_specs=[smem_full, vmem_full],
        out_specs=vmem_full,
        out_shape=jax.ShapeDtypeStruct((rows, plan.width), adv.dtype),
        name="pack_cross",
    )(table, adv)


def starts(plan, table_ref, start_ref):
    me = plan.me()

    def scan(s, start):
        start_ref[s] = start
        return start + table_ref[s, 0, me]

    lax.fori_loop(0, plan.devices, scan, 0)


def slots_kernel(table_ref, adv_ref, out_ref, start_ref, *, plan, inner):
    per_step = out_ref.shape[0]
    first = pl.program_id(0) * per_step
    slots = plan.over if inner else plan.slots

    @pl.when(first == 0)
    def _():
        starts(plan, table_ref, start_ref)

    for d in range(per_step):
        to = first + d
        if inner:
            start = start_ref[plan.device(to, plan.half(plan.me()))] + plan.slots
        else:
            start = start_ref[to]

        def put(base, size, vals):
            out_ref[d, base : base + size, :] = vals

        for k in range(slots):
            put_block(
                plan,
                adv_ref,
                jnp.minimum(start + k, plan.blocks - 1),
                put,
                k * plan.full,
                lambda e: slots * plan.full + e * slots + k,
            )


def pack_slots(plan, table, adv, inner):
    count = plan.mates if inner else plan.devices
    rows = plan.spill_rows if inner else plan.direct_rows
    per_step = fitting_blocks(count, 4)
    return pl.pallas_call(
        functools.partial(slots_kernel, plan=plan, inner=inner),
        grid_spec=pltpu.PrefetchScalarGridSpec(
            num_scalar_prefetch=1,
            grid=(count // per_step,),
            in_specs=[pl.BlockSpec(adv.shape, lambda i, *_: (0, 0))],
            out_specs=pl.BlockSpec((per_step, rows, plan.width), lambda i, *_: (i, 0, 0)),
            scratch_shapes=[pltpu.SMEM((plan.devices,), jnp.int32)],
        ),
        out_shape=jax.ShapeDtypeStruct((count, rows, plan.width), adv.dtype),
        name="pack_inner" if inner else "pack_direct",
    )(table, adv)


def relay_kernel(table_ref, params_ref, cross_ref, *refs, plan, room):
    outs, (far_ref, done_ref) = refs[: plan.mates], refs[plan.mates :]
    me = plan.me()
    mine = plan.half(me)
    other = plan.partner(me)

    def scan(s, at):
        far_ref[s] = at
        near = (plan.half(s) == mine).astype(jnp.int32)
        return at + jnp.maximum(table_ref[s, 0, other] - plan.slots, 0) * near

    total = lax.fori_loop(0, plan.devices, scan, 0)

    def step(i, carry):
        rows = pl.ds(pl.multiple_of(i * plan.full, plan.full), plan.full)
        tails = [pl.ds(room * plan.full + e * room + i, 1) for e in range(plan.extra)]
        tail = None
        if tails:
            tail = jnp.concatenate([cross_ref[t, :] for t in tails], axis=0)
        done = advanced(params_ref, cross_ref[rows, :], tail)
        done_ref[rows, :] = done[0]
        for e, t in enumerate(tails):
            done_ref[t, :] = done[1][e : e + 1]
        return carry

    lax.fori_loop(0, jnp.minimum(total, room), step, 0)
    here = plan.mate(me)
    slots = plan.over
    for d, out_ref in enumerate(outs):
        at = far_ref[plan.device(here ^ d, mine)]
        for k in range(slots):
            slot = jnp.minimum(at + k, room - 1)
            out_ref[k * plan.full : (k + 1) * plan.full, :] = done_ref[
                pl.ds(pl.multiple_of(slot * plan.full, plan.full), plan.full), :
            ]
            for e in range(plan.extra):
                row = slots * plan.full + e * slots + k
                out_ref[row : row + 1, :] = done_ref[
                    pl.ds(room * plan.full + e * room + slot, 1), :
                ]


def relay(plan, table, params, crossed, room):
    piece = jax.ShapeDtypeStruct((plan.spill_rows, plan.width), crossed.dtype)
    return pl.pallas_call(
        functools.partial(relay_kernel, plan=plan, room=room),
        in_specs=[smem_full, vmem_full, vmem_full],
        out_specs=[vmem_full] * plan.mates,
        out_shape=[piece] * plan.mates,
        scratch_shapes=[
            pltpu.SMEM((plan.devices,), jnp.int32),
            pltpu.VMEM(crossed.shape, crossed.dtype),
        ],
        name="relay",
    )(table, params, crossed)


def permuted(vals, lanes):
    return jnp.take_along_axis(vals, lanes, axis=1, mode="promise_in_bounds")


def unpack_kernel(
    base_ref, tail_ref, step_ref, perm_ref, direct_ref, inner_ref, *refs, plan
):
    pieces = refs[: plan.mates]
    out_ref, got_ref, last_ref, sem = refs[plan.mates :]
    per_step, width = perm_ref.shape
    first = pl.program_id(0) * per_step

    @pl.when(first == 0)
    def _():
        direct = plan.devices * plan.direct_rows
        inner = plan.mates * plan.spill_rows
        sizes = [direct, inner] + [plan.spill_rows] * plan.mates
        copies, at = [], 0
        for i, (src_ref, size) in enumerate(zip([direct_ref, inner_ref, *pieces], sizes)):
            rows = pl.ds(at, size)
            copies.append(pltpu.make_async_copy(src_ref, got_ref.at[rows], sem.at[i]))
            at += size
        for copy in copies:
            copy.start()
        for copy in copies:
            copy.wait()

    for i in range(per_step):
        base = pl.multiple_of(base_ref[first + i], sublanes)
        tail = tail_ref[first + i]
        stride = step_ref[first + i]
        lanes = jnp.broadcast_to(perm_ref[i : i + 1, :], (plan.full, width))
        vals = got_ref[pl.ds(base, plan.full), :]
        out_ref[0 : plan.full, i * width : (i + 1) * width] = permuted(vals, lanes)
        for e in range(plan.extra):
            last_ref[e, i : i + 1, :] = got_ref[pl.ds(tail + e * stride, 1), :]
    for e in range(plan.extra):
        last = permuted(last_ref[e], perm_ref[...])
        for i in range(per_step):
            cols = slice(i * width, (i + 1) * width)
            out_ref[plan.full + e : plan.full + e + 1, cols] = last[i : i + 1, :]


def unpack(plan, places, perm, direct, inner, pieces):
    per_step = fitting_blocks(plan.blocks, 16)
    total = plan.devices * plan.direct_rows + 2 * plan.mates * plan.spill_rows
    return pl.pallas_call(
        functools.partial(unpack_kernel, plan=plan),
        grid_spec=pltpu.PrefetchScalarGridSpec(
            num_scalar_prefetch=3,
            grid=(plan.blocks // per_step,),
            in_specs=[pl.BlockSpec((per_step, plan.width), lambda i, *_: (i, 0))]
            + [any_full] * (2 + plan.mates),
            out_specs=pl.BlockSpec((plan.rows, per_step * plan.width), lambda i, *_: (0, i)),
            scratch_shapes=[
                pltpu.VMEM((total, plan.width), direct.dtype),
                pltpu.VMEM((max(plan.extra, 1), per_step, plan.width), direct.dtype),
                pltpu.SemaphoreType.DMA((2 + plan.mates,)),
            ],
        ),
        out_shape=jax.ShapeDtypeStruct((plan.rows, plan.blocks * plan.width), direct.dtype),
        name="unpack",
    )(*places, perm, direct, inner, *pieces)


def fitting_blocks(total, most):
    size = min(total, most)
    while total % size:
        size -= 1
    return size


def find_places(plan, block_part, me):
    same = block_part[:, None] == block_part[None, :]
    position = jnp.arange(plan.blocks, dtype=jnp.int32)
    ahead = position[None, :] < position[:, None]
    rank = jnp.sum((same & ahead).astype(jnp.int32), axis=1, dtype=jnp.int32)
    direct = rank < plan.slots
    home = plan.half(block_part) == plan.half(me)
    mate = plan.mate(block_part)
    piece = jnp.where(home, mate, plan.mates + (mate ^ plan.mate(me)))
    origin = plan.devices * plan.direct_rows + piece * plan.spill_rows
    slot = rank - plan.slots
    base = jnp.where(
        direct, block_part * plan.direct_rows + rank * plan.full, origin + slot * plan.full
    )
    tail = jnp.where(
        direct,
        block_part * plan.direct_rows + plan.slots * plan.full + rank,
        origin + plan.over * plan.full + slot,
    )
    return base, tail, jnp.where(direct, plan.slots, plan.over)


def exchange(plan, room, table, states, params, places, tile_perm):
    over = range(plan.devices)
    halves = [[plan.device(m, h) for m in range(plan.mates)] for h in range(2)]
    cross = pack_cross(plan, table, states, room)
    crossed = lax.ppermute(cross, both, [(i, plan.partner(i)) for i in over])
    adv = advance(params, states)
    inner = pack_slots(plan, table, adv, True)
    inner = lax.all_to_all(
        inner, both, split_axis=0, concat_axis=0, tiled=True, axis_index_groups=halves
    )
    direct = pack_slots(plan, table, adv, False)
    direct, crossed = lax.optimization_barrier((direct, crossed))
    direct = lax.all_to_all(direct, both, split_axis=0, concat_axis=0, tiled=True)
    pieces = list(relay(plan, table, params, crossed, room))
    for d in range(1, plan.mates):
        pairs = [(i, plan.device(plan.mate(i) ^ d, plan.half(i))) for i in over]
        pieces[d] = lax.ppermute(pieces[d], both, pairs)
    direct = direct.reshape(plan.devices * plan.direct_rows, plan.width)
    inner = inner.reshape(plan.mates * plan.spill_rows, plan.width)
    return unpack(plan, places, tile_perm, direct, inner, pieces)


def on_device(
    states, block_part, tile_perm, half_volt, steepness, gate_rate, conductance, reversal
):
    blocks, width = tile_perm.shape
    plan = Plan(states.shape[0], blocks, width)
    devices = plan.devices
    me = plan.me()
    ids = jnp.arange(devices, dtype=jnp.int32)
    onehot = (block_part[:, None] == ids[None, :]).astype(jnp.int32)
    counts = jnp.sum(onehot, axis=0, dtype=jnp.int32)
    told = jnp.broadcast_to(counts[None, None, :], (devices, 1, devices))
    table = lax.all_to_all(told, both, split_axis=0, concat_axis=0, tiled=True)
    params = gate_params(half_volt, steepness, gate_rate, conductance, reversal, width)
    far = plan.half(ids)[:, None] != plan.half(ids)[None, :]
    spilled = jnp.maximum(table - plan.slots, 0)
    spilled = jnp.sum(jnp.where(far[:, None, :], spilled, 0), axis=0)
    spilled = jnp.max(spilled)
    places = find_places(plan, block_part, me)
    rooms = [plan.worst * 3 // 8, plan.worst // 2, plan.worst]
    rooms = [round_up(room, sublanes) for room in rooms]
    choice = sum((spilled > room).astype(jnp.int32) for room in rooms[:-1])
    return lax.switch(
        choice,
        [functools.partial(exchange, plan, room) for room in rooms],
        table,
        states,
        params,
        places,
        tile_perm,
    )


def solution(mesh):
    return jax.shard_map(
        on_device,
        mesh=mesh,
        in_specs=(
            P(None, both),
            P(both),
            P(both, None),
            P(),
            P(),
            P(),
            P(),
            P(),
        ),
        out_specs=P(None, both),
        check_vma=False,
    )
```

time: 324 us -> 268 us (0.83)
  the two profiles are of different devices: /device:TPU:25 before, /device:TPU:0 now
where the time goes in v1:
time: 268 us; the launch traced here: 267 us
  waiting for transfers between devices  170 us (63%)
  Pallas kernels  49.9 us (19%)
  starting transfers between devices  36.2 us (14%)
  other arithmetic  5.01 us (2%)
  local copies, waits for them, and re-layouts  4.35 us (2%)
    ppermute x15, waiting for transfers between devices, exchange(): pieces[d] = lax.ppermute(pieces[d], both, pairs)  113 us
    ppermute x1, waiting for transfers between devices, exchange(): crossed = lax.ppermute(cross, both, [(i, plan.partner(i)) for i in over])  53.4 us
    ppermute x15, starting transfers between devices, exchange(): pieces[d] = lax.ppermute(pieces[d], both, pairs)  20.5 us
    pallas_call x2, Pallas kernels, pack_slots(): pl.pallas_call(functools.partial(slots_kernel, plan=plan, inner=inner), g...  13.5 us
    pallas_call x1, Pallas kernels, advance(): pl.pallas_call(functools.partial(advance_kernel, width=width), grid=(node...  13 us
    pallas_call x1, Pallas kernels, unpack(): pl.pallas_call(functools.partial(unpack_kernel, plan=plan), grid_spec=plt...  12.8 us
    all_to_all x1, starting transfers between devices, on_device(): table = lax.all_to_all(told, both, split_axis=0, concat_axis=0, tiled=True)  7.33 us
    pallas_call x1, Pallas kernels, relay(): pl.pallas_call(functools.partial(relay_kernel, plan=plan, room=room), in_...  5.59 us
  transfers between devices with their start and end apart: 19, of which 9 were waited for; matrix products, arithmetic and copies ran while one was open for 2% of the time, Pallas kernels for 7%

profile of v1, /device:TPU:0, one launch (start us, length us, event | category | flops | bytes accessed | tf_op | source)
XLA Modules:
  0.0 267.3 jit_solution(6674590535541352284)
XLA Ops:
  1.4 7.3 %all-to-all-start.6 = ((s32[32,1,32]{2,1,0:T(1,128)}), s32[32,1,32]{2,1,0:T(1,128)S(1)}, u32[]{:S(2)}, u32[]{:S(2)}) async-start(s32[32,1,32]{2,1,0:T(1,128)} %broadcast_in_dim.7), calls=%async_computation.6 | async-start | bytes 32768 | tf_op jit(solution)/shard_map/all_to_all | solution.py:420
  11.8 4.0 %all-to-all-done.6 = s32[32,1,32]{2,1,0:T(1,128)S(1)} async-done(((s32[32,1,32]{2,1,0:T(1,128)}), s32[32,1,32]{2,1,0:T(1,128)S(1)}, u32[]{:S(2)}, u32[]{:S(2)}) %all-to-all-start.6) | async-done | bytes 4128 | tf_op jit(solution)/shard_map/all_to_all | solution.py:420
  17.9 249.4 %conditional.1 = (f32[41,32768]{1,0:T(8,128)}) conditional(s32[]{:T(128)} %clamp.3, (f32[5,40]{1,0:T(8,128)S(1)}, f32[41,32768]{1,0:T(8,128)}, s32[32,1,32]{2,1,0:T(1,128)S(1)}, s32[256]{0:T(256)S(1)}, s32[]{:T(128)}, /*index=5*/(), s32[256,128]{1,0:T(8,128)}, s32[256]{0:T(256)}, s32[256]{0:T(256)S(1)}, s32[256]{0:T(256)S(1)}, ...), branch_computations={%region_4.5_spmd, %region_5.6_spmd, %region_6.7_spmd} | conditional | flops 53747220 | bytes 77242896 | solution.py:430
  18.8 13.0 %advance.4.adv_ref = f32[41,32768]{1,0:T(8,128)} custom-call(f32[5,41,128]{2,1,0:T(8,128)} %broadcast_in_dim.10.params_ref, f32[41,32768]{1,0:T(8,128)} %get-tuple-element.161.states_ref.adv_ref), custom_call_target="tpu_custom_call" | custom-call | flops 53739520 | bytes 10747904 | tf_op jit(solution)/shard_map/cond/branch_1_fun/advance/pallas_call | solution.py:101
  31.8 5.8 %pack_inner.4 = f32[16,328,128]{2,1,0:T(8,128)} custom-call(s32[32,1,32]{2,1,0:T(1,128)S(1)} %get-tuple-element.80.table_ref, f32[41,32768]{1,0:T(8,128)} %advance.4.adv_ref), custom_call_target="tpu_custom_call" | custom-call | tf_op jit(solution)/shard_map/cond/branch_1_fun/pack_inner/pallas_call | solution.py:222
  37.6 3.7 %all-to-all-start.3 = ((f32[16,328,128]{2,1,0:T(8,128)}), f32[16,328,128]{2,1,0:T(8,128)S(1)}, u32[]{:S(2)}, u32[]{:S(2)}) async-start(f32[16,328,128]{2,1,0:T(8,128)} %pack_inner.4), calls=%async_computation.3 | async-start | bytes 5373952 | tf_op jit(solution)/shard_map/cond/branch_1_fun/all_to_all | solution.py:394
  41.3 5.0 %pack_cross.4 = f32[2624,128]{1,0:T(8,128)} custom-call(s32[32,1,32]{2,1,0:T(1,128)S(1)} %get-tuple-element.80.table_ref, f32[41,32768]{1,0:T(8,128)} %get-tuple-element.161.states_ref.adv_ref), custom_call_target="tpu_custom_call" | custom-call | tf_op jit(solution)/shard_map/cond/branch_1_fun/pack_cross/pallas_call | solution.py:169
  47.0 7.7 %pack_direct.4 = f32[32,328,128]{2,1,0:T(8,128)} custom-call(s32[32,1,32]{2,1,0:T(1,128)S(1)} %get-tuple-element.80.table_ref, f32[41,32768]{1,0:T(8,128)} %advance.4.adv_ref), custom_call_target="tpu_custom_call" | custom-call | tf_op jit(solution)/shard_map/cond/branch_1_fun/pack_direct/pallas_call | solution.py:222
  54.7 53.4 %collective-permute-done.16.cross_ref = f32[2624,128]{1,0:T(8,128)} collective-permute-done((f32[2624,128]{1,0:T(8,128)}, f32[2624,128]{1,0:T(8,128)}, u32[]{:S(2)}, u32[]{:S(2)}) %collective-permute-start.16) | collective-permute-done | bytes 1343520 | tf_op jit(solution)/shard_map/cond/branch_1_fun/ppermute | solution.py:391
  109.6 4.0 %all-to-all-start.2 = ((f32[32,328,128]{2,1,0:T(8,128)}), f32[32,328,128]{2,1,0:T(8,128)}, u32[]{:S(2)}, u32[]{:S(2)}) async-start(f32[32,328,128]{2,1,0:T(8,128)} %pack_direct.4), calls=%async_computation.2 | async-start | bytes 10747904 | tf_op jit(solution)/shard_map/cond/branch_1_fun/all_to_all | solution.py:399
  113.6 5.6 %relay.4 = (f32[328,128]{1,0:T(8,128)}, f32[328,128]{1,0:T(8,128)}, f32[328,128]{1,0:T(8,128)}, f32[328,128]{1,0:T(8,128)}, f32[328,128]{1,0:T(8,128)}, /*index=...) custom-call(s32[32,1,32]{2,1,0:T(1,128)S(1)} %get-tuple-element.80.t, ...), custom_call_target="tpu_custom_call" | custom-call | tf_op jit(solution)/shard_map/cond/branch_1_fun/relay/pallas_call | solution.py:280
  123.8 53.7 %collective-permute-done.17.refs_1_ = f32[328,128]{1,0:T(8,128)S(1)} collective-permute-done((f32[328,128]{1,0:T(8,128)}, f32[328,128]{1,0:T(8,128)S(1)}, u32[]{:S(2)}, u32[]{:S(2)}) %collective-permute-start.17) | collective-permute-done | bytes 167968 | tf_op jit(solution)/shard_map/cond/branch_1_fun/ppermute | solution.py:403
  177.5 32.2 %collective-permute-done.18.refs_2_ = f32[328,128]{1,0:T(8,128)S(1)} collective-permute-done((f32[328,128]{1,0:T(8,128)}, f32[328,128]{1,0:T(8,128)S(1)}, u32[]{:S(2)}, u32[]{:S(2)}) %collective-permute-start.18) | collective-permute-done | bytes 167968 | tf_op jit(solution)/shard_map/cond/branch_1_fun/ppermute | solution.py:403
  209.7 2.0 collective-permute-start.23
  211.7 2.1 collective-permute-done.19.refs_3_
  213.8 1.7 collective-permute-start.24
  216.3 4.0 %collective-permute-start.26 = (f32[328,128]{1,0:T(8,128)}, f32[328,128]{1,0:T(8,128)S(1)}, u32[]{:S(2)}, u32[]{:S(2)}) collective-permute-start(f32[328,128]{1,0:T(8,128)} %get-tuple-element.95), channel_id=1, source_target_pairs={{0,18},{1,19},{2,16},{3,17},{4,22},{5,23},{6,20},{7,21},{8,26},{9,... | collective-permute-start | bytes 503816 | tf_op jit(solution)/shard_map/cond/branch_1_fun/ppermute | solution.py:403
  221.2 1.7 collective-permute-done.23.refs_7_
  224.7 14.4 %collective-permute-done.25.refs_9_ = f32[328,128]{1,0:T(8,128)S(1)} collective-permute-done((f32[328,128]{1,0:T(8,128)}, f32[328,128]{1,0:T(8,128)S(1)}, u32[]{:S(2)}, u32[]{:S(2)}) %collective-permute-start.25) | collective-permute-done | bytes 167968 | tf_op jit(solution)/shard_map/cond/branch_1_fun/ppermute | solution.py:403
  239.1 3.0 %collective-permute-start.30 = (f32[328,128]{1,0:T(8,128)}, f32[328,128]{1,0:T(8,128)S(1)}, u32[]{:S(2)}, u32[]{:S(2)}) collective-permute-start(f32[328,128]{1,0:T(8,128)} %get-tuple-element.99), channel_id=1, source_target_pairs={{0,26},{1,27},{2,24},{3,25},{4,30},{5,31},{6,28},{7,29},{8,18},{9,... | collective-permute-start | bytes 503816 | tf_op jit(solution)/shard_map/cond/branch_1_fun/ppermute | solution.py:403
  242.1 2.4 collective-permute-start.31
  245.1 2.4 collective-permute-done.30.refs_14_
  247.5 6.2 %collective-permute-done.31.refs_15_ = f32[328,128]{1,0:T(8,128)S(1)} collective-permute-done((f32[328,128]{1,0:T(8,128)}, f32[328,128]{1,0:T(8,128)S(1)}, u32[]{:S(2)}, u32[]{:S(2)}) %collective-permute-start.31) | collective-permute-done | bytes 167968 | tf_op jit(solution)/shard_map/cond/branch_1_fun/ppermute | solution.py:403
  254.5 12.8 %unpack.4 = f32[41,32768]{1,0:T(8,128)} custom-call(s32[256]{0:T(256)} %fusion.7.base_ref, s32[256]{0:T(256)} %get-tuple-element.471.tail_ref, s32[256]{0:T(256)} %select_n.105.step_ref, s32[256,128]{1,0:T(8,128)S(1)} %copy-done.4, f32[10496,128]{1,0:T(8,128)} %bitcast.2.direct_ref, f32[5248,128]{1,0:T(8,128)} %bitcast.14, ...), custom_call_target="tpu_custom_call" | custom-call | tf_op jit(solution)/shard_map/cond/branch_1_fun/unpack/pallas_call | solution.py:339
  (77 shorter events, 17.5 us)
Async XLA Ops:
  1.4 14.4 %all-to-all-start.6 = ((s32[32,1,32]{2,1,0:T(1,128)}), s32[32,1,32]{2,1,0:T(1,128)S(1)}, u32[]{:S(2)}, u32[]{:S(2)}) async-start(s32[32,1,32]{2,1,0:T(1,128)} %broadcast_in_dim.7), calls=%async_computation.6 | async-start | bytes 32768 | tf_op jit(solution)/shard_map/all_to_all | solution.py:420
  37.6 70.5 %all-to-all-start.3 = ((f32[16,328,128]{2,1,0:T(8,128)}), f32[16,328,128]{2,1,0:T(8,128)S(1)}, u32[]{:S(2)}, u32[]{:S(2)}) async-start(f32[16,328,128]{2,1,0:T(8,128)} %pack_inner.4), calls=%async_computation.3 | async-start | bytes 5373952 | tf_op jit(solution)/shard_map/cond/branch_1_fun/all_to_all | solution.py:394
  46.3 61.8 %collective-permute-start.16 = (f32[2624,128]{1,0:T(8,128)}, f32[2624,128]{1,0:T(8,128)}, u32[]{:S(2)}, u32[]{:S(2)}) collective-permute-start(f32[2624,128]{1,0:T(8,128)} %pack_cross.4), channel_id=1, source_target_pairs={{0,4},{1,5},{2,6},{3,7},{4,0},{5,1},{6,2},{7,3},{8,12},{9,13},{10,... | collective-permute-start | bytes 4030472 | tf_op jit(solution)/shard_map/cond/branch_1_fun/ppermute | solution.py:391
  54.7 165.6 %copy-start.52 = (s32[256]{0:T(256)S(1)}, s32[256]{0:T(256)}, u32[]{:S(2)}) copy-start(s32[256]{0:T(256)} %get-tuple-element.240) | copy-start | bytes 3076 | tf_op jit(solution)/shard_map/cond
  54.7 199.8 %copy-start.4 = (s32[256,128]{1,0:T(8,128)S(1)}, s32[256,128]{1,0:T(8,128)}, u32[]{:S(2)}) copy-start(s32[256,128]{1,0:T(8,128)} %get-tuple-element.188.perm_ref) | copy-start | bytes 393220 | tf_op jit(solution)/shard_map/cond
  109.6 144.1 %all-to-all-start.2 = ((f32[32,328,128]{2,1,0:T(8,128)}), f32[32,328,128]{2,1,0:T(8,128)}, u32[]{:S(2)}, u32[]{:S(2)}) async-start(f32[32,328,128]{2,1,0:T(8,128)} %pack_direct.4), calls=%async_computation.2 | async-start | bytes 10747904 | tf_op jit(solution)/shard_map/cond/branch_1_fun/all_to_all | solution.py:399
  119.2 58.3 %collective-permute-start.17 = (f32[328,128]{1,0:T(8,128)}, f32[328,128]{1,0:T(8,128)S(1)}, u32[]{:S(2)}, u32[]{:S(2)}) collective-permute-start(f32[328,128]{1,0:T(8,128)} %get-tuple-element.86), channel_id=1, source_target_pairs={{0,1},{1,0},{2,3},{3,2},{4,5},{5,4},{6,7},{7,6},{8,9},{9,8},{10,11... | collective-permute-start | bytes 503816 | tf_op jit(solution)/shard_map/cond/branch_1_fun/ppermute | solution.py:403
  120.2 89.5 %collective-permute-start.18 = (f32[328,128]{1,0:T(8,128)}, f32[328,128]{1,0:T(8,128)S(1)}, u32[]{:S(2)}, u32[]{:S(2)}) collective-permute-start(f32[328,128]{1,0:T(8,128)} %get-tuple-element.87), channel_id=1, source_target_pairs={{0,2},{1,3},{2,0},{3,1},{4,6},{5,7},{6,4},{7,5},{8,10},{9,11},{10,... | collective-permute-start | bytes 503816 | tf_op jit(solution)/shard_map/cond/branch_1_fun/ppermute | solution.py:403
  121.7 92.1 %collective-permute-start.19 = (f32[328,128]{1,0:T(8,128)}, f32[328,128]{1,0:T(8,128)S(1)}, u32[]{:S(2)}, u32[]{:S(2)}) collective-permute-start(f32[328,128]{1,0:T(8,128)} %get-tuple-element.88), channel_id=1, source_target_pairs={{0,3},{1,2},{2,1},{3,0},{4,7},{5,6},{6,5},{7,4},{8,11},{9,10},{10,... | collective-permute-start | bytes 503816 | tf_op jit(solution)/shard_map/cond/branch_1_fun/ppermute | solution.py:403
  122.7 92.8 %collective-permute-start.20 = (f32[328,128]{1,0:T(8,128)}, f32[328,128]{1,0:T(8,128)S(1)}, u32[]{:S(2)}, u32[]{:S(2)}) collective-permute-start(f32[328,128]{1,0:T(8,128)} %get-tuple-element.89), channel_id=1, source_target_pairs={{0,8},{1,9},{2,10},{3,11},{4,12},{5,13},{6,14},{7,15},{8,0},{9,1},... | collective-permute-start | bytes 503816 | tf_op jit(solution)/shard_map/cond/branch_1_fun/ppermute | solution.py:403
  122.7 93.5 %collective-permute-start.21 = (f32[328,128]{1,0:T(8,128)}, f32[328,128]{1,0:T(8,128)S(1)}, u32[]{:S(2)}, u32[]{:S(2)}) collective-permute-start(f32[328,128]{1,0:T(8,128)} %get-tuple-element.90), channel_id=1, source_target_pairs={{0,9},{1,8},{2,11},{3,10},{4,13},{5,12},{6,15},{7,14},{8,1},{9,0},... | collective-permute-start | bytes 503816 | tf_op jit(solution)/shard_map/cond/branch_1_fun/ppermute | solution.py:403
  177.5 76.9 %copy-start.7 = (f32[328,128]{1,0:T(8,128)}, f32[328,128]{1,0:T(8,128)S(1)}, u32[]{:S(2)}) copy-start(f32[328,128]{1,0:T(8,128)S(1)} %collective-permute-done.17.refs_1_) | copy-start | bytes 503812 | tf_op jit(solution)/shard_map/cond
  177.5 43.3 %collective-permute-start.22 = (f32[328,128]{1,0:T(8,128)}, f32[328,128]{1,0:T(8,128)S(1)}, u32[]{:S(2)}, u32[]{:S(2)}) collective-permute-start(f32[328,128]{1,0:T(8,128)} %get-tuple-element.91), channel_id=1, source_target_pairs={{0,10},{1,11},{2,8},{3,9},{4,14},{5,15},{6,12},{7,13},{8,2},{9,3},... | collective-permute-start | bytes 503816 | tf_op jit(solution)/shard_map/cond/branch_1_fun/ppermute | solution.py:403
  209.7 44.7 %copy-start.10 = (f32[328,128]{1,0:T(8,128)}, f32[328,128]{1,0:T(8,128)S(1)}, u32[]{:S(2)}) copy-start(f32[328,128]{1,0:T(8,128)S(1)} %collective-permute-done.18.refs_2_) | copy-start | bytes 503812 | tf_op jit(solution)/shard_map/cond
  209.7 13.1 %collective-permute-start.23 = (f32[328,128]{1,0:T(8,128)}, f32[328,128]{1,0:T(8,128)S(1)}, u32[]{:S(2)}, u32[]{:S(2)}) collective-permute-start(f32[328,128]{1,0:T(8,128)} %get-tuple-element.92), channel_id=1, source_target_pairs={{0,11},{1,10},{2,9},{3,8},{4,15},{5,14},{6,13},{7,12},{8,3},{9,2},... | collective-permute-start | bytes 503816 | tf_op jit(solution)/shard_map/cond/branch_1_fun/ppermute | solution.py:403
  213.8 40.6 %copy-start.13 = (f32[328,128]{1,0:T(8,128)}, f32[328,128]{1,0:T(8,128)S(1)}, u32[]{:S(2)}) copy-start(f32[328,128]{1,0:T(8,128)S(1)} %collective-permute-done.19.refs_3_) | copy-start | bytes 503812 | tf_op jit(solution)/shard_map/cond
  213.8 10.4 %collective-permute-start.24 = (f32[328,128]{1,0:T(8,128)}, f32[328,128]{1,0:T(8,128)S(1)}, u32[]{:S(2)}, u32[]{:S(2)}) collective-permute-start(f32[328,128]{1,0:T(8,128)} %get-tuple-element.93), channel_id=1, source_target_pairs={{0,16},{1,17},{2,18},{3,19},{4,20},{5,21},{6,22},{7,23},{8,24},{9,... | collective-permute-start | bytes 503816 | tf_op jit(solution)/shard_map/cond/branch_1_fun/ppermute | solution.py:403
  215.5 23.6 %collective-permute-start.25 = (f32[328,128]{1,0:T(8,128)}, f32[328,128]{1,0:T(8,128)S(1)}, u32[]{:S(2)}, u32[]{:S(2)}) collective-permute-start(f32[328,128]{1,0:T(8,128)} %get-tuple-element.94), channel_id=1, source_target_pairs={{0,17},{1,16},{2,19},{3,18},{4,21},{5,20},{6,23},{7,22},{8,25},{9,... | collective-permute-start | bytes 503816 | tf_op jit(solution)/shard_map/cond/branch_1_fun/ppermute | solution.py:403
  216.3 25.9 %collective-permute-start.26 = (f32[328,128]{1,0:T(8,128)}, f32[328,128]{1,0:T(8,128)S(1)}, u32[]{:S(2)}, u32[]{:S(2)}) collective-permute-start(f32[328,128]{1,0:T(8,128)} %get-tuple-element.95), channel_id=1, source_target_pairs={{0,18},{1,19},{2,16},{3,17},{4,22},{5,23},{6,20},{7,21},{8,26},{9,... | collective-permute-start | bytes 503816 | tf_op jit(solution)/shard_map/cond/branch_1_fun/ppermute | solution.py:403
  220.9 24.2 %collective-permute-start.27 = (f32[328,128]{1,0:T(8,128)}, f32[328,128]{1,0:T(8,128)S(1)}, u32[]{:S(2)}, u32[]{:S(2)}) collective-permute-start(f32[328,128]{1,0:T(8,128)} %get-tuple-element.96), channel_id=1, source_target_pairs={{0,19},{1,18},{2,17},{3,16},{4,23},{5,22},{6,21},{7,20},{8,27},{9,... | collective-permute-start | bytes 503816 | tf_op jit(solution)/shard_map/cond/branch_1_fun/ppermute | solution.py:403
  222.8 22.2 %collective-permute-start.28 = (f32[328,128]{1,0:T(8,128)}, f32[328,128]{1,0:T(8,128)S(1)}, u32[]{:S(2)}, u32[]{:S(2)}) collective-permute-start(f32[328,128]{1,0:T(8,128)} %get-tuple-element.97), channel_id=1, source_target_pairs={{0,24},{1,25},{2,26},{3,27},{4,28},{5,29},{6,30},{7,31},{8,16},{9,... | collective-permute-start | bytes 503816 | tf_op jit(solution)/shard_map/cond/branch_1_fun/ppermute | solution.py:403
  224.2 20.9 %collective-permute-start.29 = (f32[328,128]{1,0:T(8,128)}, f32[328,128]{1,0:T(8,128)S(1)}, u32[]{:S(2)}, u32[]{:S(2)}) collective-permute-start(f32[328,128]{1,0:T(8,128)} %get-tuple-element.98), channel_id=1, source_target_pairs={{0,25},{1,24},{2,27},{3,26},{4,29},{5,28},{6,31},{7,30},{8,17},{9,... | collective-permute-start | bytes 503816 | tf_op jit(solution)/shard_map/cond/branch_1_fun/ppermute | solution.py:403
  239.1 8.4 %collective-permute-start.30 = (f32[328,128]{1,0:T(8,128)}, f32[328,128]{1,0:T(8,128)S(1)}, u32[]{:S(2)}, u32[]{:S(2)}) collective-permute-start(f32[328,128]{1,0:T(8,128)} %get-tuple-element.99), channel_id=1, source_target_pairs={{0,26},{1,27},{2,24},{3,25},{4,30},{5,31},{6,28},{7,29},{8,18},{9,... | collective-permute-start | bytes 503816 | tf_op jit(solution)/shard_map/cond/branch_1_fun/ppermute | solution.py:403
  242.1 11.6 %collective-permute-start.31 = (f32[328,128]{1,0:T(8,128)}, f32[328,128]{1,0:T(8,128)S(1)}, u32[]{:S(2)}, u32[]{:S(2)}) collective-permute-start(f32[328,128]{1,0:T(8,128)} %get-tuple-element.100), channel_id=1, source_target_pairs={{0,27},{1,26},{2,25},{3,24},{4,31},{5,30},{6,29},{7,28},{8,19},{9,... | collective-permute-start | bytes 503816 | tf_op jit(solution)/shard_map/cond/branch_1_fun/ppermute | solution.py:403
  (13 other events, 237.4 us)

commit v2 on v1

--- a/solution.py
+++ b/solution.py
@@ -32,8 +32,12 @@
         self.over = most - self.slots
         self.full = rows // sublanes * sublanes
         self.extra = rows - self.full
-        self.direct_rows = round_up(rows * self.slots, sublanes)
-        self.spill_rows = round_up(rows * self.over, sublanes)
+        self.most = self.slots + self.over
+        self.inner_rows = round_up(rows * self.most, sublanes)
+        self.cross_rows = round_up(rows * self.slots, sublanes)
+        self.relay_rows = round_up(rows * self.over, sublanes)
+        self.chunk = 16
+        self.chunk_rows = round_up(rows * self.chunk, sublanes)
         self.worst = self.mates * self.over
 
     def half(self, device):
@@ -130,7 +134,9 @@
         put(tail(e), 1, adv_ref[plan.full + e : plan.full + e + 1, cols])
 
 
-def cross_kernel(table_ref, adv_ref, cross_ref, *, plan, room):
+def dense_kernel(table_ref, states_ref, *refs, plan):
+    outs, all_ref = refs[:-1], refs[-1]
+    room = len(outs) * plan.chunk
     me = plan.me()
     mine = plan.half(me)
 
@@ -146,11 +152,11 @@
             def put(base, size, vals):
                 if size == plan.full:
                     base = pl.multiple_of(base, sublanes)
-                cross_ref[pl.ds(base, size), :] = vals
+                all_ref[pl.ds(base, size), :] = vals
 
             put_block(
                 plan,
-                adv_ref,
+                states_ref,
                 start + plan.slots + k,
                 put,
                 slot * plan.full,
@@ -162,47 +168,45 @@
         return start + count, at + more
 
     lax.fori_loop(0, plan.devices, one, (0, 0))
-
-
-def pack_cross(plan, table, adv, room):
-    rows = round_up(room * plan.rows, sublanes)
+    for c, out_ref in enumerate(outs):
+        size = plan.chunk * plan.full
+        out_ref[0:size, :] = all_ref[c * size : (c + 1) * size, :]
+        for e in range(plan.extra):
+            row = room * plan.full + e * room + c * plan.chunk
+            to = size + e * plan.chunk
+            out_ref[to : to + plan.chunk, :] = all_ref[row : row + plan.chunk, :]
+
+
+def pack_dense(plan, table, states, chunks):
+    piece = jax.ShapeDtypeStruct((plan.chunk_rows, plan.width), states.dtype)
+    rows = round_up(chunks * plan.chunk * plan.rows, sublanes)
     return pl.pallas_call(
-        functools.partial(cross_kernel, plan=plan, room=room),
+        functools.partial(dense_kernel, plan=plan),
         in_specs=[smem_full, vmem_full],
-        out_specs=vmem_full,
-        out_shape=jax.ShapeDtypeStruct((rows, plan.width), adv.dtype),
-        name="pack_cross",
-    )(table, adv)
-
-
-def starts(plan, table_ref, start_ref):
+        out_specs=[vmem_full] * chunks,
+        out_shape=[piece] * chunks,
+        scratch_shapes=[pltpu.VMEM((rows, plan.width), states.dtype)],
+        name="pack_dense",
+    )(table, states)
+
+
+def pieces_kernel(table_ref, adv_ref, *refs, plan, inner, cross):
+    outs, start_ref = refs[:-1], refs[-1]
     me = plan.me()
+    mine = plan.half(me)
+    here = plan.mate(me)
 
     def scan(s, start):
         start_ref[s] = start
         return start + table_ref[s, 0, me]
 
     lax.fori_loop(0, plan.devices, scan, 0)
-
-
-def slots_kernel(table_ref, adv_ref, out_ref, start_ref, *, plan, inner):
-    per_step = out_ref.shape[0]
-    first = pl.program_id(0) * per_step
-    slots = plan.over if inner else plan.slots
-
-    @pl.when(first == 0)
-    def _():
-        starts(plan, table_ref, start_ref)
-
-    for d in range(per_step):
-        to = first + d
-        if inner:
-            start = start_ref[plan.device(to, plan.half(plan.me()))] + plan.slots
-        else:
-            start = start_ref[to]
+    jobs = [(d, mine, plan.most) for d in inner] + [(d, 1 - mine, plan.slots) for d in cross]
+    for (d, half, slots), out_ref in zip(jobs, outs):
+        start = start_ref[plan.device(here ^ d, half)]
 
         def put(base, size, vals):
-            out_ref[d, base : base + size, :] = vals
+            out_ref[base : base + size, :] = vals
 
         for k in range(slots):
             put_block(
@@ -215,26 +219,21 @@
             )
 
 
-def pack_slots(plan, table, adv, inner):
-    count = plan.mates if inner else plan.devices
-    rows = plan.spill_rows if inner else plan.direct_rows
-    per_step = fitting_blocks(count, 4)
+def pack_pieces(plan, table, adv, inner, cross):
+    rows = [plan.inner_rows] * len(inner) + [plan.cross_rows] * len(cross)
     return pl.pallas_call(
-        functools.partial(slots_kernel, plan=plan, inner=inner),
-        grid_spec=pltpu.PrefetchScalarGridSpec(
-            num_scalar_prefetch=1,
-            grid=(count // per_step,),
-            in_specs=[pl.BlockSpec(adv.shape, lambda i, *_: (0, 0))],
-            out_specs=pl.BlockSpec((per_step, rows, plan.width), lambda i, *_: (i, 0, 0)),
-            scratch_shapes=[pltpu.SMEM((plan.devices,), jnp.int32)],
-        ),
-        out_shape=jax.ShapeDtypeStruct((count, rows, plan.width), adv.dtype),
-        name="pack_inner" if inner else "pack_direct",
+        functools.partial(pieces_kernel, plan=plan, inner=inner, cross=cross),
+        in_specs=[smem_full, vmem_full],
+        out_specs=[vmem_full] * len(rows),
+        out_shape=[jax.ShapeDtypeStruct((size, plan.width), adv.dtype) for size in rows],
+        scratch_shapes=[pltpu.SMEM((plan.devices,), jnp.int32)],
     )(table, adv)
 
 
-def relay_kernel(table_ref, params_ref, cross_ref, *refs, plan, room):
-    outs, (far_ref, done_ref) = refs[: plan.mates], refs[plan.mates :]
+def relay_kernel(table_ref, params_ref, *refs, plan, chunks):
+    dense, outs = refs[:chunks], refs[chunks : chunks + plan.mates]
+    far_ref, done_ref = refs[chunks + plan.mates :]
+    room = chunks * plan.chunk
     me = plan.me()
     mine = plan.half(me)
     other = plan.partner(me)
@@ -245,20 +244,25 @@
         return at + jnp.maximum(table_ref[s, 0, other] - plan.slots, 0) * near
 
     total = lax.fori_loop(0, plan.devices, scan, 0)
-
-    def step(i, carry):
-        rows = pl.ds(pl.multiple_of(i * plan.full, plan.full), plan.full)
-        tails = [pl.ds(room * plan.full + e * room + i, 1) for e in range(plan.extra)]
-        tail = None
-        if tails:
-            tail = jnp.concatenate([cross_ref[t, :] for t in tails], axis=0)
-        done = advanced(params_ref, cross_ref[rows, :], tail)
-        done_ref[rows, :] = done[0]
-        for e, t in enumerate(tails):
-            done_ref[t, :] = done[1][e : e + 1]
-        return carry
-
-    lax.fori_loop(0, jnp.minimum(total, room), step, 0)
+    for c, dense_ref in enumerate(dense):
+
+        def step(i, carry):
+            rows = pl.ds(pl.multiple_of(i * plan.full, plan.full), plan.full)
+            tail = None
+            if plan.extra:
+                lasts = [plan.chunk * plan.full + e * plan.chunk + i for e in range(plan.extra)]
+                tail = [dense_ref[pl.ds(last, 1), :] for last in lasts]
+                tail = jnp.concatenate(tail, axis=0) if plan.extra > 1 else tail[0]
+            done = advanced(params_ref, dense_ref[rows, :], tail)
+            slot = c * plan.chunk + i
+            to = pl.ds(pl.multiple_of(slot * plan.full, plan.full), plan.full)
+            done_ref[to, :] = done[0]
+            for e in range(plan.extra):
+                row = room * plan.full + e * room + slot
+                done_ref[pl.ds(row, 1), :] = done[1][e : e + 1]
+            return carry
+
+        lax.fori_loop(0, jnp.clip(total - c * plan.chunk, 0, plan.chunk), step, 0)
     here = plan.mate(me)
     slots = plan.over
     for d, out_ref in enumerate(outs):
@@ -275,42 +279,38 @@
                 ]
 
 
-def relay(plan, table, params, crossed, room):
-    piece = jax.ShapeDtypeStruct((plan.spill_rows, plan.width), crossed.dtype)
+def relay(plan, table, params, dense):
+    piece = jax.ShapeDtypeStruct((plan.relay_rows, plan.width), dense[0].dtype)
+    rows = round_up(len(dense) * plan.chunk * plan.rows, sublanes)
     return pl.pallas_call(
-        functools.partial(relay_kernel, plan=plan, room=room),
-        in_specs=[smem_full, vmem_full, vmem_full],
+        functools.partial(relay_kernel, plan=plan, chunks=len(dense)),
+        in_specs=[smem_full] + [vmem_full] * (1 + len(dense)),
         out_specs=[vmem_full] * plan.mates,
         out_shape=[piece] * plan.mates,
         scratch_shapes=[
             pltpu.SMEM((plan.devices,), jnp.int32),
-            pltpu.VMEM(crossed.shape, crossed.dtype),
+            pltpu.VMEM((rows, plan.width), dense[0].dtype),
         ],
         name="relay",
-    )(table, params, crossed)
+    )(table, params, *dense)
 
 
 def permuted(vals, lanes):
     return jnp.take_along_axis(vals, lanes, axis=1, mode="promise_in_bounds")
 
 
-def unpack_kernel(
-    base_ref, tail_ref, step_ref, perm_ref, direct_ref, inner_ref, *refs, plan
-):
-    pieces = refs[: plan.mates]
-    out_ref, got_ref, last_ref, sem = refs[plan.mates :]
+def unpack_kernel(base_ref, tail_ref, step_ref, perm_ref, *refs, plan, sizes):
+    pieces = refs[: len(sizes)]
+    out_ref, got_ref, last_ref, sem = refs[len(sizes) :]
     per_step, width = perm_ref.shape
     first = pl.program_id(0) * per_step
 
     @pl.when(first == 0)
     def _():
-        direct = plan.devices * plan.direct_rows
-        inner = plan.mates * plan.spill_rows
-        sizes = [direct, inner] + [plan.spill_rows] * plan.mates
         copies, at = [], 0
-        for i, (src_ref, size) in enumerate(zip([direct_ref, inner_ref, *pieces], sizes)):
+        for i, (piece_ref, size) in enumerate(zip(pieces, sizes)):
             rows = pl.ds(at, size)
-            copies.append(pltpu.make_async_copy(src_ref, got_ref.at[rows], sem.at[i]))
+            copies.append(pltpu.make_async_copy(piece_ref, got_ref.at[rows], sem.at[i]))
             at += size
         for copy in copies:
             copy.start()
@@ -333,26 +333,27 @@
             out_ref[plan.full + e : plan.full + e + 1, cols] = last[i : i + 1, :]
 
 
-def unpack(plan, places, perm, direct, inner, pieces):
+def unpack(plan, places, perm, pieces):
     per_step = fitting_blocks(plan.blocks, 16)
-    total = plan.devices * plan.direct_rows + 2 * plan.mates * plan.spill_rows
+    sizes = [piece.shape[0] for piece in pieces]
+    dtype = pieces[0].dtype
     return pl.pallas_call(
-        functools.partial(unpack_kernel, plan=plan),
+        functools.partial(unpack_kernel, plan=plan, sizes=sizes),
         grid_spec=pltpu.PrefetchScalarGridSpec(
             num_scalar_prefetch=3,
             grid=(plan.blocks // per_step,),
             in_specs=[pl.BlockSpec((per_step, plan.width), lambda i, *_: (i, 0))]
-            + [any_full] * (2 + plan.mates),
+            + [any_full] * len(pieces),
             out_specs=pl.BlockSpec((plan.rows, per_step * plan.width), lambda i, *_: (0, i)),
             scratch_shapes=[
-                pltpu.VMEM((total, plan.width), direct.dtype),
-                pltpu.VMEM((max(plan.extra, 1), per_step, plan.width), direct.dtype),
-                pltpu.SemaphoreType.DMA((2 + plan.mates,)),
+                pltpu.VMEM((sum(sizes), plan.width), dtype),
+                pltpu.VMEM((max(plan.extra, 1), per_step, plan.width), dtype),
+                pltpu.SemaphoreType.DMA((len(pieces),)),
             ],
         ),
-        out_shape=jax.ShapeDtypeStruct((plan.rows, plan.blocks * plan.width), direct.dtype),
+        out_shape=jax.ShapeDtypeStruct((plan.rows, plan.blocks * plan.width), dtype),
         name="unpack",
-    )(*places, perm, direct, inner, *pieces)
+    )(*places, perm, *pieces)
 
 
 def fitting_blocks(total, most):
@@ -367,43 +368,47 @@
     position = jnp.arange(plan.blocks, dtype=jnp.int32)
     ahead = position[None, :] < position[:, None]
     rank = jnp.sum((same & ahead).astype(jnp.int32), axis=1, dtype=jnp.int32)
+    home = plan.half(block_part) == plan.half(me)
     direct = rank < plan.slots
-    home = plan.half(block_part) == plan.half(me)
-    mate = plan.mate(block_part)
-    piece = jnp.where(home, mate, plan.mates + (mate ^ plan.mate(me)))
-    origin = plan.devices * plan.direct_rows + piece * plan.spill_rows
-    slot = rank - plan.slots
-    base = jnp.where(
-        direct, block_part * plan.direct_rows + rank * plan.full, origin + slot * plan.full
-    )
-    tail = jnp.where(
-        direct,
-        block_part * plan.direct_rows + plan.slots * plan.full + rank,
-        origin + plan.over * plan.full + slot,
-    )
-    return base, tail, jnp.where(direct, plan.slots, plan.over)
-
-
-def exchange(plan, room, table, states, params, places, tile_perm):
+    piece = plan.mate(block_part) ^ plan.mate(me)
+    crossed = plan.mates * plan.inner_rows + piece * plan.cross_rows
+    relayed = plan.mates * (plan.inner_rows + plan.cross_rows) + piece * plan.relay_rows
+    origin = jnp.where(home, piece * plan.inner_rows, jnp.where(direct, crossed, relayed))
+    slots = jnp.where(home, plan.most, jnp.where(direct, plan.slots, plan.over))
+    slot = jnp.where(home | direct, rank, rank - plan.slots)
+    return origin + slot * plan.full, origin + slots * plan.full + slot, slots
+
+
+def exchange(plan, chunks, table, states, params, places, tile_perm):
     over = range(plan.devices)
-    halves = [[plan.device(m, h) for m in range(plan.mates)] for h in range(2)]
-    cross = pack_cross(plan, table, states, room)
-    crossed = lax.ppermute(cross, both, [(i, plan.partner(i)) for i in over])
+    split = plan.mates // 2
+    ends = {"inner": plan.half, "again": plan.half, "cross": lambda i: 1 - plan.half(i)}
+
+    def send(kind, d, piece):
+        pairs = [(i, plan.device(plan.mate(i) ^ d, ends[kind](i))) for i in over]
+        return lax.ppermute(piece, both, pairs)
+
+    dense = pack_dense(plan, table, states, chunks)
+    crossed = []
+    for c in range(chunks):
+        crossed.append(
+            lax.ppermute(dense[c], both, [(i, plan.partner(i)) for i in over])
+        )
     adv = advance(params, states)
-    inner = pack_slots(plan, table, adv, True)
-    inner = lax.all_to_all(
-        inner, both, split_axis=0, concat_axis=0, tiled=True, axis_index_groups=halves
-    )
-    direct = pack_slots(plan, table, adv, False)
-    direct, crossed = lax.optimization_barrier((direct, crossed))
-    direct = lax.all_to_all(direct, both, split_axis=0, concat_axis=0, tiled=True)
-    pieces = list(relay(plan, table, params, crossed, room))
-    for d in range(1, plan.mates):
-        pairs = [(i, plan.device(plan.mate(i) ^ d, plan.half(i))) for i in over]
-        pieces[d] = lax.ppermute(pieces[d], both, pairs)
-    direct = direct.reshape(plan.devices * plan.direct_rows, plan.width)
-    inner = inner.reshape(plan.mates * plan.spill_rows, plan.width)
-    return unpack(plan, places, tile_perm, direct, inner, pieces)
+    first = list(range(1, split))
+    second = [0] + list(range(split, plan.mates))
+    inner = dict(zip(first, pack_pieces(plan, table, adv, first, [])))
+    more = pack_pieces(plan, table, adv, second, list(range(plan.mates)))
+    inner.update(zip(second, more))
+    cross = list(more[len(second) :])
+    again = list(relay(plan, table, params, crossed))
+    for d in range(plan.mates):
+        cross[d] = send("cross", d, cross[d])
+        if d:
+            inner[d] = send("inner", d, inner[d])
+            again[d] = send("again", d, again[d])
+    inner = [inner[d] for d in range(plan.mates)]
+    return unpack(plan, places, tile_perm, [*inner, *cross, *again])
 
 
 def on_device(
@@ -424,9 +429,10 @@
     spilled = jnp.sum(jnp.where(far[:, None, :], spilled, 0), axis=0)
     spilled = jnp.max(spilled)
     places = find_places(plan, block_part, me)
-    rooms = [plan.worst * 3 // 8, plan.worst // 2, plan.worst]
-    rooms = [round_up(room, sublanes) for room in rooms]
-    choice = sum((spilled > room).astype(jnp.int32) for room in rooms[:-1])
+    most = -(-plan.worst // plan.chunk)
+    rooms = sorted({-(-most * 3 // 8), -(-most // 2), most})
+    choice = sum((spilled > room * plan.chunk).astype(jnp.int32) for room in rooms[:-1])
+    choice = jnp.asarray(choice, jnp.int32)
     return lax.switch(
         choice,
         [functools.partial(exchange, plan, room) for room in rooms],

time: 268 us -> 361 us (1.35)
  the two profiles are of different devices: /device:TPU:0 before, /device:TPU:25 now
where the time goes in v2:
time: 361 us; the launch traced here: 357 us
  starting transfers between devices  183 us (51%)
  waiting for transfers between devices  112 us (31%)
  Pallas kernels  47.8 us (13%)
  other arithmetic  5.71 us (2%)
  local copies, waits for them, and re-layouts  5.55 us (2%)
    ppermute x46, starting transfers between devices, send(): return lax.ppermute(piece, both, pairs)  174 us
    ppermute x46, waiting for transfers between devices, send(): return lax.ppermute(piece, both, pairs)  110 us
    pallas_call x1, Pallas kernels, unpack(): pl.pallas_call(functools.partial(unpack_kernel, plan=plan, sizes=sizes),...  13.1 us
    pallas_call x1, Pallas kernels, advance(): pl.pallas_call(functools.partial(advance_kernel, width=width), grid=(node...  13 us
    pallas_call x2, Pallas kernels, pack_pieces(): pl.pallas_call(functools.partial(pieces_kernel, plan=plan, inner=inner, c...  11.3 us
  transfers between devices with their start and end apart: 51, of which 20 were waited for; matrix products, arithmetic and copies ran while one was open for 1% of the time, Pallas kernels for 4%

profile of v2, /device:TPU:25, one launch (start us, length us, event | category | flops | bytes accessed | tf_op | source)
XLA Modules:
  0.0 356.8 jit_solution(18416917853036895627)
XLA Ops:
  1.4 6.2 %all-to-all-start = ((s32[32,1,32]{2,1,0:T(1,128)}), s32[32,1,32]{2,1,0:T(1,128)S(1)}, u32[]{:S(2)}, u32[]{:S(2)}) async-start(s32[32,1,32]{2,1,0:T(1,128)} %broadcast_in_dim.10), calls=%async_computation | async-start | bytes 32768 | tf_op jit(solution)/shard_map/all_to_all | solution.py:425
  13.5 343.1 %conditional.1 = (f32[41,32768]{1,0:T(8,128)}) conditional(s32[]{:T(128)} %clamp.3, (f32[5,40]{1,0:T(8,128)S(1)}, f32[41,32768]{1,0:T(8,128)}, s32[32,1,32]{2,1,0:T(1,128)S(1)}, pred[256]{0:T(512)(128)(4,1)S(1)}, s32[256]{0:T(256)S(1)}, /*index=5*/pred[256]{0:T(512)(128)(4,1)S(1)}, s32[256,128]{1,0:T(8,128)}, ...), branch_computations={%region_4.5_spmd, %region_5.6_spmd, %region_6.7_spmd} | conditional | flops 53743104 | bytes 98723984 | solution.py:436
  14.5 13.0 %advance.4.adv_ref = f32[41,32768]{1,0:T(8,128)} custom-call(f32[5,41,128]{2,1,0:T(8,128)} %broadcast_in_dim.15.params_ref, f32[41,32768]{1,0:T(8,128)} %get-tuple-element.260.states_ref), custom_call_target="tpu_custom_call" | custom-call | flops 53739520 | bytes 10747904 | tf_op jit(solution)/shard_map/cond/branch_1_fun/advance/pallas_call | solution.py:105
  27.5 6.5 %branch_1_fun.2 = (f32[656,128]{1,0:T(8,128)}, f32[656,128]{1,0:T(8,128)}, f32[656,128]{1,0:T(8,128)}, f32[656,128]{1,0:T(8,128)}, f32[656,128]{1,0:T(8,128)}, /...) custom-call(s32[32,1,32]{2,1,0:T(1,128)S(1)} %get-tuple-element.113., ...), custom_call_target="tpu_custom_call" | custom-call | tf_op jit(solution)/shard_map/cond/branch_1_fun/pallas_call | solution.py:224
  42.5 16.0 %collective-permute-done.64.refs_16_ = f32[328,128]{1,0:T(8,128)S(1)} collective-permute-done((f32[328,128]{1,0:T(8,128)}, f32[328,128]{1,0:T(8,128)S(1)}, u32[]{:S(2)}, u32[]{:S(2)}) %collective-permute-start.64) | collective-permute-done | bytes 167968 | tf_op jit(solution)/shard_map/cond/branch_1_fun/ppermute | solution.py:389
  63.9 6.2 %collective-permute-start.70 = (f32[328,128]{1,0:T(8,128)}, f32[328,128]{1,0:T(8,128)S(1)}, u32[]{:S(2)}, u32[]{:S(2)}) collective-permute-start(f32[328,128]{1,0:T(8,128)} %get-tuple-element.138), channel_id=1, source_target_pairs={{0,14},{1,15},{2,12},{3,13},{4,10},{5,11},{6,8},{7,9},{8,6},{9,7},... | collective-permute-start | bytes 503816 | tf_op jit(solution)/shard_map/cond/branch_1_fun/ppermute | solution.py:389
  70.9 12.1 %collective-permute-start.72 = (f32[328,128]{1,0:T(8,128)}, f32[328,128]{1,0:T(8,128)S(1)}, u32[]{:S(2)}, u32[]{:S(2)}) collective-permute-start(f32[328,128]{1,0:T(8,128)} %get-tuple-element.140), channel_id=1, source_target_pairs={{0,20},{1,21},{2,22},{3,23},{4,16},{5,17},{6,18},{7,19},{8,28},{9,... | collective-permute-start | bytes 503816 | tf_op jit(solution)/shard_map/cond/branch_1_fun/ppermute | solution.py:389
  87.4 8.8 %collective-permute-done.69.refs_21_ = f32[328,128]{1,0:T(8,128)S(1)} collective-permute-done((f32[328,128]{1,0:T(8,128)}, f32[328,128]{1,0:T(8,128)S(1)}, u32[]{:S(2)}, u32[]{:S(2)}) %collective-permute-start.69) | collective-permute-done | bytes 167968 | tf_op jit(solution)/shard_map/cond/branch_1_fun/ppermute | solution.py:389
  101.2 10.8 %collective-permute-start.76 = (f32[328,128]{1,0:T(8,128)}, f32[328,128]{1,0:T(8,128)S(1)}, u32[]{:S(2)}, u32[]{:S(2)}) collective-permute-start(f32[328,128]{1,0:T(8,128)} %get-tuple-element.144), channel_id=1, source_target_pairs={{0,28},{1,29},{2,30},{3,31},{4,24},{5,25},{6,26},{7,27},{8,20},{9,... | collective-permute-start | bytes 503816 | tf_op jit(solution)/shard_map/cond/branch_1_fun/ppermute | solution.py:389
  118.5 7.4 %collective-permute-done.73.refs_25_ = f32[328,128]{1,0:T(8,128)S(1)} collective-permute-done((f32[328,128]{1,0:T(8,128)}, f32[328,128]{1,0:T(8,128)S(1)}, u32[]{:S(2)}, u32[]{:S(2)}) %collective-permute-start.73) | collective-permute-done | bytes 167968 | tf_op jit(solution)/shard_map/cond/branch_1_fun/ppermute | solution.py:389
  129.2 5.1 %pack_dense.4 = (f32[656,128]{1,0:T(8,128)}, f32[656,128]{1,0:T(8,128)}, f32[656,128]{1,0:T(8,128)}, f32[656,128]{1,0:T(8,128)}) custom-call(s32[32,1,32]{2,1,0:T(1,128)S(1)} %get-tuple-element.113.table_ref, f32[41,32768]{1,0:T(8,128)} %get-tuple-element.260.states_ref), custom_call_target="tpu_custom_call" | custom-call | tf_op jit(solution)/shard_map/cond/branch_1_fun/pack_dense/pallas_call | solution.py:183
  138.0 15.8 %collective-permute-done.76.refs_28_ = f32[328,128]{1,0:T(8,128)S(1)} collective-permute-done((f32[328,128]{1,0:T(8,128)}, f32[328,128]{1,0:T(8,128)S(1)}, u32[]{:S(2)}, u32[]{:S(2)}) %collective-permute-start.76) | collective-permute-done | bytes 167968 | tf_op jit(solution)/shard_map/cond/branch_1_fun/ppermute | solution.py:389
  159.0 17.6 %collective-permute-start.79 = (f32[328,128]{1,0:T(8,128)S(1)}, f32[328,128]{1,0:T(8,128)S(1)}, u32[]{:S(2)}, u32[]{:S(2)}) collective-permute-start(f32[328,128]{1,0:T(8,128)S(1)} %copy-done.113), channel_id=1, source_target_pairs={{0,31},{1,30},{2,29},{3,28},{4,27},{5,26},{6,25},{7,24},{8,23},{9,... | collective-permute-start | bytes 503816 | tf_op jit(solution)/shard_map/cond/branch_1_fun/ppermute | solution.py:389
  176.7 11.7 %collective-permute-done.79.refs_31_ = f32[328,128]{1,0:T(8,128)S(1)} collective-permute-done((f32[328,128]{1,0:T(8,128)S(1)}, f32[328,128]{1,0:T(8,128)S(1)}, u32[]{:S(2)}, u32[]{:S(2)}) %collective-permute-start.79) | collective-permute-done | bytes 167968 | tf_op jit(solution)/shard_map/cond/branch_1_fun/ppermute | solution.py:389
  191.7 22.3 %collective-permute-start.58 = (f32[656,128]{1,0:T(8,128)}, f32[656,128]{1,0:T(8,128)S(1)}, u32[]{:S(2)}, u32[]{:S(2)}) collective-permute-start(f32[656,128]{1,0:T(8,128)} %get-tuple-element.126), channel_id=1, source_target_pairs={{0,18},{1,19},{2,16},{3,17},{4,22},{5,23},{6,20},{7,21},{8,26},{9,... | collective-permute-start | bytes 1007624 | tf_op jit(solution)/shard_map/cond/branch_1_fun/ppermute | solution.py:389
  217.5 4.8 %branch_1_fun.3 = (f32[656,128]{1,0:T(8,128)}, f32[656,128]{1,0:T(8,128)}, f32[656,128]{1,0:T(8,128)}, f32[656,128]{1,0:T(8,128)}, f32[656,128]{1,0:T(8,128)}, /*index=5*/f32[656,128]{1,0:T(8,128)}, f32[656,128]{1,0:T(8,128)}) custom-call(s32[32,1,32]{2,1,0:T(1,128)S(1)} %get-tuple-element.113.table_ref, f32[41,32768]{1,0:T(8,128)} %advance.4.adv_ref), custom_call_target="tpu_custom_call" | custom-call | tf_op jit(solution)/shard_map/cond/branch_1_fun/pallas_call | solution.py:224
  222.5 22.9 %collective-permute-start.62 = (f32[656,128]{1,0:T(8,128)}, f32[656,128]{1,0:T(8,128)}, u32[]{:S(2)}, u32[]{:S(2)}) collective-permute-start(f32[656,128]{1,0:T(8,128)} %get-tuple-element.130), channel_id=1, source_target_pairs={{0,26},{1,27},{2,24},{3,25},{4,30},{5,31},{6,28},{7,29},{8,18},{9,... | collective-permute-start | bytes 1007624 | tf_op jit(solution)/shard_map/cond/branch_1_fun/ppermute | solution.py:389
  246.7 26.4 %collective-permute-start.50 = (f32[656,128]{1,0:T(8,128)}, f32[656,128]{1,0:T(8,128)}, u32[]{:S(2)}, u32[]{:S(2)}) collective-permute-start(f32[656,128]{1,0:T(8,128)} %get-tuple-element.118), channel_id=1, source_target_pairs={{0,2},{1,3},{2,0},{3,1},{4,6},{5,7},{6,4},{7,5},{8,10},{9,11},{10,... | collective-permute-start | bytes 1007624 | tf_op jit(solution)/shard_map/cond/branch_1_fun/ppermute | solution.py:389
  276.1 5.7 %collective-permute-done.50.refs_2_ = f32[656,128]{1,0:T(8,128)} collective-permute-done((f32[656,128]{1,0:T(8,128)}, f32[656,128]{1,0:T(8,128)}, u32[]{:S(2)}, u32[]{:S(2)}) %collective-permute-start.50) | collective-permute-done | bytes 335904 | tf_op jit(solution)/shard_map/cond/branch_1_fun/ppermute | solution.py:389
  283.4 5.3 %relay.4 = (f32[328,128]{1,0:T(8,128)}, f32[328,128]{1,0:T(8,128)}, f32[328,128]{1,0:T(8,128)}, f32[328,128]{1,0:T(8,128)}, f32[328,128]{1,0:T(8,128)}, /*index=...) custom-call(s32[32,1,32]{2,1,0:T(1,128)S(1)} %get-tuple-element.113., ...), custom_call_target="tpu_custom_call" | custom-call | tf_op jit(solution)/shard_map/cond/branch_1_fun/relay/pallas_call | solution.py:285
  296.7 6.1 %collective-permute-done.55.refs_7_ = f32[656,128]{1,0:T(8,128)} collective-permute-done((f32[656,128]{1,0:T(8,128)}, f32[656,128]{1,0:T(8,128)}, u32[]{:S(2)}, u32[]{:S(2)}) %collective-permute-start.55) | collective-permute-done | bytes 335904 | tf_op jit(solution)/shard_map/cond/branch_1_fun/ppermute | solution.py:389
  319.7 8.6 %collective-permute-done.92.refs_41_ = f32[328,128]{1,0:T(8,128)} collective-permute-done((f32[328,128]{1,0:T(8,128)}, f32[328,128]{1,0:T(8,128)}, u32[]{:S(2)}, u32[]{:S(2)}) %collective-permute-start.92) | collective-permute-done | bytes 167968 | tf_op jit(solution)/shard_map/cond/branch_1_fun/ppermute | solution.py:389
  332.0 10.8 %collective-permute-done.95.refs_44_ = f32[328,128]{1,0:T(8,128)} collective-permute-done((f32[328,128]{1,0:T(8,128)}, f32[328,128]{1,0:T(8,128)}, u32[]{:S(2)}, u32[]{:S(2)}) %collective-permute-start.95) | collective-permute-done | bytes 167968 | tf_op jit(solution)/shard_map/cond/branch_1_fun/ppermute | solution.py:389
  343.0 13.1 %unpack.4 = f32[41,32768]{1,0:T(8,128)} custom-call(s32[256]{0:T(256)} %multiply_add_fusion.3.base_ref, s32[256]{0:T(256)} %get-tuple-element.371.tail_ref, s32[256]{0:T(256)} %get-tuple-element.372.step_ref, s32[256,128]{1,0:T(8,128)S(1)} %copy-done.1, f32[656,128]{1,0:T(8,128)} %get-tuple-element.116.refs_0_, f32[656,128]{1,0:T(8,128)} %collective-permute-done.49.refs_1_, ...), custom_call_target="tpu_custom_call" | custom-call | tf_op jit(solution)/shard_map/cond/branch_1_fun/unpack/pallas_call | solution.py:340
  (174 shorter events, 90.8 us)
Async XLA Ops:
  37.4 32.7 %collective-permute-start.66 = (f32[328,128]{1,0:T(8,128)}, f32[328,128]{1,0:T(8,128)S(1)}, u32[]{:S(2)}, u32[]{:S(2)}) collective-permute-start(f32[328,128]{1,0:T(8,128)} %get-tuple-element.134), channel_id=1, source_target_pairs={{0,6},{1,7},{2,4},{3,5},{4,2},{5,3},{6,0},{7,1},{8,14},{9,15},{10,... | collective-permute-start | bytes 503816 | tf_op jit(solution)/shard_map/cond/branch_1_fun/ppermute | solution.py:389
  39.4 31.5 %collective-permute-start.67 = (f32[328,128]{1,0:T(8,128)}, f32[328,128]{1,0:T(8,128)S(1)}, u32[]{:S(2)}, u32[]{:S(2)}) collective-permute-start(f32[328,128]{1,0:T(8,128)} %get-tuple-element.135), channel_id=1, source_target_pairs={{0,7},{1,6},{2,5},{3,4},{4,3},{5,2},{6,1},{7,0},{8,15},{9,14},{10,... | collective-permute-start | bytes 503816 | tf_op jit(solution)/shard_map/cond/branch_1_fun/ppermute | solution.py:389
  40.6 45.1 %collective-permute-start.68 = (f32[328,128]{1,0:T(8,128)}, f32[328,128]{1,0:T(8,128)S(1)}, u32[]{:S(2)}, u32[]{:S(2)}) collective-permute-start(f32[328,128]{1,0:T(8,128)} %get-tuple-element.136), channel_id=1, source_target_pairs={{0,12},{1,13},{2,14},{3,15},{4,8},{5,9},{6,10},{7,11},{8,4},{9,5},... | collective-permute-start | bytes 503816 | tf_op jit(solution)/shard_map/cond/branch_1_fun/ppermute | solution.py:389
  58.5 37.7 %collective-permute-start.69 = (f32[328,128]{1,0:T(8,128)}, f32[328,128]{1,0:T(8,128)S(1)}, u32[]{:S(2)}, u32[]{:S(2)}) collective-permute-start(f32[328,128]{1,0:T(8,128)} %get-tuple-element.137), channel_id=1, source_target_pairs={{0,13},{1,12},{2,15},{3,14},{4,9},{5,8},{6,11},{7,10},{8,5},{9,4},... | collective-permute-start | bytes 503816 | tf_op jit(solution)/shard_map/cond/branch_1_fun/ppermute | solution.py:389
  63.9 34.5 %collective-permute-start.70 = (f32[328,128]{1,0:T(8,128)}, f32[328,128]{1,0:T(8,128)S(1)}, u32[]{:S(2)}, u32[]{:S(2)}) collective-permute-start(f32[328,128]{1,0:T(8,128)} %get-tuple-element.138), channel_id=1, source_target_pairs={{0,14},{1,15},{2,12},{3,13},{4,10},{5,11},{6,8},{7,9},{8,6},{9,7},... | collective-permute-start | bytes 503816 | tf_op jit(solution)/shard_map/cond/branch_1_fun/ppermute | solution.py:389
  70.9 43.3 %collective-permute-start.72 = (f32[328,128]{1,0:T(8,128)}, f32[328,128]{1,0:T(8,128)S(1)}, u32[]{:S(2)}, u32[]{:S(2)}) collective-permute-start(f32[328,128]{1,0:T(8,128)} %get-tuple-element.140), channel_id=1, source_target_pairs={{0,20},{1,21},{2,22},{3,23},{4,16},{5,17},{6,18},{7,19},{8,28},{9,... | collective-permute-start | bytes 503816 | tf_op jit(solution)/shard_map/cond/branch_1_fun/ppermute | solution.py:389
  85.7 40.3 %collective-permute-start.73 = (f32[328,128]{1,0:T(8,128)}, f32[328,128]{1,0:T(8,128)S(1)}, u32[]{:S(2)}, u32[]{:S(2)}) collective-permute-start(f32[328,128]{1,0:T(8,128)} %get-tuple-element.141), channel_id=1, source_target_pairs={{0,21},{1,20},{2,23},{3,22},{4,17},{5,16},{6,19},{7,18},{8,29},{9,... | collective-permute-start | bytes 503816 | tf_op jit(solution)/shard_map/cond/branch_1_fun/ppermute | solution.py:389
  96.3 38.1 %collective-permute-start.74 = (f32[328,128]{1,0:T(8,128)}, f32[328,128]{1,0:T(8,128)S(1)}, u32[]{:S(2)}, u32[]{:S(2)}) collective-permute-start(f32[328,128]{1,0:T(8,128)} %get-tuple-element.142), channel_id=1, source_target_pairs={{0,22},{1,23},{2,20},{3,21},{4,18},{5,19},{6,16},{7,17},{8,30},{9,... | collective-permute-start | bytes 503816 | tf_op jit(solution)/shard_map/cond/branch_1_fun/ppermute | solution.py:389
  98.3 36.7 %collective-permute-start.75 = (f32[328,128]{1,0:T(8,128)}, f32[328,128]{1,0:T(8,128)S(1)}, u32[]{:S(2)}, u32[]{:S(2)}) collective-permute-start(f32[328,128]{1,0:T(8,128)} %get-tuple-element.143), channel_id=1, source_target_pairs={{0,23},{1,22},{2,21},{3,20},{4,19},{5,18},{6,17},{7,16},{8,31},{9,... | collective-permute-start | bytes 503816 | tf_op jit(solution)/shard_map/cond/branch_1_fun/ppermute | solution.py:389
  101.2 52.6 %collective-permute-start.76 = (f32[328,128]{1,0:T(8,128)}, f32[328,128]{1,0:T(8,128)S(1)}, u32[]{:S(2)}, u32[]{:S(2)}) collective-permute-start(f32[328,128]{1,0:T(8,128)} %get-tuple-element.144), channel_id=1, source_target_pairs={{0,28},{1,29},{2,30},{3,31},{4,24},{5,25},{6,26},{7,27},{8,20},{9,... | collective-permute-start | bytes 503816 | tf_op jit(solution)/shard_map/cond/branch_1_fun/ppermute | solution.py:389
  114.3 44.1 %collective-permute-start.77 = (f32[328,128]{1,0:T(8,128)}, f32[328,128]{1,0:T(8,128)S(1)}, u32[]{:S(2)}, u32[]{:S(2)}) collective-permute-start(f32[328,128]{1,0:T(8,128)} %get-tuple-element.145), channel_id=1, source_target_pairs={{0,29},{1,28},{2,31},{3,30},{4,25},{5,24},{6,27},{7,26},{8,21},{9,... | collective-permute-start | bytes 503816 | tf_op jit(solution)/shard_map/cond/branch_1_fun/ppermute | solution.py:389
  126.7 32.4 %collective-permute-start.78 = (f32[328,128]{1,0:T(8,128)}, f32[328,128]{1,0:T(8,128)S(1)}, u32[]{:S(2)}, u32[]{:S(2)}) collective-permute-start(f32[328,128]{1,0:T(8,128)} %get-tuple-element.146), channel_id=1, source_target_pairs={{0,30},{1,31},{2,28},{3,29},{4,26},{5,27},{6,24},{7,25},{8,22},{9,... | collective-permute-start | bytes 503816 | tf_op jit(solution)/shard_map/cond/branch_1_fun/ppermute | solution.py:389
  135.0 54.4 %collective-permute-start.80 = (f32[656,128]{1,0:T(8,128)}, f32[656,128]{1,0:T(8,128)S(1)}, u32[]{:S(2)}, u32[]{:S(2)}) collective-permute-start(f32[656,128]{1,0:T(8,128)} %get-tuple-element.148), channel_id=1, source_target_pairs={{0,4},{1,5},{2,6},{3,7},{4,0},{5,1},{6,2},{7,3},{8,12},{9,13},{10,... | collective-permute-start | bytes 1007624 | tf_op jit(solution)/shard_map/cond/branch_1_fun/ppermute | solution.py:395
  135.7 56.0 %collective-permute-start.81 = (f32[656,128]{1,0:T(8,128)}, f32[656,128]{1,0:T(8,128)S(1)}, u32[]{:S(2)}, u32[]{:S(2)}) collective-permute-start(f32[656,128]{1,0:T(8,128)} %get-tuple-element.149), channel_id=1, source_target_pairs={{0,4},{1,5},{2,6},{3,7},{4,0},{5,1},{6,2},{7,3},{8,12},{9,13},{10,... | collective-permute-start | bytes 1007624 | tf_op jit(solution)/shard_map/cond/branch_1_fun/ppermute | solution.py:395
  154.5 59.5 %collective-permute-start.82 = (f32[656,128]{1,0:T(8,128)}, f32[656,128]{1,0:T(8,128)S(1)}, u32[]{:S(2)}, u32[]{:S(2)}) collective-permute-start(f32[656,128]{1,0:T(8,128)} %get-tuple-element.150), channel_id=1, source_target_pairs={{0,4},{1,5},{2,6},{3,7},{4,0},{5,1},{6,2},{7,3},{8,12},{9,13},{10,... | collective-permute-start | bytes 1007624 | tf_op jit(solution)/shard_map/cond/branch_1_fun/ppermute | solution.py:395
  159.0 56.1 %collective-permute-start.83 = (f32[656,128]{1,0:T(8,128)}, f32[656,128]{1,0:T(8,128)S(1)}, u32[]{:S(2)}, u32[]{:S(2)}) collective-permute-start(f32[656,128]{1,0:T(8,128)} %get-tuple-element.151), channel_id=1, source_target_pairs={{0,4},{1,5},{2,6},{3,7},{4,0},{5,1},{6,2},{7,3},{8,12},{9,13},{10,... | collective-permute-start | bytes 1007624 | tf_op jit(solution)/shard_map/cond/branch_1_fun/ppermute | solution.py:395
  188.4 34.0 %collective-permute-start.56 = (f32[656,128]{1,0:T(8,128)S(1)}, f32[656,128]{1,0:T(8,128)S(1)}, u32[]{:S(2)}, u32[]{:S(2)}) collective-permute-start(f32[656,128]{1,0:T(8,128)S(1)} %copy-done.110), channel_id=1, source_target_pairs={{0,16},{1,17},{2,18},{3,19},{4,20},{5,21},{6,22},{7,23},{8,24},{9,... | collective-permute-start | bytes 1007624 | tf_op jit(solution)/shard_map/cond/branch_1_fun/ppermute | solution.py:389
  189.4 33.1 %collective-permute-start.57 = (f32[656,128]{1,0:T(8,128)}, f32[656,128]{1,0:T(8,128)S(1)}, u32[]{:S(2)}, u32[]{:S(2)}) collective-permute-start(f32[656,128]{1,0:T(8,128)} %get-tuple-element.125), channel_id=1, source_target_pairs={{0,17},{1,16},{2,19},{3,18},{4,21},{5,20},{6,23},{7,22},{8,25},{9,... | collective-permute-start | bytes 1007624 | tf_op jit(solution)/shard_map/cond/branch_1_fun/ppermute | solution.py:389
  191.7 53.7 %collective-permute-start.58 = (f32[656,128]{1,0:T(8,128)}, f32[656,128]{1,0:T(8,128)S(1)}, u32[]{:S(2)}, u32[]{:S(2)}) collective-permute-start(f32[656,128]{1,0:T(8,128)} %get-tuple-element.126), channel_id=1, source_target_pairs={{0,18},{1,19},{2,16},{3,17},{4,22},{5,23},{6,20},{7,21},{8,26},{9,... | collective-permute-start | bytes 1007624 | tf_op jit(solution)/shard_map/cond/branch_1_fun/ppermute | solution.py:389
  214.0 31.8 %collective-permute-start.59 = (f32[656,128]{1,0:T(8,128)}, f32[656,128]{1,0:T(8,128)S(1)}, u32[]{:S(2)}, u32[]{:S(2)}) collective-permute-start(f32[656,128]{1,0:T(8,128)} %get-tuple-element.127), channel_id=1, source_target_pairs={{0,19},{1,18},{2,17},{3,16},{4,23},{5,22},{6,21},{7,20},{8,27},{9,... | collective-permute-start | bytes 1007624 | tf_op jit(solution)/shard_map/cond/branch_1_fun/ppermute | solution.py:389
  215.1 31.5 %collective-permute-start.60 = (f32[656,128]{1,0:T(8,128)}, f32[656,128]{1,0:T(8,128)S(1)}, u32[]{:S(2)}, u32[]{:S(2)}) collective-permute-start(f32[656,128]{1,0:T(8,128)} %get-tuple-element.128), channel_id=1, source_target_pairs={{0,24},{1,25},{2,26},{3,27},{4,28},{5,29},{6,30},{7,31},{8,16},{9,... | collective-permute-start | bytes 1007624 | tf_op jit(solution)/shard_map/cond/branch_1_fun/ppermute | solution.py:389
  222.3 50.8 %collective-permute-start.61 = (f32[656,128]{1,0:T(8,128)}, f32[656,128]{1,0:T(8,128)S(1)}, u32[]{:S(2)}, u32[]{:S(2)}) collective-permute-start(f32[656,128]{1,0:T(8,128)} %get-tuple-element.129), channel_id=1, source_target_pairs={{0,25},{1,24},{2,27},{3,26},{4,29},{5,28},{6,31},{7,30},{8,17},{9,... | collective-permute-start | bytes 1007624 | tf_op jit(solution)/shard_map/cond/branch_1_fun/ppermute | solution.py:389
  222.5 50.7 %collective-permute-start.62 = (f32[656,128]{1,0:T(8,128)}, f32[656,128]{1,0:T(8,128)}, u32[]{:S(2)}, u32[]{:S(2)}) collective-permute-start(f32[656,128]{1,0:T(8,128)} %get-tuple-element.130), channel_id=1, source_target_pairs={{0,26},{1,27},{2,24},{3,25},{4,30},{5,31},{6,28},{7,29},{8,18},{9,... | collective-permute-start | bytes 1007624 | tf_op jit(solution)/shard_map/cond/branch_1_fun/ppermute | solution.py:389
  246.7 35.2 %collective-permute-start.50 = (f32[656,128]{1,0:T(8,128)}, f32[656,128]{1,0:T(8,128)}, u32[]{:S(2)}, u32[]{:S(2)}) collective-permute-start(f32[656,128]{1,0:T(8,128)} %get-tuple-element.118), channel_id=1, source_target_pairs={{0,2},{1,3},{2,0},{3,1},{4,6},{5,7},{6,4},{7,5},{8,10},{9,11},{10,... | collective-permute-start | bytes 1007624 | tf_op jit(solution)/shard_map/cond/branch_1_fun/ppermute | solution.py:389
  (64 other events, 2607.0 us)

commit v3 on v2

--- a/solution.py
+++ b/solution.py
@@ -379,9 +379,17 @@
     return origin + slot * plan.full, origin + slots * plan.full + slot, slots
 
 
+def mixed(mates):
+    pairs = [(d, mates - 1 - d) for d in range(mates // 2)]
+    return [d for pair in pairs[1:] + pairs[:1] for d in pair]
+
+
+def early_inner(mates):
+    return [d for d in mixed(mates) if d][: mates // 2 - 1]
+
+
 def exchange(plan, chunks, table, states, params, places, tile_perm):
     over = range(plan.devices)
-    split = plan.mates // 2
     ends = {"inner": plan.half, "again": plan.half, "cross": lambda i: 1 - plan.half(i)}
 
     def send(kind, d, piece):
@@ -395,8 +403,8 @@
             lax.ppermute(dense[c], both, [(i, plan.partner(i)) for i in over])
         )
     adv = advance(params, states)
-    first = list(range(1, split))
-    second = [0] + list(range(split, plan.mates))
+    first = early_inner(plan.mates)
+    second = [d for d in range(plan.mates) if d not in first]
     inner = dict(zip(first, pack_pieces(plan, table, adv, first, [])))
     more = pack_pieces(plan, table, adv, second, list(range(plan.mates)))
     inner.update(zip(second, more))

time: 361 us -> 344 us (0.953)
  starting transfers between devices: 183 us -> 165 us
    ppermute x46, starting transfers between devices: 174 us -> 157 us  [send(): return lax.ppermute(piece, both, pairs)]
  transfers between devices with their start and end apart: 51 -> 51, of which waited for: 20 -> 19; matrix products, arithmetic and copies ran while one was open for 1% -> 1% of each run, Pallas kernels for 4% -> 4%
where the time goes in v3:
time: 344 us; the launch traced here: 339 us
  starting transfers between devices  165 us (48%)
  waiting for transfers between devices  112 us (33%)
  Pallas kernels  47.8 us (14%)
  other arithmetic  5.71 us (2%)
  local copies, waits for them, and re-layouts  5.55 us (2%)
    ppermute x46, starting transfers between devices, send(): return lax.ppermute(piece, both, pairs)  157 us
    ppermute x46, waiting for transfers between devices, send(): return lax.ppermute(piece, both, pairs)  112 us
    pallas_call x1, Pallas kernels, unpack(): pl.pallas_call(functools.partial(unpack_kernel, plan=plan, sizes=sizes),...  13.1 us
    pallas_call x1, Pallas kernels, advance(): pl.pallas_call(functools.partial(advance_kernel, width=width), grid=(node...  13 us
    pallas_call x2, Pallas kernels, pack_pieces(): pl.pallas_call(functools.partial(pieces_kernel, plan=plan, inner=inner, c...  11.3 us
  transfers between devices with their start and end apart: 51, of which 19 were waited for; matrix products, arithmetic and copies ran while one was open for 1% of the time, Pallas kernels for 4%

profile of v3, /device:TPU:25, one launch (start us, length us, event | category | flops | bytes accessed | tf_op | source)
XLA Modules:
  0.0 339.5 jit_solution(12293796884946580329)
XLA Ops:
  1.4 6.2 %all-to-all-start = ((s32[32,1,32]{2,1,0:T(1,128)}), s32[32,1,32]{2,1,0:T(1,128)S(1)}, u32[]{:S(2)}, u32[]{:S(2)}) async-start(s32[32,1,32]{2,1,0:T(1,128)} %broadcast_in_dim.10), calls=%async_computation | async-start | bytes 32768 | tf_op jit(solution)/shard_map/all_to_all | solution.py:433
  13.5 325.8 %conditional.1 = (f32[41,32768]{1,0:T(8,128)}) conditional(s32[]{:T(128)} %clamp.3, (f32[5,40]{1,0:T(8,128)S(1)}, f32[41,32768]{1,0:T(8,128)}, s32[32,1,32]{2,1,0:T(1,128)S(1)}, pred[256]{0:T(512)(128)(4,1)S(1)}, s32[256]{0:T(256)S(1)}, /*index=5*/pred[256]{0:T(512)(128)(4,1)S(1)}, s32[256,128]{1,0:T(8,128)}, ...), branch_computations={%region_4.5_spmd, %region_5.6_spmd, %region_6.7_spmd} | conditional | flops 53743104 | bytes 98723984 | solution.py:444
  14.5 13.0 %advance.4.adv_ref = f32[41,32768]{1,0:T(8,128)} custom-call(f32[5,41,128]{2,1,0:T(8,128)} %broadcast_in_dim.15.params_ref, f32[41,32768]{1,0:T(8,128)} %get-tuple-element.260.states_ref), custom_call_target="tpu_custom_call" | custom-call | flops 53739520 | bytes 10747904 | tf_op jit(solution)/shard_map/cond/branch_1_fun/advance/pallas_call | solution.py:105
  27.5 6.5 %branch_1_fun.2 = (f32[656,128]{1,0:T(8,128)}, f32[656,128]{1,0:T(8,128)}, f32[656,128]{1,0:T(8,128)}, f32[656,128]{1,0:T(8,128)}, f32[656,128]{1,0:T(8,128)}, /...) custom-call(s32[32,1,32]{2,1,0:T(1,128)S(1)} %get-tuple-element.113., ...), custom_call_target="tpu_custom_call" | custom-call | tf_op jit(solution)/shard_map/cond/branch_1_fun/pallas_call | solution.py:224
  42.5 16.0 %collective-permute-done.64.refs_16_ = f32[328,128]{1,0:T(8,128)S(1)} collective-permute-done((f32[328,128]{1,0:T(8,128)}, f32[328,128]{1,0:T(8,128)S(1)}, u32[]{:S(2)}, u32[]{:S(2)}) %collective-permute-start.64) | collective-permute-done | bytes 167968 | tf_op jit(solution)/shard_map/cond/branch_1_fun/ppermute | solution.py:397
  63.9 6.2 %collective-permute-start.70 = (f32[328,128]{1,0:T(8,128)}, f32[328,128]{1,0:T(8,128)S(1)}, u32[]{:S(2)}, u32[]{:S(2)}) collective-permute-start(f32[328,128]{1,0:T(8,128)} %get-tuple-element.138), channel_id=1, source_target_pairs={{0,14},{1,15},{2,12},{3,13},{4,10},{5,11},{6,8},{7,9},{8,6},{9,7},... | collective-permute-start | bytes 503816 | tf_op jit(solution)/shard_map/cond/branch_1_fun/ppermute | solution.py:397
  70.9 12.1 %collective-permute-start.72 = (f32[328,128]{1,0:T(8,128)}, f32[328,128]{1,0:T(8,128)S(1)}, u32[]{:S(2)}, u32[]{:S(2)}) collective-permute-start(f32[328,128]{1,0:T(8,128)} %get-tuple-element.140), channel_id=1, source_target_pairs={{0,20},{1,21},{2,22},{3,23},{4,16},{5,17},{6,18},{7,19},{8,28},{9,... | collective-permute-start | bytes 503816 | tf_op jit(solution)/shard_map/cond/branch_1_fun/ppermute | solution.py:397
  87.4 8.8 %collective-permute-done.69.refs_21_ = f32[328,128]{1,0:T(8,128)S(1)} collective-permute-done((f32[328,128]{1,0:T(8,128)}, f32[328,128]{1,0:T(8,128)S(1)}, u32[]{:S(2)}, u32[]{:S(2)}) %collective-permute-start.69) | collective-permute-done | bytes 167968 | tf_op jit(solution)/shard_map/cond/branch_1_fun/ppermute | solution.py:397
  101.3 10.8 %collective-permute-start.76 = (f32[328,128]{1,0:T(8,128)}, f32[328,128]{1,0:T(8,128)S(1)}, u32[]{:S(2)}, u32[]{:S(2)}) collective-permute-start(f32[328,128]{1,0:T(8,128)} %get-tuple-element.144), channel_id=1, source_target_pairs={{0,28},{1,29},{2,30},{3,31},{4,24},{5,25},{6,26},{7,27},{8,20},{9,... | collective-permute-start | bytes 503816 | tf_op jit(solution)/shard_map/cond/branch_1_fun/ppermute | solution.py:397
  118.6 7.4 %collective-permute-done.73.refs_25_ = f32[328,128]{1,0:T(8,128)S(1)} collective-permute-done((f32[328,128]{1,0:T(8,128)}, f32[328,128]{1,0:T(8,128)S(1)}, u32[]{:S(2)}, u32[]{:S(2)}) %collective-permute-start.73) | collective-permute-done | bytes 167968 | tf_op jit(solution)/shard_map/cond/branch_1_fun/ppermute | solution.py:397
  129.2 5.1 %pack_dense.4 = (f32[656,128]{1,0:T(8,128)}, f32[656,128]{1,0:T(8,128)}, f32[656,128]{1,0:T(8,128)}, f32[656,128]{1,0:T(8,128)}) custom-call(s32[32,1,32]{2,1,0:T(1,128)S(1)} %get-tuple-element.113.table_ref, f32[41,32768]{1,0:T(8,128)} %get-tuple-element.260.states_ref), custom_call_target="tpu_custom_call" | custom-call | tf_op jit(solution)/shard_map/cond/branch_1_fun/pack_dense/pallas_call | solution.py:183
  138.1 15.8 %collective-permute-done.76.refs_28_ = f32[328,128]{1,0:T(8,128)S(1)} collective-permute-done((f32[328,128]{1,0:T(8,128)}, f32[328,128]{1,0:T(8,128)S(1)}, u32[]{:S(2)}, u32[]{:S(2)}) %collective-permute-start.76) | collective-permute-done | bytes 167968 | tf_op jit(solution)/shard_map/cond/branch_1_fun/ppermute | solution.py:397
  159.1 17.6 %collective-permute-start.79 = (f32[328,128]{1,0:T(8,128)S(1)}, f32[328,128]{1,0:T(8,128)S(1)}, u32[]{:S(2)}, u32[]{:S(2)}) collective-permute-start(f32[328,128]{1,0:T(8,128)S(1)} %copy-done.113), channel_id=1, source_target_pairs={{0,31},{1,30},{2,29},{3,28},{4,27},{5,26},{6,25},{7,24},{8,23},{9,... | collective-permute-start | bytes 503816 | tf_op jit(solution)/shard_map/cond/branch_1_fun/ppermute | solution.py:397
  176.7 11.7 %collective-permute-done.79.refs_31_ = f32[328,128]{1,0:T(8,128)S(1)} collective-permute-done((f32[328,128]{1,0:T(8,128)S(1)}, f32[328,128]{1,0:T(8,128)S(1)}, u32[]{:S(2)}, u32[]{:S(2)}) %collective-permute-start.79) | collective-permute-done | bytes 167968 | tf_op jit(solution)/shard_map/cond/branch_1_fun/ppermute | solution.py:397
  188.5 24.8 %collective-permute-start.54 = (f32[656,128]{1,0:T(8,128)}, f32[656,128]{1,0:T(8,128)S(1)}, u32[]{:S(2)}, u32[]{:S(2)}) collective-permute-start(f32[656,128]{1,0:T(8,128)} %get-tuple-element.122), channel_id=1, source_target_pairs={{0,10},{1,11},{2,8},{3,9},{4,14},{5,15},{6,12},{7,13},{8,2},{9,3},... | collective-permute-start | bytes 1007624 | tf_op jit(solution)/shard_map/cond/branch_1_fun/ppermute | solution.py:397
  215.8 4.8 %branch_1_fun.3 = (f32[656,128]{1,0:T(8,128)}, f32[656,128]{1,0:T(8,128)}, f32[656,128]{1,0:T(8,128)}, f32[656,128]{1,0:T(8,128)}, f32[656,128]{1,0:T(8,128)}, /*index=5*/f32[656,128]{1,0:T(8,128)}, f32[656,128]{1,0:T(8,128)}) custom-call(s32[32,1,32]{2,1,0:T(1,128)S(1)} %get-tuple-element.113.table_ref, f32[41,32768]{1,0:T(8,128)} %advance.4.adv_ref), custom_call_target="tpu_custom_call" | custom-call | tf_op jit(solution)/shard_map/cond/branch_1_fun/pallas_call | solution.py:224
  224.8 5.5 %collective-permute-done.55.refs_7_ = f32[656,128]{1,0:T(8,128)S(1)} collective-permute-done((f32[656,128]{1,0:T(8,128)}, f32[656,128]{1,0:T(8,128)S(1)}, u32[]{:S(2)}, u32[]{:S(2)}) %collective-permute-start.55) | collective-permute-done | bytes 335904 | tf_op jit(solution)/shard_map/cond/branch_1_fun/ppermute | solution.py:397
  233.2 8.8 %collective-permute-start.50 = (f32[656,128]{1,0:T(8,128)}, f32[656,128]{1,0:T(8,128)}, u32[]{:S(2)}, u32[]{:S(2)}) collective-permute-start(f32[656,128]{1,0:T(8,128)} %get-tuple-element.118), channel_id=1, source_target_pairs={{0,2},{1,3},{2,0},{3,1},{4,6},{5,7},{6,4},{7,5},{8,10},{9,11},{10,... | collective-permute-start | bytes 1007624 | tf_op jit(solution)/shard_map/cond/branch_1_fun/ppermute | solution.py:397
  249.0 5.7 %collective-permute-done.63.refs_15_ = f32[656,128]{1,0:T(8,128)} collective-permute-done((f32[656,128]{1,0:T(8,128)}, f32[656,128]{1,0:T(8,128)}, u32[]{:S(2)}, u32[]{:S(2)}) %collective-permute-start.63) | collective-permute-done | bytes 335904 | tf_op jit(solution)/shard_map/cond/branch_1_fun/ppermute | solution.py:397
  265.0 5.3 %relay.4 = (f32[328,128]{1,0:T(8,128)}, f32[328,128]{1,0:T(8,128)}, f32[328,128]{1,0:T(8,128)}, f32[328,128]{1,0:T(8,128)}, f32[328,128]{1,0:T(8,128)}, /*index=...) custom-call(s32[32,1,32]{2,1,0:T(1,128)S(1)} %get-tuple-element.113., ...), custom_call_target="tpu_custom_call" | custom-call | tf_op jit(solution)/shard_map/cond/branch_1_fun/relay/pallas_call | solution.py:285
  284.0 9.2 %collective-permute-start.89 = (f32[328,128]{1,0:T(8,128)}, f32[328,128]{1,0:T(8,128)S(1)}, u32[]{:S(2)}, u32[]{:S(2)}) collective-permute-start(f32[328,128]{1,0:T(8,128)} %get-tuple-element.158), channel_id=1, source_target_pairs={{0,10},{1,11},{2,8},{3,9},{4,14},{5,15},{6,12},{7,13},{8,2},{9,3},... | collective-permute-start | bytes 503816 | tf_op jit(solution)/shard_map/cond/branch_1_fun/ppermute | solution.py:397
  307.9 4.9 %collective-permute-start.98 = (f32[328,128]{1,0:T(8,128)}, f32[328,128]{1,0:T(8,128)}, u32[]{:S(2)}, u32[]{:S(2)}) collective-permute-start(f32[328,128]{1,0:T(8,128)} %get-tuple-element.167), channel_id=1, source_target_pairs={{0,27},{1,26},{2,25},{3,24},{4,31},{5,30},{6,29},{7,28},{8,19},{9,... | collective-permute-start | bytes 503816 | tf_op jit(solution)/shard_map/cond/branch_1_fun/ppermute | solution.py:397
  313.5 12.1 %collective-permute-done.95.refs_44_ = f32[328,128]{1,0:T(8,128)} collective-permute-done((f32[328,128]{1,0:T(8,128)}, f32[328,128]{1,0:T(8,128)}, u32[]{:S(2)}, u32[]{:S(2)}) %collective-permute-start.95) | collective-permute-done | bytes 167968 | tf_op jit(solution)/shard_map/cond/branch_1_fun/ppermute | solution.py:397
  325.7 13.1 %unpack.4 = f32[41,32768]{1,0:T(8,128)} custom-call(s32[256]{0:T(256)} %multiply_add_fusion.3.base_ref, s32[256]{0:T(256)} %get-tuple-element.371.tail_ref, s32[256]{0:T(256)} %get-tuple-element.372.step_ref, s32[256,128]{1,0:T(8,128)S(1)} %copy-done.1, f32[656,128]{1,0:T(8,128)} %get-tuple-element.116.refs_0_, f32[656,128]{1,0:T(8,128)} %collective-permute-done.49.refs_1_, ...), custom_call_target="tpu_custom_call" | custom-call | tf_op jit(solution)/shard_map/cond/branch_1_fun/unpack/pallas_call | solution.py:340
  (174 shorter events, 105.4 us)
Async XLA Ops:
  34.0 24.5 %collective-permute-start.64 = (f32[328,128]{1,0:T(8,128)}, f32[328,128]{1,0:T(8,128)S(1)}, u32[]{:S(2)}, u32[]{:S(2)}) collective-permute-start(f32[328,128]{1,0:T(8,128)} %get-tuple-element.132), channel_id=1, source_target_pairs={{0,4},{1,5},{2,6},{3,7},{4,0},{5,1},{6,2},{7,3},{8,12},{9,13},{10,... | collective-permute-start | bytes 503816 | tf_op jit(solution)/shard_map/cond/branch_1_fun/ppermute | solution.py:397
  36.1 27.8 %collective-permute-start.65 = (f32[328,128]{1,0:T(8,128)}, f32[328,128]{1,0:T(8,128)S(1)}, u32[]{:S(2)}, u32[]{:S(2)}) collective-permute-start(f32[328,128]{1,0:T(8,128)} %get-tuple-element.133), channel_id=1, source_target_pairs={{0,5},{1,4},{2,7},{3,6},{4,1},{5,0},{6,3},{7,2},{8,13},{9,12},{10,... | collective-permute-start | bytes 503816 | tf_op jit(solution)/shard_map/cond/branch_1_fun/ppermute | solution.py:397
  37.4 32.7 %collective-permute-start.66 = (f32[328,128]{1,0:T(8,128)}, f32[328,128]{1,0:T(8,128)S(1)}, u32[]{:S(2)}, u32[]{:S(2)}) collective-permute-start(f32[328,128]{1,0:T(8,128)} %get-tuple-element.134), channel_id=1, source_target_pairs={{0,6},{1,7},{2,4},{3,5},{4,2},{5,3},{6,0},{7,1},{8,14},{9,15},{10,... | collective-permute-start | bytes 503816 | tf_op jit(solution)/shard_map/cond/branch_1_fun/ppermute | solution.py:397
  39.4 31.5 %collective-permute-start.67 = (f32[328,128]{1,0:T(8,128)}, f32[328,128]{1,0:T(8,128)S(1)}, u32[]{:S(2)}, u32[]{:S(2)}) collective-permute-start(f32[328,128]{1,0:T(8,128)} %get-tuple-element.135), channel_id=1, source_target_pairs={{0,7},{1,6},{2,5},{3,4},{4,3},{5,2},{6,1},{7,0},{8,15},{9,14},{10,... | collective-permute-start | bytes 503816 | tf_op jit(solution)/shard_map/cond/branch_1_fun/ppermute | solution.py:397
  40.6 45.1 %collective-permute-start.68 = (f32[328,128]{1,0:T(8,128)}, f32[328,128]{1,0:T(8,128)S(1)}, u32[]{:S(2)}, u32[]{:S(2)}) collective-permute-start(f32[328,128]{1,0:T(8,128)} %get-tuple-element.136), channel_id=1, source_target_pairs={{0,12},{1,13},{2,14},{3,15},{4,8},{5,9},{6,10},{7,11},{8,4},{9,5},... | collective-permute-start | bytes 503816 | tf_op jit(solution)/shard_map/cond/branch_1_fun/ppermute | solution.py:397
  58.5 37.7 %collective-permute-start.69 = (f32[328,128]{1,0:T(8,128)}, f32[328,128]{1,0:T(8,128)S(1)}, u32[]{:S(2)}, u32[]{:S(2)}) collective-permute-start(f32[328,128]{1,0:T(8,128)} %get-tuple-element.137), channel_id=1, source_target_pairs={{0,13},{1,12},{2,15},{3,14},{4,9},{5,8},{6,11},{7,10},{8,5},{9,4},... | collective-permute-start | bytes 503816 | tf_op jit(solution)/shard_map/cond/branch_1_fun/ppermute | solution.py:397
  63.9 34.5 %collective-permute-start.70 = (f32[328,128]{1,0:T(8,128)}, f32[328,128]{1,0:T(8,128)S(1)}, u32[]{:S(2)}, u32[]{:S(2)}) collective-permute-start(f32[328,128]{1,0:T(8,128)} %get-tuple-element.138), channel_id=1, source_target_pairs={{0,14},{1,15},{2,12},{3,13},{4,10},{5,11},{6,8},{7,9},{8,6},{9,7},... | collective-permute-start | bytes 503816 | tf_op jit(solution)/shard_map/cond/branch_1_fun/ppermute | solution.py:397
  70.0 31.2 %collective-permute-start.71 = (f32[328,128]{1,0:T(8,128)}, f32[328,128]{1,0:T(8,128)S(1)}, u32[]{:S(2)}, u32[]{:S(2)}) collective-permute-start(f32[328,128]{1,0:T(8,128)} %get-tuple-element.139), channel_id=1, source_target_pairs={{0,15},{1,14},{2,13},{3,12},{4,11},{5,10},{6,9},{7,8},{8,7},{9,6},... | collective-permute-start | bytes 503816 | tf_op jit(solution)/shard_map/cond/branch_1_fun/ppermute | solution.py:397
  70.9 43.3 %collective-permute-start.72 = (f32[328,128]{1,0:T(8,128)}, f32[328,128]{1,0:T(8,128)S(1)}, u32[]{:S(2)}, u32[]{:S(2)}) collective-permute-start(f32[328,128]{1,0:T(8,128)} %get-tuple-element.140), channel_id=1, source_target_pairs={{0,20},{1,21},{2,22},{3,23},{4,16},{5,17},{6,18},{7,19},{8,28},{9,... | collective-permute-start | bytes 503816 | tf_op jit(solution)/shard_map/cond/branch_1_fun/ppermute | solution.py:397
  85.7 40.3 %collective-permute-start.73 = (f32[328,128]{1,0:T(8,128)}, f32[328,128]{1,0:T(8,128)S(1)}, u32[]{:S(2)}, u32[]{:S(2)}) collective-permute-start(f32[328,128]{1,0:T(8,128)} %get-tuple-element.141), channel_id=1, source_target_pairs={{0,21},{1,20},{2,23},{3,22},{4,17},{5,16},{6,19},{7,18},{8,29},{9,... | collective-permute-start | bytes 503816 | tf_op jit(solution)/shard_map/cond/branch_1_fun/ppermute | solution.py:397
  96.3 38.1 %collective-permute-start.74 = (f32[328,128]{1,0:T(8,128)}, f32[328,128]{1,0:T(8,128)S(1)}, u32[]{:S(2)}, u32[]{:S(2)}) collective-permute-start(f32[328,128]{1,0:T(8,128)} %get-tuple-element.142), channel_id=1, source_target_pairs={{0,22},{1,23},{2,20},{3,21},{4,18},{5,19},{6,16},{7,17},{8,30},{9,... | collective-permute-start | bytes 503816 | tf_op jit(solution)/shard_map/cond/branch_1_fun/ppermute | solution.py:397
  98.3 36.7 %collective-permute-start.75 = (f32[328,128]{1,0:T(8,128)}, f32[328,128]{1,0:T(8,128)S(1)}, u32[]{:S(2)}, u32[]{:S(2)}) collective-permute-start(f32[328,128]{1,0:T(8,128)} %get-tuple-element.143), channel_id=1, source_target_pairs={{0,23},{1,22},{2,21},{3,20},{4,19},{5,18},{6,17},{7,16},{8,31},{9,... | collective-permute-start | bytes 503816 | tf_op jit(solution)/shard_map/cond/branch_1_fun/ppermute | solution.py:397
  101.3 52.6 %collective-permute-start.76 = (f32[328,128]{1,0:T(8,128)}, f32[328,128]{1,0:T(8,128)S(1)}, u32[]{:S(2)}, u32[]{:S(2)}) collective-permute-start(f32[328,128]{1,0:T(8,128)} %get-tuple-element.144), channel_id=1, source_target_pairs={{0,28},{1,29},{2,30},{3,31},{4,24},{5,25},{6,26},{7,27},{8,20},{9,... | collective-permute-start | bytes 503816 | tf_op jit(solution)/shard_map/cond/branch_1_fun/ppermute | solution.py:397
  114.3 44.1 %collective-permute-start.77 = (f32[328,128]{1,0:T(8,128)}, f32[328,128]{1,0:T(8,128)S(1)}, u32[]{:S(2)}, u32[]{:S(2)}) collective-permute-start(f32[328,128]{1,0:T(8,128)} %get-tuple-element.145), channel_id=1, source_target_pairs={{0,29},{1,28},{2,31},{3,30},{4,25},{5,24},{6,27},{7,26},{8,21},{9,... | collective-permute-start | bytes 503816 | tf_op jit(solution)/shard_map/cond/branch_1_fun/ppermute | solution.py:397
  126.7 32.4 %collective-permute-start.78 = (f32[328,128]{1,0:T(8,128)}, f32[328,128]{1,0:T(8,128)S(1)}, u32[]{:S(2)}, u32[]{:S(2)}) collective-permute-start(f32[328,128]{1,0:T(8,128)} %get-tuple-element.146), channel_id=1, source_target_pairs={{0,30},{1,31},{2,28},{3,29},{4,26},{5,27},{6,24},{7,25},{8,22},{9,... | collective-permute-start | bytes 503816 | tf_op jit(solution)/shard_map/cond/branch_1_fun/ppermute | solution.py:397
  135.0 53.4 %collective-permute-start.80 = (f32[656,128]{1,0:T(8,128)}, f32[656,128]{1,0:T(8,128)S(1)}, u32[]{:S(2)}, u32[]{:S(2)}) collective-permute-start(f32[656,128]{1,0:T(8,128)} %get-tuple-element.148), channel_id=1, source_target_pairs={{0,4},{1,5},{2,6},{3,7},{4,0},{5,1},{6,2},{7,3},{8,12},{9,13},{10,... | collective-permute-start | bytes 1007624 | tf_op jit(solution)/shard_map/cond/branch_1_fun/ppermute | solution.py:403
  135.7 77.6 %collective-permute-start.81 = (f32[656,128]{1,0:T(8,128)}, f32[656,128]{1,0:T(8,128)S(1)}, u32[]{:S(2)}, u32[]{:S(2)}) collective-permute-start(f32[656,128]{1,0:T(8,128)} %get-tuple-element.149), channel_id=1, source_target_pairs={{0,4},{1,5},{2,6},{3,7},{4,0},{5,1},{6,2},{7,3},{8,12},{9,13},{10,... | collective-permute-start | bytes 1007624 | tf_op jit(solution)/shard_map/cond/branch_1_fun/ppermute | solution.py:403
  154.5 59.7 %collective-permute-start.82 = (f32[656,128]{1,0:T(8,128)}, f32[656,128]{1,0:T(8,128)S(1)}, u32[]{:S(2)}, u32[]{:S(2)}) collective-permute-start(f32[656,128]{1,0:T(8,128)} %get-tuple-element.150), channel_id=1, source_target_pairs={{0,4},{1,5},{2,6},{3,7},{4,0},{5,1},{6,2},{7,3},{8,12},{9,13},{10,... | collective-permute-start | bytes 1007624 | tf_op jit(solution)/shard_map/cond/branch_1_fun/ppermute | solution.py:403
  159.0 55.5 %collective-permute-start.83 = (f32[656,128]{1,0:T(8,128)}, f32[656,128]{1,0:T(8,128)S(1)}, u32[]{:S(2)}, u32[]{:S(2)}) collective-permute-start(f32[656,128]{1,0:T(8,128)} %get-tuple-element.151), channel_id=1, source_target_pairs={{0,4},{1,5},{2,6},{3,7},{4,0},{5,1},{6,2},{7,3},{8,12},{9,13},{10,... | collective-permute-start | bytes 1007624 | tf_op jit(solution)/shard_map/cond/branch_1_fun/ppermute | solution.py:403
  159.1 29.3 %collective-permute-start.79 = (f32[328,128]{1,0:T(8,128)S(1)}, f32[328,128]{1,0:T(8,128)S(1)}, u32[]{:S(2)}, u32[]{:S(2)}) collective-permute-start(f32[328,128]{1,0:T(8,128)S(1)} %copy-done.113), channel_id=1, source_target_pairs={{0,31},{1,30},{2,29},{3,28},{4,27},{5,26},{6,25},{7,24},{8,23},{9,... | collective-permute-start | bytes 503816 | tf_op jit(solution)/shard_map/cond/branch_1_fun/ppermute | solution.py:397
  188.4 32.2 %collective-permute-start.53 = (f32[656,128]{1,0:T(8,128)S(1)}, f32[656,128]{1,0:T(8,128)S(1)}, u32[]{:S(2)}, u32[]{:S(2)}) collective-permute-start(f32[656,128]{1,0:T(8,128)S(1)} %copy-done.110), channel_id=1, source_target_pairs={{0,9},{1,8},{2,11},{3,10},{4,13},{5,12},{6,15},{7,14},{8,1},{9,0},... | collective-permute-start | bytes 1007624 | tf_op jit(solution)/shard_map/cond/branch_1_fun/ppermute | solution.py:397
  188.5 34.7 %collective-permute-start.54 = (f32[656,128]{1,0:T(8,128)}, f32[656,128]{1,0:T(8,128)S(1)}, u32[]{:S(2)}, u32[]{:S(2)}) collective-permute-start(f32[656,128]{1,0:T(8,128)} %get-tuple-element.122), channel_id=1, source_target_pairs={{0,10},{1,11},{2,8},{3,9},{4,14},{5,15},{6,12},{7,13},{8,2},{9,3},... | collective-permute-start | bytes 1007624 | tf_op jit(solution)/shard_map/cond/branch_1_fun/ppermute | solution.py:397
  233.2 28.6 %collective-permute-start.50 = (f32[656,128]{1,0:T(8,128)}, f32[656,128]{1,0:T(8,128)}, u32[]{:S(2)}, u32[]{:S(2)}) collective-permute-start(f32[656,128]{1,0:T(8,128)} %get-tuple-element.118), channel_id=1, source_target_pairs={{0,2},{1,3},{2,0},{3,1},{4,6},{5,7},{6,4},{7,5},{8,10},{9,11},{10,... | collective-permute-start | bytes 1007624 | tf_op jit(solution)/shard_map/cond/branch_1_fun/ppermute | solution.py:397
  242.0 28.2 %collective-permute-start.51 = (f32[656,128]{1,0:T(8,128)}, f32[656,128]{1,0:T(8,128)}, u32[]{:S(2)}, u32[]{:S(2)}) collective-permute-start(f32[656,128]{1,0:T(8,128)} %get-tuple-element.119), channel_id=1, source_target_pairs={{0,3},{1,2},{2,1},{3,0},{4,7},{5,6},{6,5},{7,4},{8,11},{9,10},{10,... | collective-permute-start | bytes 1007624 | tf_op jit(solution)/shard_map/cond/branch_1_fun/ppermute | solution.py:397
  (64 other events, 2440.8 us)

commit v4 on v3

--- a/solution.py
+++ b/solution.py
@@ -80,16 +80,20 @@
     rows = states_ref.shape[0]
     full = rows // sublanes * sublanes
 
+    lanes = 4 * width if states_ref.shape[1] % (4 * width) == 0 else width
+
     def one(i, carry):
-        cols = pl.ds(pl.multiple_of(i * width, width), width)
-        tail = states_ref[full:rows, cols] if rows > full else None
-        done = advanced(params_ref, states_ref[0:full, cols], tail)
-        out_ref[0:full, cols] = done[0]
-        if rows > full:
-            out_ref[full:rows, cols] = done[1]
+        for j in range(lanes // width):
+            at = pl.multiple_of(i * lanes + j * width, width)
+            cols = pl.ds(at, width)
+            tail = states_ref[full:rows, cols] if rows > full else None
+            done = advanced(params_ref, states_ref[0:full, cols], tail)
+            out_ref[0:full, cols] = done[0]
+            if rows > full:
+                out_ref[full:rows, cols] = done[1]
         return carry
 
-    lax.fori_loop(0, states_ref.shape[1] // width, one, 0)
+    lax.fori_loop(0, states_ref.shape[1] // lanes, one, 0)
 
 
 def gate_params(half_volt, steepness, gate_rate, conductance, reversal, width):
@@ -385,7 +389,7 @@
 
 
 def early_inner(mates):
-    return [d for d in mixed(mates) if d][: mates // 2 - 1]
+    return [d for d in mixed(mates) if d][: mates // 4]
 
 
 def exchange(plan, chunks, table, states, params, places, tile_perm):

time: 344 us -> 343 us (level)
  waiting for transfers between devices: 112 us -> 139 us
  starting transfers between devices: 165 us -> 141 us
    ppermute x46, waiting for transfers between devices: 112 us -> 139 us  [send(): return lax.ppermute(piece, both, pairs)]
    ppermute x46, starting transfers between devices: 157 us -> 133 us  [send(): return lax.ppermute(piece, both, pairs)]
    pallas_call x1, Pallas kernels: 13 us -> 9.55 us  [advance(): pl.pallas_call(functools.partial(advance_kernel, width=width), grid=(node...]
  transfers between devices with their start and end apart: 51 -> 51, of which waited for: 19 -> 22; matrix products, arithmetic and copies ran while one was open for 1% -> 1% of each run, Pallas kernels for 4% -> 4%
where the time goes in v4:
time: 343 us; the launch traced here: 339 us
  starting transfers between devices  141 us (41%)
  waiting for transfers between devices  139 us (41%)
  Pallas kernels  44.4 us (13%)
  other arithmetic  5.73 us (2%)
  local copies, waits for them, and re-layouts  5.56 us (2%)
    ppermute x46, waiting for transfers between devices, send(): return lax.ppermute(piece, both, pairs)  139 us
    ppermute x46, starting transfers between devices, send(): return lax.ppermute(piece, both, pairs)  133 us
    pallas_call x1, Pallas kernels, unpack(): pl.pallas_call(functools.partial(unpack_kernel, plan=plan, sizes=sizes),...  13.1 us
    pallas_call x2, Pallas kernels, pack_pieces(): pl.pallas_call(functools.partial(pieces_kernel, plan=plan, inner=inner, c...  11.3 us
    pallas_call x1, Pallas kernels, advance(): pl.pallas_call(functools.partial(advance_kernel, width=width), grid=(node...  9.55 us
  transfers between devices with their start and end apart: 51, of which 22 were waited for; matrix products, arithmetic and copies ran while one was open for 1% of the time, Pallas kernels for 4%

profile of v4, /device:TPU:25, one launch (start us, length us, event | category | flops | bytes accessed | tf_op | source)
XLA Modules:
  0.0 338.5 jit_solution(7911007643295590164)
XLA Ops:
  1.4 6.2 %all-to-all-start = ((s32[32,1,32]{2,1,0:T(1,128)}), s32[32,1,32]{2,1,0:T(1,128)S(1)}, u32[]{:S(2)}, u32[]{:S(2)}) async-start(s32[32,1,32]{2,1,0:T(1,128)} %broadcast_in_dim.10), calls=%async_computation | async-start | bytes 32768 | tf_op jit(solution)/shard_map/all_to_all | solution.py:437
  13.5 324.9 %conditional.1 = (f32[41,32768]{1,0:T(8,128)}) conditional(s32[]{:T(128)} %clamp.3, (f32[5,40]{1,0:T(8,128)S(1)}, f32[41,32768]{1,0:T(8,128)}, s32[32,1,32]{2,1,0:T(1,128)S(1)}, pred[256]{0:T(512)(128)(4,1)S(1)}, s32[256]{0:T(256)S(1)}, /*index=5*/pred[256]{0:T(512)(128)(4,1)S(1)}, s32[256,128]{1,0:T(8,128)}, ...), branch_computations={%region_4.5_spmd, %region_5.6_spmd, %region_6.7_spmd} | conditional | flops 53743104 | bytes 98723984 | solution.py:448
  14.5 9.5 %advance.4.adv_ref = f32[41,32768]{1,0:T(8,128)} custom-call(f32[5,41,128]{2,1,0:T(8,128)} %broadcast_in_dim.15.params_ref, f32[41,32768]{1,0:T(8,128)} %get-tuple-element.260.states_ref), custom_call_target="tpu_custom_call" | custom-call | flops 53739520 | bytes 10747904 | tf_op jit(solution)/shard_map/cond/branch_1_fun/advance/pallas_call | solution.py:109
  24.0 6.9 %branch_1_fun.2 = (f32[656,128]{1,0:T(8,128)}, f32[656,128]{1,0:T(8,128)}, f32[656,128]{1,0:T(8,128)}, f32[656,128]{1,0:T(8,128)}, f32[656,128]{1,0:T(8,128)}, /...) custom-call(s32[32,1,32]{2,1,0:T(1,128)S(1)} %get-tuple-element.113., ...), custom_call_target="tpu_custom_call" | custom-call | tf_op jit(solution)/shard_map/cond/branch_1_fun/pallas_call | solution.py:228
  39.4 16.0 %collective-permute-done.64.refs_16_ = f32[328,128]{1,0:T(8,128)S(1)} collective-permute-done((f32[328,128]{1,0:T(8,128)}, f32[328,128]{1,0:T(8,128)S(1)}, u32[]{:S(2)}, u32[]{:S(2)}) %collective-permute-start.64) | collective-permute-done | bytes 167968 | tf_op jit(solution)/shard_map/cond/branch_1_fun/ppermute | solution.py:401
  60.8 6.2 %collective-permute-start.70 = (f32[328,128]{1,0:T(8,128)}, f32[328,128]{1,0:T(8,128)S(1)}, u32[]{:S(2)}, u32[]{:S(2)}) collective-permute-start(f32[328,128]{1,0:T(8,128)} %get-tuple-element.138), channel_id=1, source_target_pairs={{0,14},{1,15},{2,12},{3,13},{4,10},{5,11},{6,8},{7,9},{8,6},{9,7},... | collective-permute-start | bytes 503816 | tf_op jit(solution)/shard_map/cond/branch_1_fun/ppermute | solution.py:401
  67.9 12.1 %collective-permute-start.72 = (f32[328,128]{1,0:T(8,128)}, f32[328,128]{1,0:T(8,128)S(1)}, u32[]{:S(2)}, u32[]{:S(2)}) collective-permute-start(f32[328,128]{1,0:T(8,128)} %get-tuple-element.140), channel_id=1, source_target_pairs={{0,20},{1,21},{2,22},{3,23},{4,16},{5,17},{6,18},{7,19},{8,28},{9,... | collective-permute-start | bytes 503816 | tf_op jit(solution)/shard_map/cond/branch_1_fun/ppermute | solution.py:401
  84.4 8.8 %collective-permute-done.69.refs_21_ = f32[328,128]{1,0:T(8,128)S(1)} collective-permute-done((f32[328,128]{1,0:T(8,128)}, f32[328,128]{1,0:T(8,128)S(1)}, u32[]{:S(2)}, u32[]{:S(2)}) %collective-permute-start.69) | collective-permute-done | bytes 167968 | tf_op jit(solution)/shard_map/cond/branch_1_fun/ppermute | solution.py:401
  98.2 10.8 %collective-permute-start.76 = (f32[328,128]{1,0:T(8,128)}, f32[328,128]{1,0:T(8,128)S(1)}, u32[]{:S(2)}, u32[]{:S(2)}) collective-permute-start(f32[328,128]{1,0:T(8,128)} %get-tuple-element.144), channel_id=1, source_target_pairs={{0,28},{1,29},{2,30},{3,31},{4,24},{5,25},{6,26},{7,27},{8,20},{9,... | collective-permute-start | bytes 503816 | tf_op jit(solution)/shard_map/cond/branch_1_fun/ppermute | solution.py:401
  115.5 7.4 %collective-permute-done.73.refs_25_ = f32[328,128]{1,0:T(8,128)S(1)} collective-permute-done((f32[328,128]{1,0:T(8,128)}, f32[328,128]{1,0:T(8,128)S(1)}, u32[]{:S(2)}, u32[]{:S(2)}) %collective-permute-start.73) | collective-permute-done | bytes 167968 | tf_op jit(solution)/shard_map/cond/branch_1_fun/ppermute | solution.py:401
  126.1 5.1 %pack_dense.4 = (f32[656,128]{1,0:T(8,128)}, f32[656,128]{1,0:T(8,128)}, f32[656,128]{1,0:T(8,128)}, f32[656,128]{1,0:T(8,128)}) custom-call(s32[32,1,32]{2,1,0:T(1,128)S(1)} %get-tuple-element.113.table_ref, f32[41,32768]{1,0:T(8,128)} %get-tuple-element.260.states_ref), custom_call_target="tpu_custom_call" | custom-call | tf_op jit(solution)/shard_map/cond/branch_1_fun/pack_dense/pallas_call | solution.py:187
  135.0 15.8 %collective-permute-done.76.refs_28_ = f32[328,128]{1,0:T(8,128)S(1)} collective-permute-done((f32[328,128]{1,0:T(8,128)}, f32[328,128]{1,0:T(8,128)S(1)}, u32[]{:S(2)}, u32[]{:S(2)}) %collective-permute-start.76) | collective-permute-done | bytes 167968 | tf_op jit(solution)/shard_map/cond/branch_1_fun/ppermute | solution.py:401
  156.0 17.6 %collective-permute-start.79 = (f32[328,128]{1,0:T(8,128)S(1)}, f32[328,128]{1,0:T(8,128)S(1)}, u32[]{:S(2)}, u32[]{:S(2)}) collective-permute-start(f32[328,128]{1,0:T(8,128)S(1)} %copy-done.114), channel_id=1, source_target_pairs={{0,31},{1,30},{2,29},{3,28},{4,27},{5,26},{6,25},{7,24},{8,23},{9,... | collective-permute-start | bytes 503816 | tf_op jit(solution)/shard_map/cond/branch_1_fun/ppermute | solution.py:401
  173.6 11.7 %collective-permute-done.79.refs_31_ = f32[328,128]{1,0:T(8,128)S(1)} collective-permute-done((f32[328,128]{1,0:T(8,128)S(1)}, f32[328,128]{1,0:T(8,128)S(1)}, u32[]{:S(2)}, u32[]{:S(2)}) %collective-permute-start.79) | collective-permute-done | bytes 167968 | tf_op jit(solution)/shard_map/cond/branch_1_fun/ppermute | solution.py:401
  185.3 24.3 %collective-permute-start.51 = (f32[656,128]{1,0:T(8,128)S(1)}, f32[656,128]{1,0:T(8,128)S(1)}, u32[]{:S(2)}, u32[]{:S(2)}) collective-permute-start(f32[656,128]{1,0:T(8,128)S(1)} %copy-done.110), channel_id=1, source_target_pairs={{0,3},{1,2},{2,1},{3,0},{4,7},{5,6},{6,5},{7,4},{8,11},{9,10},{10,... | collective-permute-start | bytes 1007624 | tf_op jit(solution)/shard_map/cond/branch_1_fun/ppermute | solution.py:401
  213.2 4.3 %collective-permute-done.51.refs_3_ = f32[656,128]{1,0:T(8,128)S(1)} collective-permute-done((f32[656,128]{1,0:T(8,128)S(1)}, f32[656,128]{1,0:T(8,128)S(1)}, u32[]{:S(2)}, u32[]{:S(2)}) %collective-permute-start.51) | collective-permute-done | bytes 335904 | tf_op jit(solution)/shard_map/cond/branch_1_fun/ppermute | solution.py:401
  219.9 6.1 %collective-permute-done.53.refs_5_ = f32[656,128]{1,0:T(8,128)S(1)} collective-permute-done((f32[656,128]{1,0:T(8,128)}, f32[656,128]{1,0:T(8,128)S(1)}, u32[]{:S(2)}, u32[]{:S(2)}) %collective-permute-start.53) | collective-permute-done | bytes 335904 | tf_op jit(solution)/shard_map/cond/branch_1_fun/ppermute | solution.py:401
  233.2 4.4 %branch_1_fun.3 = (f32[656,128]{1,0:T(8,128)}, f32[656,128]{1,0:T(8,128)}, f32[656,128]{1,0:T(8,128)}, f32[656,128]{1,0:T(8,128)}) custom-call(s32[32,1,32]{2,1,0:T(1,128)S(1)} %get-tuple-element.113.table_ref, f32[41,32768]{1,0:T(8,128)} %advance.4.adv_ref), custom_call_target="tpu_custom_call" | custom-call | tf_op jit(solution)/shard_map/cond/branch_1_fun/pallas_call | solution.py:228
  241.7 19.2 %collective-permute-done.57.refs_9_ = f32[656,128]{1,0:T(8,128)} collective-permute-done((f32[656,128]{1,0:T(8,128)}, f32[656,128]{1,0:T(8,128)}, u32[]{:S(2)}, u32[]{:S(2)}) %collective-permute-start.57) | collective-permute-done | bytes 335904 | tf_op jit(solution)/shard_map/cond/branch_1_fun/ppermute | solution.py:401
  270.5 5.3 %relay.4 = (f32[328,128]{1,0:T(8,128)}, f32[328,128]{1,0:T(8,128)}, f32[328,128]{1,0:T(8,128)}, f32[328,128]{1,0:T(8,128)}, f32[328,128]{1,0:T(8,128)}, /*index=...) custom-call(s32[32,1,32]{2,1,0:T(1,128)S(1)} %get-tuple-element.113., ...), custom_call_target="tpu_custom_call" | custom-call | tf_op jit(solution)/shard_map/cond/branch_1_fun/relay/pallas_call | solution.py:289
  278.5 6.4 %collective-permute-done.61.refs_13_ = f32[656,128]{1,0:T(8,128)} collective-permute-done((f32[656,128]{1,0:T(8,128)}, f32[656,128]{1,0:T(8,128)}, u32[]{:S(2)}, u32[]{:S(2)}) %collective-permute-start.61) | collective-permute-done | bytes 335904 | tf_op jit(solution)/shard_map/cond/branch_1_fun/ppermute | solution.py:401
  302.5 7.6 %collective-permute-done.92.refs_41_ = f32[328,128]{1,0:T(8,128)} collective-permute-done((f32[328,128]{1,0:T(8,128)}, f32[328,128]{1,0:T(8,128)}, u32[]{:S(2)}, u32[]{:S(2)}) %collective-permute-start.92) | collective-permute-done | bytes 167968 | tf_op jit(solution)/shard_map/cond/branch_1_fun/ppermute | solution.py:401
  313.6 11.0 %collective-permute-done.95.refs_44_ = f32[328,128]{1,0:T(8,128)} collective-permute-done((f32[328,128]{1,0:T(8,128)}, f32[328,128]{1,0:T(8,128)}, u32[]{:S(2)}, u32[]{:S(2)}) %collective-permute-start.95) | collective-permute-done | bytes 167968 | tf_op jit(solution)/shard_map/cond/branch_1_fun/ppermute | solution.py:401
  324.7 13.1 %unpack.4 = f32[41,32768]{1,0:T(8,128)} custom-call(s32[256]{0:T(256)} %multiply_add_fusion.3.base_ref, s32[256]{0:T(256)} %get-tuple-element.371.tail_ref, s32[256]{0:T(256)} %get-tuple-element.372.step_ref, s32[256,128]{1,0:T(8,128)S(1)} %copy-done.1, f32[656,128]{1,0:T(8,128)} %get-tuple-element.116.refs_0_, f32[656,128]{1,0:T(8,128)} %collective-permute-done.49.refs_1_, ...), custom_call_target="tpu_custom_call" | custom-call | tf_op jit(solution)/shard_map/cond/branch_1_fun/unpack/pallas_call | solution.py:344
  (174 shorter events, 100.0 us)
Async XLA Ops:
  34.3 32.7 %collective-permute-start.66 = (f32[328,128]{1,0:T(8,128)}, f32[328,128]{1,0:T(8,128)S(1)}, u32[]{:S(2)}, u32[]{:S(2)}) collective-permute-start(f32[328,128]{1,0:T(8,128)} %get-tuple-element.134), channel_id=1, source_target_pairs={{0,6},{1,7},{2,4},{3,5},{4,2},{5,3},{6,0},{7,1},{8,14},{9,15},{10,... | collective-permute-start | bytes 503816 | tf_op jit(solution)/shard_map/cond/branch_1_fun/ppermute | solution.py:401
  36.3 31.5 %collective-permute-start.67 = (f32[328,128]{1,0:T(8,128)}, f32[328,128]{1,0:T(8,128)S(1)}, u32[]{:S(2)}, u32[]{:S(2)}) collective-permute-start(f32[328,128]{1,0:T(8,128)} %get-tuple-element.135), channel_id=1, source_target_pairs={{0,7},{1,6},{2,5},{3,4},{4,3},{5,2},{6,1},{7,0},{8,15},{9,14},{10,... | collective-permute-start | bytes 503816 | tf_op jit(solution)/shard_map/cond/branch_1_fun/ppermute | solution.py:401
  37.6 45.1 %collective-permute-start.68 = (f32[328,128]{1,0:T(8,128)}, f32[328,128]{1,0:T(8,128)S(1)}, u32[]{:S(2)}, u32[]{:S(2)}) collective-permute-start(f32[328,128]{1,0:T(8,128)} %get-tuple-element.136), channel_id=1, source_target_pairs={{0,12},{1,13},{2,14},{3,15},{4,8},{5,9},{6,10},{7,11},{8,4},{9,5},... | collective-permute-start | bytes 503816 | tf_op jit(solution)/shard_map/cond/branch_1_fun/ppermute | solution.py:401
  55.4 37.7 %collective-permute-start.69 = (f32[328,128]{1,0:T(8,128)}, f32[328,128]{1,0:T(8,128)S(1)}, u32[]{:S(2)}, u32[]{:S(2)}) collective-permute-start(f32[328,128]{1,0:T(8,128)} %get-tuple-element.137), channel_id=1, source_target_pairs={{0,13},{1,12},{2,15},{3,14},{4,9},{5,8},{6,11},{7,10},{8,5},{9,4},... | collective-permute-start | bytes 503816 | tf_op jit(solution)/shard_map/cond/branch_1_fun/ppermute | solution.py:401
  60.8 34.5 %collective-permute-start.70 = (f32[328,128]{1,0:T(8,128)}, f32[328,128]{1,0:T(8,128)S(1)}, u32[]{:S(2)}, u32[]{:S(2)}) collective-permute-start(f32[328,128]{1,0:T(8,128)} %get-tuple-element.138), channel_id=1, source_target_pairs={{0,14},{1,15},{2,12},{3,13},{4,10},{5,11},{6,8},{7,9},{8,6},{9,7},... | collective-permute-start | bytes 503816 | tf_op jit(solution)/shard_map/cond/branch_1_fun/ppermute | solution.py:401
  67.0 31.2 %collective-permute-start.71 = (f32[328,128]{1,0:T(8,128)}, f32[328,128]{1,0:T(8,128)S(1)}, u32[]{:S(2)}, u32[]{:S(2)}) collective-permute-start(f32[328,128]{1,0:T(8,128)} %get-tuple-element.139), channel_id=1, source_target_pairs={{0,15},{1,14},{2,13},{3,12},{4,11},{5,10},{6,9},{7,8},{8,7},{9,6},... | collective-permute-start | bytes 503816 | tf_op jit(solution)/shard_map/cond/branch_1_fun/ppermute | solution.py:401
  67.9 43.3 %collective-permute-start.72 = (f32[328,128]{1,0:T(8,128)}, f32[328,128]{1,0:T(8,128)S(1)}, u32[]{:S(2)}, u32[]{:S(2)}) collective-permute-start(f32[328,128]{1,0:T(8,128)} %get-tuple-element.140), channel_id=1, source_target_pairs={{0,20},{1,21},{2,22},{3,23},{4,16},{5,17},{6,18},{7,19},{8,28},{9,... | collective-permute-start | bytes 503816 | tf_op jit(solution)/shard_map/cond/branch_1_fun/ppermute | solution.py:401
  82.6 40.3 %collective-permute-start.73 = (f32[328,128]{1,0:T(8,128)}, f32[328,128]{1,0:T(8,128)S(1)}, u32[]{:S(2)}, u32[]{:S(2)}) collective-permute-start(f32[328,128]{1,0:T(8,128)} %get-tuple-element.141), channel_id=1, source_target_pairs={{0,21},{1,20},{2,23},{3,22},{4,17},{5,16},{6,19},{7,18},{8,29},{9,... | collective-permute-start | bytes 503816 | tf_op jit(solution)/shard_map/cond/branch_1_fun/ppermute | solution.py:401
  93.2 38.1 %collective-permute-start.74 = (f32[328,128]{1,0:T(8,128)}, f32[328,128]{1,0:T(8,128)S(1)}, u32[]{:S(2)}, u32[]{:S(2)}) collective-permute-start(f32[328,128]{1,0:T(8,128)} %get-tuple-element.142), channel_id=1, source_target_pairs={{0,22},{1,23},{2,20},{3,21},{4,18},{5,19},{6,16},{7,17},{8,30},{9,... | collective-permute-start | bytes 503816 | tf_op jit(solution)/shard_map/cond/branch_1_fun/ppermute | solution.py:401
  95.3 36.7 %collective-permute-start.75 = (f32[328,128]{1,0:T(8,128)}, f32[328,128]{1,0:T(8,128)S(1)}, u32[]{:S(2)}, u32[]{:S(2)}) collective-permute-start(f32[328,128]{1,0:T(8,128)} %get-tuple-element.143), channel_id=1, source_target_pairs={{0,23},{1,22},{2,21},{3,20},{4,19},{5,18},{6,17},{7,16},{8,31},{9,... | collective-permute-start | bytes 503816 | tf_op jit(solution)/shard_map/cond/branch_1_fun/ppermute | solution.py:401
  98.2 52.6 %collective-permute-start.76 = (f32[328,128]{1,0:T(8,128)}, f32[328,128]{1,0:T(8,128)S(1)}, u32[]{:S(2)}, u32[]{:S(2)}) collective-permute-start(f32[328,128]{1,0:T(8,128)} %get-tuple-element.144), channel_id=1, source_target_pairs={{0,28},{1,29},{2,30},{3,31},{4,24},{5,25},{6,26},{7,27},{8,20},{9,... | collective-permute-start | bytes 503816 | tf_op jit(solution)/shard_map/cond/branch_1_fun/ppermute | solution.py:401
  111.2 44.1 %collective-permute-start.77 = (f32[328,128]{1,0:T(8,128)}, f32[328,128]{1,0:T(8,128)S(1)}, u32[]{:S(2)}, u32[]{:S(2)}) collective-permute-start(f32[328,128]{1,0:T(8,128)} %get-tuple-element.145), channel_id=1, source_target_pairs={{0,29},{1,28},{2,31},{3,30},{4,25},{5,24},{6,27},{7,26},{8,21},{9,... | collective-permute-start | bytes 503816 | tf_op jit(solution)/shard_map/cond/branch_1_fun/ppermute | solution.py:401
  123.6 32.4 %collective-permute-start.78 = (f32[328,128]{1,0:T(8,128)}, f32[328,128]{1,0:T(8,128)S(1)}, u32[]{:S(2)}, u32[]{:S(2)}) collective-permute-start(f32[328,128]{1,0:T(8,128)} %get-tuple-element.146), channel_id=1, source_target_pairs={{0,30},{1,31},{2,28},{3,29},{4,26},{5,27},{6,24},{7,25},{8,22},{9,... | collective-permute-start | bytes 503816 | tf_op jit(solution)/shard_map/cond/branch_1_fun/ppermute | solution.py:401
  131.9 77.7 %collective-permute-start.80 = (f32[656,128]{1,0:T(8,128)}, f32[656,128]{1,0:T(8,128)S(1)}, u32[]{:S(2)}, u32[]{:S(2)}) collective-permute-start(f32[656,128]{1,0:T(8,128)} %get-tuple-element.148), channel_id=1, source_target_pairs={{0,4},{1,5},{2,6},{3,7},{4,0},{5,1},{6,2},{7,3},{8,12},{9,13},{10,... | collective-permute-start | bytes 1007624 | tf_op jit(solution)/shard_map/cond/branch_1_fun/ppermute | solution.py:407
  132.6 77.7 %collective-permute-start.81 = (f32[656,128]{1,0:T(8,128)}, f32[656,128]{1,0:T(8,128)S(1)}, u32[]{:S(2)}, u32[]{:S(2)}) collective-permute-start(f32[656,128]{1,0:T(8,128)} %get-tuple-element.149), channel_id=1, source_target_pairs={{0,4},{1,5},{2,6},{3,7},{4,0},{5,1},{6,2},{7,3},{8,12},{9,13},{10,... | collective-permute-start | bytes 1007624 | tf_op jit(solution)/shard_map/cond/branch_1_fun/ppermute | solution.py:407
  151.5 60.0 %collective-permute-start.82 = (f32[656,128]{1,0:T(8,128)}, f32[656,128]{1,0:T(8,128)S(1)}, u32[]{:S(2)}, u32[]{:S(2)}) collective-permute-start(f32[656,128]{1,0:T(8,128)} %get-tuple-element.150), channel_id=1, source_target_pairs={{0,4},{1,5},{2,6},{3,7},{4,0},{5,1},{6,2},{7,3},{8,12},{9,13},{10,... | collective-permute-start | bytes 1007624 | tf_op jit(solution)/shard_map/cond/branch_1_fun/ppermute | solution.py:407
  156.0 55.5 %collective-permute-start.83 = (f32[656,128]{1,0:T(8,128)}, f32[656,128]{1,0:T(8,128)S(1)}, u32[]{:S(2)}, u32[]{:S(2)}) collective-permute-start(f32[656,128]{1,0:T(8,128)} %get-tuple-element.151), channel_id=1, source_target_pairs={{0,4},{1,5},{2,6},{3,7},{4,0},{5,1},{6,2},{7,3},{8,12},{9,13},{10,... | collective-permute-start | bytes 1007624 | tf_op jit(solution)/shard_map/cond/branch_1_fun/ppermute | solution.py:407
  156.0 29.3 %collective-permute-start.79 = (f32[328,128]{1,0:T(8,128)S(1)}, f32[328,128]{1,0:T(8,128)S(1)}, u32[]{:S(2)}, u32[]{:S(2)}) collective-permute-start(f32[328,128]{1,0:T(8,128)S(1)} %copy-done.114), channel_id=1, source_target_pairs={{0,31},{1,30},{2,29},{3,28},{4,27},{5,26},{6,25},{7,24},{8,23},{9,... | collective-permute-start | bytes 503816 | tf_op jit(solution)/shard_map/cond/branch_1_fun/ppermute | solution.py:401
  185.3 32.2 %collective-permute-start.51 = (f32[656,128]{1,0:T(8,128)S(1)}, f32[656,128]{1,0:T(8,128)S(1)}, u32[]{:S(2)}, u32[]{:S(2)}) collective-permute-start(f32[656,128]{1,0:T(8,128)S(1)} %copy-done.110), channel_id=1, source_target_pairs={{0,3},{1,2},{2,1},{3,0},{4,7},{5,6},{6,5},{7,4},{8,11},{9,10},{10,... | collective-permute-start | bytes 1007624 | tf_op jit(solution)/shard_map/cond/branch_1_fun/ppermute | solution.py:401
  218.0 42.9 %collective-permute-start.57 = (f32[656,128]{1,0:T(8,128)}, f32[656,128]{1,0:T(8,128)}, u32[]{:S(2)}, u32[]{:S(2)}) collective-permute-start(f32[656,128]{1,0:T(8,128)} %get-tuple-element.125), channel_id=1, source_target_pairs={{0,17},{1,16},{2,19},{3,18},{4,21},{5,20},{6,23},{7,22},{8,25},{9,... | collective-permute-start | bytes 1007624 | tf_op jit(solution)/shard_map/cond/branch_1_fun/ppermute | solution.py:401
  226.0 35.3 %collective-permute-start.58 = (f32[656,128]{1,0:T(8,128)}, f32[656,128]{1,0:T(8,128)}, u32[]{:S(2)}, u32[]{:S(2)}) collective-permute-start(f32[656,128]{1,0:T(8,128)} %get-tuple-element.126), channel_id=1, source_target_pairs={{0,18},{1,19},{2,16},{3,17},{4,22},{5,23},{6,20},{7,21},{8,26},{9,... | collective-permute-start | bytes 1007624 | tf_op jit(solution)/shard_map/cond/branch_1_fun/ppermute | solution.py:401
  228.6 33.6 %collective-permute-start.59 = (f32[656,128]{1,0:T(8,128)}, f32[656,128]{1,0:T(8,128)}, u32[]{:S(2)}, u32[]{:S(2)}) collective-permute-start(f32[656,128]{1,0:T(8,128)} %get-tuple-element.127), channel_id=1, source_target_pairs={{0,19},{1,18},{2,17},{3,16},{4,23},{5,22},{6,21},{7,20},{8,27},{9,... | collective-permute-start | bytes 1007624 | tf_op jit(solution)/shard_map/cond/branch_1_fun/ppermute | solution.py:401
  233.2 34.8 %collective-permute-start.60 = (f32[656,128]{1,0:T(8,128)}, f32[656,128]{1,0:T(8,128)}, u32[]{:S(2)}, u32[]{:S(2)}) collective-permute-start(f32[656,128]{1,0:T(8,128)} %get-tuple-element.128), channel_id=1, source_target_pairs={{0,24},{1,25},{2,26},{3,27},{4,28},{5,29},{6,30},{7,31},{8,16},{9,... | collective-permute-start | bytes 1007624 | tf_op jit(solution)/shard_map/cond/branch_1_fun/ppermute | solution.py:401
  237.7 38.1 %collective-permute-start.63 = (f32[656,128]{1,0:T(8,128)}, f32[656,128]{1,0:T(8,128)}, u32[]{:S(2)}, u32[]{:S(2)}) collective-permute-start(f32[656,128]{1,0:T(8,128)} %get-tuple-element.131), channel_id=1, source_target_pairs={{0,27},{1,26},{2,25},{3,24},{4,31},{5,30},{6,29},{7,28},{8,19},{9,... | collective-permute-start | bytes 1007624 | tf_op jit(solution)/shard_map/cond/branch_1_fun/ppermute | solution.py:401
  (64 other events, 2434.2 us)

commit v5 on v4

--- a/solution.py
+++ b/solution.py
@@ -35,10 +35,10 @@
         self.most = self.slots + self.over
         self.inner_rows = round_up(rows * self.most, sublanes)
         self.cross_rows = round_up(rows * self.slots, sublanes)
-        self.relay_rows = round_up(rows * self.over, sublanes)
-        self.chunk = 16
-        self.chunk_rows = round_up(rows * self.chunk, sublanes)
-        self.worst = self.mates * self.over
+        self.relay_rows = round_up(rows * 2 * self.over, sublanes)
+        self.side = self.peers // 4
+        self.flat = self.devices // 4
+        self.worst = self.flat * self.over
 
     def half(self, device):
         return (device % self.peers) // self.near
@@ -49,9 +49,17 @@
     def device(self, mate, half):
         return mate // self.near * self.peers + half * self.near + mate % self.near
 
-    def partner(self, device):
-        flip = 1 - 2 * self.half(device)
-        return device + flip * self.near
+    def plane(self, device):
+        return device % self.peers // self.side
+
+    def spot(self, device):
+        return device // self.peers * self.side + device % self.side
+
+    def at(self, spot, plane):
+        return spot // self.side * self.peers + plane * self.side + spot % self.side
+
+    def twin(self, device, flip):
+        return self.at(self.spot(device), self.plane(device) ^ flip)
 
     def me(self):
         return lax.axis_index("group") * self.peers + lax.axis_index("peer")
@@ -138,58 +146,54 @@
         put(tail(e), 1, adv_ref[plan.full + e : plan.full + e + 1, cols])
 
 
-def dense_kernel(table_ref, states_ref, *refs, plan):
-    outs, all_ref = refs[:-1], refs[-1]
-    room = len(outs) * plan.chunk
+far_planes = (2, 3)
+
+
+def dense_kernel(table_ref, states_ref, *outs, plan, room):
     me = plan.me()
-    mine = plan.half(me)
 
     def one(s, carry):
-        start, at = carry
+        start, *places = carry
         count = table_ref[s, 0, me]
-        far = (plan.half(s) != mine).astype(jnp.int32)
-        more = jnp.maximum(count - plan.slots, 0) * far
-
-        def spill(k, carry):
-            slot = jnp.minimum(at + k, room - 1)
-
-            def put(base, size, vals):
-                if size == plan.full:
-                    base = pl.multiple_of(base, sublanes)
-                all_ref[pl.ds(base, size), :] = vals
-
-            put_block(
-                plan,
-                states_ref,
-                start + plan.slots + k,
-                put,
-                slot * plan.full,
-                lambda e: room * plan.full + e * room + slot,
-            )
-            return carry
-
-        lax.fori_loop(0, more, spill, 0)
-        return start + count, at + more
-
-    lax.fori_loop(0, plan.devices, one, (0, 0))
-    for c, out_ref in enumerate(outs):
-        size = plan.chunk * plan.full
-        out_ref[0:size, :] = all_ref[c * size : (c + 1) * size, :]
-        for e in range(plan.extra):
-            row = room * plan.full + e * room + c * plan.chunk
-            to = size + e * plan.chunk
-            out_ref[to : to + plan.chunk, :] = all_ref[row : row + plan.chunk, :]
-
-
-def pack_dense(plan, table, states, chunks):
-    piece = jax.ShapeDtypeStruct((plan.chunk_rows, plan.width), states.dtype)
-    rows = round_up(chunks * plan.chunk * plan.rows, sublanes)
+        flip = plan.plane(s) ^ plan.plane(me)
+        spilled = jnp.maximum(count - plan.slots, 0)
+        nexts = []
+        for far, at, out_ref in zip(far_planes, places, outs):
+            more = spilled * (flip == far).astype(jnp.int32)
+
+            def spill(k, carry, at=at, out_ref=out_ref):
+                slot = jnp.minimum(at + k, room - 1)
+
+                def put(base, size, vals):
+                    if size == plan.full:
+                        base = pl.multiple_of(base, sublanes)
+                    out_ref[pl.ds(base, size), :] = vals
+
+                put_block(
+                    plan,
+                    states_ref,
+                    start + plan.slots + k,
+                    put,
+                    slot * plan.full,
+                    lambda e: room * plan.full + e * room + slot,
+                )
+                return carry
+
+            lax.fori_loop(0, more, spill, 0)
+            nexts.append(at + more)
+        return (start + count, *nexts)
+
+    lax.fori_loop(0, plan.devices, one, (0, 0, 0))
+
+
+def pack_dense(plan, table, states, room):
+    rows = round_up(room * plan.rows, sublanes)
+    piece = jax.ShapeDtypeStruct((rows, plan.width), states.dtype)
     return pl.pallas_call(
-        functools.partial(dense_kernel, plan=plan),
+        functools.partial(dense_kernel, plan=plan, room=room),
         in_specs=[smem_full, vmem_full],
-        out_specs=[vmem_full] * chunks,
-        out_shape=[piece] * chunks,
-        scratch_shapes=[pltpu.VMEM((rows, plan.width), states.dtype)],
+        out_specs=[vmem_full] * 2,
+        out_shape=[piece] * 2,
         name="pack_dense",
     )(table, states)
 
@@ -234,67 +238,62 @@
     )(table, adv)
 
 
-def relay_kernel(table_ref, params_ref, *refs, plan, chunks):
-    dense, outs = refs[:chunks], refs[chunks : chunks + plan.mates]
-    far_ref, done_ref = refs[chunks + plan.mates :]
-    room = chunks * plan.chunk
+def relay_kernel(table_ref, params_ref, *refs, plan, room):
+    dense, outs = refs[:2], refs[2 : 2 + plan.flat]
+    first_refs, done_refs = refs[2 + plan.flat : 4 + plan.flat], refs[4 + plan.flat :]
     me = plan.me()
-    mine = plan.half(me)
-    other = plan.partner(me)
-
-    def scan(s, at):
-        far_ref[s] = at
-        near = (plan.half(s) == mine).astype(jnp.int32)
-        return at + jnp.maximum(table_ref[s, 0, other] - plan.slots, 0) * near
-
-    total = lax.fori_loop(0, plan.devices, scan, 0)
-    for c, dense_ref in enumerate(dense):
+    plane = plan.plane(me)
+    here = plan.spot(me)
+    slots = 2 * plan.over
+    for j, far in enumerate(far_planes):
+        dense_ref, done_ref, first_ref = dense[j], done_refs[j], first_refs[j]
+        source = plan.twin(me, far)
+
+        def scan(t, at):
+            first_ref[t] = at
+            return at + jnp.maximum(table_ref[plan.at(t, plane), 0, source] - plan.slots, 0)
+
+        total = lax.fori_loop(0, plan.flat, scan, 0)
 
         def step(i, carry):
             rows = pl.ds(pl.multiple_of(i * plan.full, plan.full), plan.full)
+            lasts = [pl.ds(room * plan.full + e * room + i, 1) for e in range(plan.extra)]
             tail = None
             if plan.extra:
-                lasts = [plan.chunk * plan.full + e * plan.chunk + i for e in range(plan.extra)]
-                tail = [dense_ref[pl.ds(last, 1), :] for last in lasts]
+                tail = [dense_ref[last, :] for last in lasts]
                 tail = jnp.concatenate(tail, axis=0) if plan.extra > 1 else tail[0]
             done = advanced(params_ref, dense_ref[rows, :], tail)
-            slot = c * plan.chunk + i
-            to = pl.ds(pl.multiple_of(slot * plan.full, plan.full), plan.full)
-            done_ref[to, :] = done[0]
-            for e in range(plan.extra):
-                row = room * plan.full + e * room + slot
-                done_ref[pl.ds(row, 1), :] = done[1][e : e + 1]
+            done_ref[rows, :] = done[0]
+            for e, last in enumerate(lasts):
+                done_ref[last, :] = done[1][e : e + 1]
             return carry
 
-        lax.fori_loop(0, jnp.clip(total - c * plan.chunk, 0, plan.chunk), step, 0)
-    here = plan.mate(me)
-    slots = plan.over
-    for d, out_ref in enumerate(outs):
-        at = far_ref[plan.device(here ^ d, mine)]
-        for k in range(slots):
-            slot = jnp.minimum(at + k, room - 1)
-            out_ref[k * plan.full : (k + 1) * plan.full, :] = done_ref[
-                pl.ds(pl.multiple_of(slot * plan.full, plan.full), plan.full), :
-            ]
-            for e in range(plan.extra):
-                row = slots * plan.full + e * slots + k
-                out_ref[row : row + 1, :] = done_ref[
-                    pl.ds(room * plan.full + e * room + slot, 1), :
+        lax.fori_loop(0, jnp.minimum(total, room), step, 0)
+        for d, out_ref in enumerate(outs):
+            at = first_ref[here ^ d]
+            for k in range(plan.over):
+                slot = jnp.minimum(at + k, room - 1)
+                to = j * plan.over + k
+                out_ref[to * plan.full : (to + 1) * plan.full, :] = done_ref[
+                    pl.ds(pl.multiple_of(slot * plan.full, plan.full), plan.full), :
                 ]
-
-
-def relay(plan, table, params, dense):
+                for e in range(plan.extra):
+                    row = slots * plan.full + e * slots + to
+                    out_ref[row : row + 1, :] = done_ref[
+                        pl.ds(room * plan.full + e * room + slot, 1), :
+                    ]
+
+
+def relay(plan, table, params, dense, room):
     piece = jax.ShapeDtypeStruct((plan.relay_rows, plan.width), dense[0].dtype)
-    rows = round_up(len(dense) * plan.chunk * plan.rows, sublanes)
+    starts = pltpu.SMEM((plan.flat,), jnp.int32)
+    blocks = pltpu.VMEM(dense[0].shape, dense[0].dtype)
     return pl.pallas_call(
-        functools.partial(relay_kernel, plan=plan, chunks=len(dense)),
-        in_specs=[smem_full] + [vmem_full] * (1 + len(dense)),
-        out_specs=[vmem_full] * plan.mates,
-        out_shape=[piece] * plan.mates,
-        scratch_shapes=[
-            pltpu.SMEM((plan.devices,), jnp.int32),
-            pltpu.VMEM((rows, plan.width), dense[0].dtype),
-        ],
+        functools.partial(relay_kernel, plan=plan, room=room),
+        in_specs=[smem_full] + [vmem_full] * 3,
+        out_specs=[vmem_full] * plan.flat,
+        out_shape=[piece] * plan.flat,
+        scratch_shapes=[starts, starts, blocks, blocks],
         name="relay",
     )(table, params, *dense)
 
@@ -376,10 +375,13 @@
     direct = rank < plan.slots
     piece = plan.mate(block_part) ^ plan.mate(me)
     crossed = plan.mates * plan.inner_rows + piece * plan.cross_rows
-    relayed = plan.mates * (plan.inner_rows + plan.cross_rows) + piece * plan.relay_rows
+    spot = plan.spot(block_part) ^ plan.spot(me)
+    relayed = plan.mates * (plan.inner_rows + plan.cross_rows) + spot * plan.relay_rows
     origin = jnp.where(home, piece * plan.inner_rows, jnp.where(direct, crossed, relayed))
-    slots = jnp.where(home, plan.most, jnp.where(direct, plan.slots, plan.over))
-    slot = jnp.where(home | direct, rank, rank - plan.slots)
+    slots = jnp.where(home, plan.most, jnp.where(direct, plan.slots, 2 * plan.over))
+    flip = plan.plane(block_part) ^ plan.plane(me)
+    shift = jnp.where(flip == far_planes[0], 0, plan.over) - plan.slots
+    slot = jnp.where(home | direct, rank, rank + shift)
     return origin + slot * plan.full, origin + slots * plan.full + slot, slots
 
 
@@ -388,37 +390,36 @@
     return [d for pair in pairs[1:] + pairs[:1] for d in pair]
 
 
-def early_inner(mates):
-    return [d for d in mixed(mates) if d][: mates // 4]
-
-
-def exchange(plan, chunks, table, states, params, places, tile_perm):
+def early_inner(mates, side):
+    across = [d for d in mixed(mates) if d & side]
+    return across[: len(across) // 2]
+
+
+def exchange(plan, room, table, states, params, places, tile_perm):
     over = range(plan.devices)
-    ends = {"inner": plan.half, "again": plan.half, "cross": lambda i: 1 - plan.half(i)}
-
-    def send(kind, d, piece):
-        pairs = [(i, plan.device(plan.mate(i) ^ d, ends[kind](i))) for i in over]
-        return lax.ppermute(piece, both, pairs)
-
-    dense = pack_dense(plan, table, states, chunks)
-    crossed = []
-    for c in range(chunks):
-        crossed.append(
-            lax.ppermute(dense[c], both, [(i, plan.partner(i)) for i in over])
-        )
+
+    def send(piece, target):
+        return lax.ppermute(piece, both, [(i, target(i)) for i in over])
+
+    dense = pack_dense(plan, table, states, room)
+    crossed = [
+        send(piece, functools.partial(plan.twin, flip=far))
+        for far, piece in zip(far_planes, dense)
+    ]
     adv = advance(params, states)
-    first = early_inner(plan.mates)
+    first = early_inner(plan.mates, plan.side)
     second = [d for d in range(plan.mates) if d not in first]
     inner = dict(zip(first, pack_pieces(plan, table, adv, first, [])))
     more = pack_pieces(plan, table, adv, second, list(range(plan.mates)))
     inner.update(zip(second, more))
     cross = list(more[len(second) :])
-    again = list(relay(plan, table, params, crossed))
+    again = list(relay(plan, table, params, crossed, room))
     for d in range(plan.mates):
-        cross[d] = send("cross", d, cross[d])
+        cross[d] = send(cross[d], lambda i: plan.device(plan.mate(i) ^ d, 1 - plan.half(i)))
         if d:
-            inner[d] = send("inner", d, inner[d])
-            again[d] = send("again", d, again[d])
+            inner[d] = send(inner[d], lambda i: plan.device(plan.mate(i) ^ d, plan.half(i)))
+    for d in range(1, plan.flat):
+        again[d] = send(again[d], lambda i: plan.at(plan.spot(i) ^ d, plan.plane(i)))
     inner = [inner[d] for d in range(plan.mates)]
     return unpack(plan, places, tile_perm, [*inner, *cross, *again])
 
@@ -436,15 +437,18 @@
     told = jnp.broadcast_to(counts[None, None, :], (devices, 1, devices))
     table = lax.all_to_all(told, both, split_axis=0, concat_axis=0, tiled=True)
     params = gate_params(half_volt, steepness, gate_rate, conductance, reversal, width)
-    far = plan.half(ids)[:, None] != plan.half(ids)[None, :]
-    spilled = jnp.maximum(table - plan.slots, 0)
-    spilled = jnp.sum(jnp.where(far[:, None, :], spilled, 0), axis=0)
-    spilled = jnp.max(spilled)
+    spilled = jnp.maximum(table[:, 0, :] - plan.slots, 0)
+    planes = plan.plane(ids)
+    across = plan.half(ids)[:, None] != plan.half(ids)[None, :]
+    totals = [
+        jnp.sum(jnp.where(across & (planes == q)[:, None], spilled, 0), axis=0)
+        for q in range(4)
+    ]
+    spilled = jnp.max(jnp.stack(totals))
     places = find_places(plan, block_part, me)
-    most = -(-plan.worst // plan.chunk)
-    rooms = sorted({-(-most * 3 // 8), -(-most // 2), most})
-    choice = sum((spilled > room * plan.chunk).astype(jnp.int32) for room in rooms[:-1])
-    choice = jnp.asarray(choice, jnp.int32)
+    rooms = {round_up(plan.worst * eighths // 8, sublanes) for eighths in (3, 4, 5, 8)}
+    rooms = sorted(rooms)
+    choice = sum((spilled > room).astype(jnp.int32) for room in rooms[:-1])
     return lax.switch(
         choice,
         [functools.partial(exchange, plan, room) for room in rooms],

time: 343 us -> 313 us (0.913); the launches traced: 339 us -> 312 us
  starting transfers between devices: 141 us -> 104 us
  waiting for transfers between devices: 139 us -> 147 us
    ppermute x50 -> x40, starting transfers between devices: 135 us -> 97.7 us  [send(): return lax.ppermute(piece, both, [(i, target(i)) for i in over])]
    ppermute x50 -> x40, waiting for transfers between devices: 139 us -> 147 us  [send(): return lax.ppermute(piece, both, [(i, target(i)) for i in over])]
  transfers between devices with their start and end apart: 51 -> 41, of which waited for: 22 -> 16; matrix products, arithmetic and copies ran while one was open for 1% -> 2% of each run, Pallas kernels for 4% -> 5%
where the time goes in v5:
time: 313 us; the launch traced here: 312 us
  waiting for transfers between devices  147 us (47%)
  starting transfers between devices  104 us (33%)
  Pallas kernels  44.7 us (14%)
  other arithmetic  8.36 us (3%)
  local copies, waits for them, and re-layouts  4.61 us (1%)
    ppermute x40, waiting for transfers between devices, send(): return lax.ppermute(piece, both, [(i, target(i)) for i in over])  147 us
    ppermute x40, starting transfers between devices, send(): return lax.ppermute(piece, both, [(i, target(i)) for i in over])  97.7 us
    pallas_call x1, Pallas kernels, unpack(): pl.pallas_call(functools.partial(unpack_kernel, plan=plan, sizes=sizes),...  13.1 us
    pallas_call x2, Pallas kernels, pack_pieces(): pl.pallas_call(functools.partial(pieces_kernel, plan=plan, inner=inner, c...  11.2 us
    pallas_call x1, Pallas kernels, advance(): pl.pallas_call(functools.partial(advance_kernel, width=width), grid=(node...  9.46 us
  transfers between devices with their start and end apart: 41, of which 16 were waited for; matrix products, arithmetic and copies ran while one was open for 2% of the time, Pallas kernels for 5%

profile of v5, /device:TPU:25, one launch (start us, length us, event | category | flops | bytes accessed | tf_op | source)
XLA Modules:
  0.0 312.4 jit_solution(18003524043244760614)
XLA Ops:
  1.4 6.2 %all-to-all-start = ((s32[32,1,32]{2,1,0:T(1,128)}), s32[32,1,32]{2,1,0:T(1,128)S(1)}, u32[]{:S(2)}, u32[]{:S(2)}) async-start(s32[32,1,32]{2,1,0:T(1,128)} %broadcast_in_dim.16), calls=%async_computation | async-start | bytes 32768 | tf_op jit(solution)/shard_map/all_to_all | solution.py:438
  18.4 293.7 %conditional.1 = (f32[41,32768]{1,0:T(8,128)}) conditional(s32[]{:T(128)} %clamp.3, (f32[5,40]{1,0:T(8,128)S(1)}, f32[41,32768]{1,0:T(8,128)}, s32[32,1,32]{2,1,0:T(1,128)S(1)}, pred[256]{0:T(512)(128)(4,1)S(1)}, s32[256]{0:T(256)S(1)}, /*index=5*/pred[256]{0:T(512)(128)(4,1)S(1)}, s32[256,128]{1,0:T(8,128)}, ...), branch_computations={%region_10.11_spmd, %region_11.12_spmd, %region_12.13_spmd, %regio... | conditional | flops 53748492 | bytes 102100176 | solution.py:452
  19.3 9.5 %advance.5.adv_ref = f32[41,32768]{1,0:T(8,128)} custom-call(f32[5,41,128]{2,1,0:T(8,128)} %broadcast_in_dim.20.params_ref, f32[41,32768]{1,0:T(8,128)} %get-tuple-element.300.states_ref), custom_call_target="tpu_custom_call" | custom-call | flops 53739520 | bytes 10747904 | tf_op jit(solution)/shard_map/cond/branch_1_fun/advance/pallas_call | solution.py:117
  28.8 6.9 %branch_1_fun.2 = (f32[656,128]{1,0:T(8,128)}, f32[656,128]{1,0:T(8,128)}, f32[656,128]{1,0:T(8,128)}, f32[656,128]{1,0:T(8,128)}, f32[656,128]{1,0:T(8,128)}, /...) custom-call(s32[32,1,32]{2,1,0:T(1,128)S(1)} %get-tuple-element.119., ...), custom_call_target="tpu_custom_call" | custom-call | tf_op jit(solution)/shard_map/cond/branch_1_fun/pallas_call | solution.py:232
  44.1 15.9 %collective-permute-done.55.refs_16_ = f32[328,128]{1,0:T(8,128)S(1)} collective-permute-done((f32[328,128]{1,0:T(8,128)}, f32[328,128]{1,0:T(8,128)S(1)}, u32[]{:S(2)}, u32[]{:S(2)}) %collective-permute-start.55) | collective-permute-done | bytes 167968 | tf_op jit(solution)/shard_map/cond/branch_1_fun/ppermute | solution.py:402
  65.5 6.2 %collective-permute-start.61 = (f32[328,128]{1,0:T(8,128)}, f32[328,128]{1,0:T(8,128)S(1)}, u32[]{:S(2)}, u32[]{:S(2)}) collective-permute-start(f32[328,128]{1,0:T(8,128)} %get-tuple-element.144), channel_id=1, source_target_pairs={{0,14},{1,15},{2,12},{3,13},{4,10},{5,11},{6,8},{7,9},{8,6},{9,7},... | collective-permute-start | bytes 503816 | tf_op jit(solution)/shard_map/cond/branch_1_fun/ppermute | solution.py:402
  72.6 12.1 %collective-permute-start.63 = (f32[328,128]{1,0:T(8,128)}, f32[328,128]{1,0:T(8,128)S(1)}, u32[]{:S(2)}, u32[]{:S(2)}) collective-permute-start(f32[328,128]{1,0:T(8,128)} %get-tuple-element.146), channel_id=1, source_target_pairs={{0,20},{1,21},{2,22},{3,23},{4,16},{5,17},{6,18},{7,19},{8,28},{9,... | collective-permute-start | bytes 503816 | tf_op jit(solution)/shard_map/cond/branch_1_fun/ppermute | solution.py:402
  89.0 8.9 %collective-permute-done.60.refs_21_ = f32[328,128]{1,0:T(8,128)S(1)} collective-permute-done((f32[328,128]{1,0:T(8,128)}, f32[328,128]{1,0:T(8,128)S(1)}, u32[]{:S(2)}, u32[]{:S(2)}) %collective-permute-start.60) | collective-permute-done | bytes 167968 | tf_op jit(solution)/shard_map/cond/branch_1_fun/ppermute | solution.py:402
  103.3 12.6 %collective-permute-done.63.refs_24_ = f32[328,128]{1,0:T(8,128)S(1)} collective-permute-done((f32[328,128]{1,0:T(8,128)}, f32[328,128]{1,0:T(8,128)S(1)}, u32[]{:S(2)}, u32[]{:S(2)}) %collective-permute-start.63) | collective-permute-done | bytes 167968 | tf_op jit(solution)/shard_map/cond/branch_1_fun/ppermute | solution.py:402
  120.4 9.9 %collective-permute-start.69 = (f32[328,128]{1,0:T(8,128)}, f32[328,128]{1,0:T(8,128)S(1)}, u32[]{:S(2)}, u32[]{:S(2)}) collective-permute-start(f32[328,128]{1,0:T(8,128)} %get-tuple-element.152), channel_id=1, source_target_pairs={{0,30},{1,31},{2,28},{3,29},{4,26},{5,27},{6,24},{7,25},{8,22},{9,... | collective-permute-start | bytes 503816 | tf_op jit(solution)/shard_map/cond/branch_1_fun/ppermute | solution.py:402
  134.7 10.0 %collective-permute-done.67.refs_28_ = f32[328,128]{1,0:T(8,128)S(1)} collective-permute-done((f32[328,128]{1,0:T(8,128)}, f32[328,128]{1,0:T(8,128)S(1)}, u32[]{:S(2)}, u32[]{:S(2)}) %collective-permute-start.67) | collective-permute-done | bytes 167968 | tf_op jit(solution)/shard_map/cond/branch_1_fun/ppermute | solution.py:402
  144.7 5.2 %collective-permute-start.41 = (f32[656,128]{1,0:T(8,128)}, f32[656,128]{1,0:T(8,128)S(1)}, u32[]{:S(2)}, u32[]{:S(2)}) collective-permute-start(f32[656,128]{1,0:T(8,128)} %get-tuple-element.124), channel_id=1, source_target_pairs={{0,2},{1,3},{2,0},{3,1},{4,6},{5,7},{6,4},{7,5},{8,10},{9,11},{10,... | collective-permute-start | bytes 1007624 | tf_op jit(solution)/shard_map/cond/branch_1_fun/ppermute | solution.py:402
  151.1 5.5 %pack_dense.5 = (f32[1312,128]{1,0:T(8,128)}, f32[1312,128]{1,0:T(8,128)}) custom-call(s32[32,1,32]{2,1,0:T(1,128)S(1)} %get-tuple-element.119.table_ref, f32[41,32768]{1,0:T(8,128)} %get-tuple-element.300.states_ref), custom_call_target="tpu_custom_call" | custom-call | tf_op jit(solution)/shard_map/cond/branch_1_fun/pack_dense/pallas_call | solution.py:192
  162.9 7.3 %collective-permute-done.42.refs_3_ = f32[656,128]{1,0:T(8,128)S(1)} collective-permute-done((f32[656,128]{1,0:T(8,128)}, f32[656,128]{1,0:T(8,128)S(1)}, u32[]{:S(2)}, u32[]{:S(2)}) %collective-permute-start.42) | collective-permute-done | bytes 335904 | tf_op jit(solution)/shard_map/cond/branch_1_fun/ppermute | solution.py:402
  175.7 5.6 %collective-permute-start.47 = (f32[656,128]{1,0:T(8,128)}, f32[656,128]{1,0:T(8,128)}, u32[]{:S(2)}, u32[]{:S(2)}) collective-permute-start(f32[656,128]{1,0:T(8,128)} %get-tuple-element.130), channel_id=1, source_target_pairs={{0,16},{1,17},{2,18},{3,19},{4,20},{5,21},{6,22},{7,23},{8,24},{9,... | collective-permute-start | bytes 1007624 | tf_op jit(solution)/shard_map/cond/branch_1_fun/ppermute | solution.py:402
  181.4 23.8 %collective-permute-done.45.refs_6_ = f32[656,128]{1,0:T(8,128)S(1)} collective-permute-done((f32[656,128]{1,0:T(8,128)}, f32[656,128]{1,0:T(8,128)S(1)}, u32[]{:S(2)}, u32[]{:S(2)}) %collective-permute-start.45) | collective-permute-done | bytes 335904 | tf_op jit(solution)/shard_map/cond/branch_1_fun/ppermute | solution.py:402
  205.1 7.9 %collective-permute-done.46.refs_7_ = f32[656,128]{1,0:T(8,128)S(1)} collective-permute-done((f32[656,128]{1,0:T(8,128)}, f32[656,128]{1,0:T(8,128)S(1)}, u32[]{:S(2)}, u32[]{:S(2)}) %collective-permute-start.46) | collective-permute-done | bytes 335904 | tf_op jit(solution)/shard_map/cond/branch_1_fun/ppermute | solution.py:402
  219.8 5.5 %relay.5 = (f32[656,128]{1,0:T(8,128)}, f32[656,128]{1,0:T(8,128)}, f32[656,128]{1,0:T(8,128)}, f32[656,128]{1,0:T(8,128)}, f32[656,128]{1,0:T(8,128)}, /*index=...) custom-call(s32[32,1,32]{2,1,0:T(1,128)S(1)} %get-tuple-element.119.table_ref, ...), custom_call_target="tpu_custom_call" | custom-call | tf_op jit(solution)/shard_map/cond/branch_1_fun/relay/pallas_call | solution.py:291
  225.4 5.0 %collective-permute-start.53 = (f32[656,128]{1,0:T(8,128)}, f32[656,128]{1,0:T(8,128)S(1)}, u32[]{:S(2)}, u32[]{:S(2)}) collective-permute-start(f32[656,128]{1,0:T(8,128)} %get-tuple-element.136), channel_id=1, source_target_pairs={{0,26},{1,27},{2,24},{3,25},{4,30},{5,31},{6,28},{7,29},{8,18},{9,... | collective-permute-start | bytes 1007624 | tf_op jit(solution)/shard_map/cond/branch_1_fun/ppermute | solution.py:402
  230.4 10.0 %collective-permute-start.54 = (f32[656,128]{1,0:T(8,128)}, f32[656,128]{1,0:T(8,128)S(1)}, u32[]{:S(2)}, u32[]{:S(2)}) collective-permute-start(f32[656,128]{1,0:T(8,128)} %get-tuple-element.137), channel_id=1, source_target_pairs={{0,27},{1,26},{2,25},{3,24},{4,31},{5,30},{6,29},{7,28},{8,19},{9,... | collective-permute-start | bytes 1007624 | tf_op jit(solution)/shard_map/cond/branch_1_fun/ppermute | solution.py:402
  240.5 21.8 %collective-permute-done.51.refs_12_ = f32[656,128]{1,0:T(8,128)} collective-permute-done((f32[656,128]{1,0:T(8,128)}, f32[656,128]{1,0:T(8,128)}, u32[]{:S(2)}, u32[]{:S(2)}) %collective-permute-start.51) | collective-permute-done | bytes 335904 | tf_op jit(solution)/shard_map/cond/branch_1_fun/ppermute | solution.py:402
  276.4 14.7 %collective-permute-done.76.refs_36_ = f32[656,128]{1,0:T(8,128)} collective-permute-done((f32[656,128]{1,0:T(8,128)}, f32[656,128]{1,0:T(8,128)}, u32[]{:S(2)}, u32[]{:S(2)}) %collective-permute-start.76) | collective-permute-done | bytes 335904 | tf_op jit(solution)/shard_map/cond/branch_1_fun/ppermute | solution.py:402
  291.1 7.8 %collective-permute-done.78.refs_38_ = f32[656,128]{1,0:T(8,128)} collective-permute-done((f32[656,128]{1,0:T(8,128)}, f32[656,128]{1,0:T(8,128)}, u32[]{:S(2)}, u32[]{:S(2)}) %collective-permute-start.78) | collective-permute-done | bytes 335904 | tf_op jit(solution)/shard_map/cond/branch_1_fun/ppermute | solution.py:402
  299.0 13.1 %unpack.5 = f32[41,32768]{1,0:T(8,128)} custom-call(s32[256]{0:T(256)} %multiply_add_fusion.5.base_ref, s32[256]{0:T(256)} %get-tuple-element.751.tail_ref, s32[256]{0:T(256)} %get-tuple-element.752.step_ref, s32[256,128]{1,0:T(8,128)S(1)} %copy-done.1, f32[656,128]{1,0:T(8,128)} %get-tuple-element.122.refs_0_, f32[656,128]{1,0:T(8,128)} %copy-done.12, ...), custom_call_target="tpu_custom_call" | custom-call | tf_op jit(solution)/shard_map/cond/branch_1_fun/unpack/pallas_call | solution.py:343
  (154 shorter events, 77.7 us)
Async XLA Ops:
  39.0 32.7 %collective-permute-start.57 = (f32[328,128]{1,0:T(8,128)}, f32[328,128]{1,0:T(8,128)S(1)}, u32[]{:S(2)}, u32[]{:S(2)}) collective-permute-start(f32[328,128]{1,0:T(8,128)} %get-tuple-element.140), channel_id=1, source_target_pairs={{0,6},{1,7},{2,4},{3,5},{4,2},{5,3},{6,0},{7,1},{8,14},{9,15},{10,... | collective-permute-start | bytes 503816 | tf_op jit(solution)/shard_map/cond/branch_1_fun/ppermute | solution.py:402
  41.1 31.5 %collective-permute-start.58 = (f32[328,128]{1,0:T(8,128)}, f32[328,128]{1,0:T(8,128)S(1)}, u32[]{:S(2)}, u32[]{:S(2)}) collective-permute-start(f32[328,128]{1,0:T(8,128)} %get-tuple-element.141), channel_id=1, source_target_pairs={{0,7},{1,6},{2,5},{3,4},{4,3},{5,2},{6,1},{7,0},{8,15},{9,14},{10,... | collective-permute-start | bytes 503816 | tf_op jit(solution)/shard_map/cond/branch_1_fun/ppermute | solution.py:402
  42.2 45.1 %collective-permute-start.59 = (f32[328,128]{1,0:T(8,128)}, f32[328,128]{1,0:T(8,128)S(1)}, u32[]{:S(2)}, u32[]{:S(2)}) collective-permute-start(f32[328,128]{1,0:T(8,128)} %get-tuple-element.142), channel_id=1, source_target_pairs={{0,12},{1,13},{2,14},{3,15},{4,8},{5,9},{6,10},{7,11},{8,4},{9,5},... | collective-permute-start | bytes 503816 | tf_op jit(solution)/shard_map/cond/branch_1_fun/ppermute | solution.py:402
  60.0 37.9 %collective-permute-start.60 = (f32[328,128]{1,0:T(8,128)}, f32[328,128]{1,0:T(8,128)S(1)}, u32[]{:S(2)}, u32[]{:S(2)}) collective-permute-start(f32[328,128]{1,0:T(8,128)} %get-tuple-element.143), channel_id=1, source_target_pairs={{0,13},{1,12},{2,15},{3,14},{4,9},{5,8},{6,11},{7,10},{8,5},{9,4},... | collective-permute-start | bytes 503816 | tf_op jit(solution)/shard_map/cond/branch_1_fun/ppermute | solution.py:402
  65.5 34.5 %collective-permute-start.61 = (f32[328,128]{1,0:T(8,128)}, f32[328,128]{1,0:T(8,128)S(1)}, u32[]{:S(2)}, u32[]{:S(2)}) collective-permute-start(f32[328,128]{1,0:T(8,128)} %get-tuple-element.144), channel_id=1, source_target_pairs={{0,14},{1,15},{2,12},{3,13},{4,10},{5,11},{6,8},{7,9},{8,6},{9,7},... | collective-permute-start | bytes 503816 | tf_op jit(solution)/shard_map/cond/branch_1_fun/ppermute | solution.py:402
  71.7 31.2 %collective-permute-start.62 = (f32[328,128]{1,0:T(8,128)}, f32[328,128]{1,0:T(8,128)S(1)}, u32[]{:S(2)}, u32[]{:S(2)}) collective-permute-start(f32[328,128]{1,0:T(8,128)} %get-tuple-element.145), channel_id=1, source_target_pairs={{0,15},{1,14},{2,13},{3,12},{4,11},{5,10},{6,9},{7,8},{8,7},{9,6},... | collective-permute-start | bytes 503816 | tf_op jit(solution)/shard_map/cond/branch_1_fun/ppermute | solution.py:402
  72.6 43.3 %collective-permute-start.63 = (f32[328,128]{1,0:T(8,128)}, f32[328,128]{1,0:T(8,128)S(1)}, u32[]{:S(2)}, u32[]{:S(2)}) collective-permute-start(f32[328,128]{1,0:T(8,128)} %get-tuple-element.146), channel_id=1, source_target_pairs={{0,20},{1,21},{2,22},{3,23},{4,16},{5,17},{6,18},{7,19},{8,28},{9,... | collective-permute-start | bytes 503816 | tf_op jit(solution)/shard_map/cond/branch_1_fun/ppermute | solution.py:402
  87.4 33.0 %collective-permute-start.64 = (f32[328,128]{1,0:T(8,128)}, f32[328,128]{1,0:T(8,128)S(1)}, u32[]{:S(2)}, u32[]{:S(2)}) collective-permute-start(f32[328,128]{1,0:T(8,128)} %get-tuple-element.147), channel_id=1, source_target_pairs={{0,21},{1,20},{2,23},{3,22},{4,17},{5,16},{6,19},{7,18},{8,29},{9,... | collective-permute-start | bytes 503816 | tf_op jit(solution)/shard_map/cond/branch_1_fun/ppermute | solution.py:402
  100.0 30.3 %collective-permute-start.66 = (f32[328,128]{1,0:T(8,128)}, f32[328,128]{1,0:T(8,128)S(1)}, u32[]{:S(2)}, u32[]{:S(2)}) collective-permute-start(f32[328,128]{1,0:T(8,128)} %get-tuple-element.149), channel_id=1, source_target_pairs={{0,23},{1,22},{2,21},{3,20},{4,19},{5,18},{6,17},{7,16},{8,31},{9,... | collective-permute-start | bytes 503816 | tf_op jit(solution)/shard_map/cond/branch_1_fun/ppermute | solution.py:402
  102.9 56.2 %collective-permute-start.40 = (f32[656,128]{1,0:T(8,128)}, f32[656,128]{1,0:T(8,128)S(1)}, u32[]{:S(2)}, u32[]{:S(2)}) collective-permute-start(f32[656,128]{1,0:T(8,128)} %get-tuple-element.123), channel_id=1, source_target_pairs={{0,1},{1,0},{2,3},{3,2},{4,5},{5,4},{6,7},{7,6},{8,9},{9,8},{10,11... | collective-permute-start | bytes 1007624 | tf_op jit(solution)/shard_map/cond/branch_1_fun/ppermute | solution.py:402
  115.9 28.8 %collective-permute-start.67 = (f32[328,128]{1,0:T(8,128)}, f32[328,128]{1,0:T(8,128)S(1)}, u32[]{:S(2)}, u32[]{:S(2)}) collective-permute-start(f32[328,128]{1,0:T(8,128)} %get-tuple-element.150), channel_id=1, source_target_pairs={{0,28},{1,29},{2,30},{3,31},{4,24},{5,25},{6,26},{7,27},{8,20},{9,... | collective-permute-start | bytes 503816 | tf_op jit(solution)/shard_map/cond/branch_1_fun/ppermute | solution.py:402
  120.4 29.6 %collective-permute-start.68 = (f32[328,128]{1,0:T(8,128)}, f32[328,128]{1,0:T(8,128)S(1)}, u32[]{:S(2)}, u32[]{:S(2)}) collective-permute-start(f32[328,128]{1,0:T(8,128)} %get-tuple-element.151), channel_id=1, source_target_pairs={{0,29},{1,28},{2,31},{3,30},{4,25},{5,24},{6,27},{7,26},{8,21},{9,... | collective-permute-start | bytes 503816 | tf_op jit(solution)/shard_map/cond/branch_1_fun/ppermute | solution.py:402
  120.4 29.6 %collective-permute-start.69 = (f32[328,128]{1,0:T(8,128)}, f32[328,128]{1,0:T(8,128)S(1)}, u32[]{:S(2)}, u32[]{:S(2)}) collective-permute-start(f32[328,128]{1,0:T(8,128)} %get-tuple-element.152), channel_id=1, source_target_pairs={{0,30},{1,31},{2,28},{3,29},{4,26},{5,27},{6,24},{7,25},{8,22},{9,... | collective-permute-start | bytes 503816 | tf_op jit(solution)/shard_map/cond/branch_1_fun/ppermute | solution.py:402
  156.6 58.0 %collective-permute-start.71 = (f32[1312,128]{1,0:T(8,128)}, f32[1312,128]{1,0:T(8,128)S(1)}, u32[]{:S(2)}, u32[]{:S(2)}) collective-permute-start(f32[1312,128]{1,0:T(8,128)} %get-tuple-element.154), channel_id=1, source_target_pairs={{0,4},{1,5},{2,6},{3,7},{4,0},{5,1},{6,2},{7,3},{8,12},{9,13},{10,... | collective-permute-start | bytes 2015240 | tf_op jit(solution)/shard_map/cond/branch_1_fun/ppermute | solution.py:402
  159.2 56.1 %collective-permute-start.72 = (f32[1312,128]{1,0:T(8,128)}, f32[1312,128]{1,0:T(8,128)S(1)}, u32[]{:S(2)}, u32[]{:S(2)}) collective-permute-start(f32[1312,128]{1,0:T(8,128)} %get-tuple-element.155), channel_id=1, source_target_pairs={{0,6},{1,7},{2,4},{3,5},{4,2},{5,3},{6,0},{7,1},{8,14},{9,15},{10,... | collective-permute-start | bytes 2015240 | tf_op jit(solution)/shard_map/cond/branch_1_fun/ppermute | solution.py:402
  170.3 34.9 %collective-permute-start.45 = (f32[656,128]{1,0:T(8,128)}, f32[656,128]{1,0:T(8,128)S(1)}, u32[]{:S(2)}, u32[]{:S(2)}) collective-permute-start(f32[656,128]{1,0:T(8,128)} %get-tuple-element.128), channel_id=1, source_target_pairs={{0,10},{1,11},{2,8},{3,9},{4,14},{5,15},{6,12},{7,13},{8,2},{9,3},... | collective-permute-start | bytes 1007624 | tf_op jit(solution)/shard_map/cond/branch_1_fun/ppermute | solution.py:402
  170.3 42.8 %collective-permute-start.46 = (f32[656,128]{1,0:T(8,128)}, f32[656,128]{1,0:T(8,128)S(1)}, u32[]{:S(2)}, u32[]{:S(2)}) collective-permute-start(f32[656,128]{1,0:T(8,128)} %get-tuple-element.129), channel_id=1, source_target_pairs={{0,11},{1,10},{2,9},{3,8},{4,15},{5,14},{6,13},{7,12},{8,3},{9,2},... | collective-permute-start | bytes 1007624 | tf_op jit(solution)/shard_map/cond/branch_1_fun/ppermute | solution.py:402
  175.7 49.7 %collective-permute-start.47 = (f32[656,128]{1,0:T(8,128)}, f32[656,128]{1,0:T(8,128)}, u32[]{:S(2)}, u32[]{:S(2)}) collective-permute-start(f32[656,128]{1,0:T(8,128)} %get-tuple-element.130), channel_id=1, source_target_pairs={{0,16},{1,17},{2,18},{3,19},{4,20},{5,21},{6,22},{7,23},{8,24},{9,... | collective-permute-start | bytes 1007624 | tf_op jit(solution)/shard_map/cond/branch_1_fun/ppermute | solution.py:402
  215.3 47.0 %collective-permute-start.51 = (f32[656,128]{1,0:T(8,128)}, f32[656,128]{1,0:T(8,128)}, u32[]{:S(2)}, u32[]{:S(2)}) collective-permute-start(f32[656,128]{1,0:T(8,128)} %get-tuple-element.134), channel_id=1, source_target_pairs={{0,24},{1,25},{2,26},{3,27},{4,28},{5,29},{6,30},{7,31},{8,16},{9,... | collective-permute-start | bytes 1007624 | tf_op jit(solution)/shard_map/cond/branch_1_fun/ppermute | solution.py:402
  225.4 37.1 %collective-permute-start.52 = (f32[656,128]{1,0:T(8,128)}, f32[656,128]{1,0:T(8,128)S(1)}, u32[]{:S(2)}, u32[]{:S(2)}) collective-permute-start(f32[656,128]{1,0:T(8,128)} %get-tuple-element.135), channel_id=1, source_target_pairs={{0,25},{1,24},{2,27},{3,26},{4,29},{5,28},{6,31},{7,30},{8,17},{9,... | collective-permute-start | bytes 1007624 | tf_op jit(solution)/shard_map/cond/branch_1_fun/ppermute | solution.py:402
  225.4 41.9 %collective-permute-start.53 = (f32[656,128]{1,0:T(8,128)}, f32[656,128]{1,0:T(8,128)S(1)}, u32[]{:S(2)}, u32[]{:S(2)}) collective-permute-start(f32[656,128]{1,0:T(8,128)} %get-tuple-element.136), channel_id=1, source_target_pairs={{0,26},{1,27},{2,24},{3,25},{4,30},{5,31},{6,28},{7,29},{8,18},{9,... | collective-permute-start | bytes 1007624 | tf_op jit(solution)/shard_map/cond/branch_1_fun/ppermute | solution.py:402
  230.4 36.9 %collective-permute-start.54 = (f32[656,128]{1,0:T(8,128)}, f32[656,128]{1,0:T(8,128)S(1)}, u32[]{:S(2)}, u32[]{:S(2)}) collective-permute-start(f32[656,128]{1,0:T(8,128)} %get-tuple-element.137), channel_id=1, source_target_pairs={{0,27},{1,26},{2,25},{3,24},{4,31},{5,30},{6,29},{7,28},{8,19},{9,... | collective-permute-start | bytes 1007624 | tf_op jit(solution)/shard_map/cond/branch_1_fun/ppermute | solution.py:402
  268.6 30.2 %collective-permute-start.78 = (f32[656,128]{1,0:T(8,128)}, f32[656,128]{1,0:T(8,128)}, u32[]{:S(2)}, u32[]{:S(2)}) collective-permute-start(f32[656,128]{1,0:T(8,128)} %get-tuple-element.162), channel_id=1, source_target_pairs={{0,24},{1,25},{2,26},{3,27},{4,28},{5,29},{6,30},{7,31},{8,16},{9,... | collective-permute-start | bytes 1007624 | tf_op jit(solution)/shard_map/cond/branch_1_fun/ppermute | solution.py:402
  269.5 29.4 %collective-permute-start.79 = (f32[656,128]{1,0:T(8,128)}, f32[656,128]{1,0:T(8,128)}, u32[]{:S(2)}, u32[]{:S(2)}) collective-permute-start(f32[656,128]{1,0:T(8,128)} %get-tuple-element.163), channel_id=1, source_target_pairs={{0,25},{1,24},{2,27},{3,26},{4,29},{5,28},{6,31},{7,30},{8,17},{9,... | collective-permute-start | bytes 1007624 | tf_op jit(solution)/shard_map/cond/branch_1_fun/ppermute | solution.py:402
  (48 other events, 2236.8 us)

commit v6 on v5

--- a/solution.py
+++ b/solution.py
@@ -28,7 +28,7 @@
         self.near = self.peers // 2
         self.mates = self.devices // 2
         most = 2 * blocks // self.devices
-        self.slots = max(most // 2, 1)
+        self.slots = max(3 * most // 8, 1)
         self.over = most - self.slots
         self.full = rows // sublanes * sublanes
         self.extra = rows - self.full
@@ -395,7 +395,7 @@
     return across[: len(across) // 2]
 
 
-def exchange(plan, room, table, states, params, places, tile_perm):
+def exchange(plan, room, table, states, params, block_part, tile_perm):
     over = range(plan.devices)
 
     def send(piece, target):
@@ -421,6 +421,7 @@
     for d in range(1, plan.flat):
         again[d] = send(again[d], lambda i: plan.at(plan.spot(i) ^ d, plan.plane(i)))
     inner = [inner[d] for d in range(plan.mates)]
+    places = find_places(plan, block_part, plan.me())
     return unpack(plan, places, tile_perm, [*inner, *cross, *again])
 
 
@@ -430,24 +431,18 @@
     blocks, width = tile_perm.shape
     plan = Plan(states.shape[0], blocks, width)
     devices = plan.devices
-    me = plan.me()
     ids = jnp.arange(devices, dtype=jnp.int32)
     onehot = (block_part[:, None] == ids[None, :]).astype(jnp.int32)
     counts = jnp.sum(onehot, axis=0, dtype=jnp.int32)
     told = jnp.broadcast_to(counts[None, None, :], (devices, 1, devices))
     table = lax.all_to_all(told, both, split_axis=0, concat_axis=0, tiled=True)
     params = gate_params(half_volt, steepness, gate_rate, conductance, reversal, width)
-    spilled = jnp.maximum(table[:, 0, :] - plan.slots, 0)
-    planes = plan.plane(ids)
-    across = plan.half(ids)[:, None] != plan.half(ids)[None, :]
-    totals = [
-        jnp.sum(jnp.where(across & (planes == q)[:, None], spilled, 0), axis=0)
-        for q in range(4)
-    ]
-    spilled = jnp.max(jnp.stack(totals))
-    places = find_places(plan, block_part, me)
-    rooms = {round_up(plan.worst * eighths // 8, sublanes) for eighths in (3, 4, 5, 8)}
-    rooms = sorted(rooms)
+    spilled = jnp.maximum(table - plan.slots, 0)
+    spilled = spilled.reshape(devices // plan.peers, 4, plan.side, devices)
+    spilled = jnp.sum(spilled, axis=(0, 2), dtype=jnp.int32)
+    across = plan.half(ids)[None, :] != jnp.arange(4, dtype=jnp.int32)[:, None] // 2
+    spilled = jnp.max(jnp.where(across, spilled, 0))
+    rooms = sorted({round_up(-(-plan.worst * part // 40), 2) for part in (18, 21, 25, 40)})
     choice = sum((spilled > room).astype(jnp.int32) for room in rooms[:-1])
     return lax.switch(
         choice,
@@ -455,7 +450,7 @@
         table,
         states,
         params,
-        places,
+        block_part,
         tile_perm,
     )
 

time: 313 us -> 356 us (1.14)
  starting transfers between devices: 104 us -> 129 us
  waiting for transfers between devices: 147 us -> 165 us
  other arithmetic: 8.36 us -> 3.57 us
    ppermute x40, starting transfers between devices: 97.7 us -> 123 us  [send(): return lax.ppermute(piece, both, [(i, target(i)) for i in over])]
    ppermute x40, waiting for transfers between devices: 147 us -> 163 us  [send(): return lax.ppermute(piece, both, [(i, target(i)) for i in over])]
    cond x62 -> x74, local copies, waits for them, and re-layouts: 0.68 us -> 5.11 us
  transfers between devices with their start and end apart: 41 -> 41, of which waited for: 16 -> 21; matrix products, arithmetic and copies ran while one was open for 2% -> 1% of each run, Pallas kernels for 5% -> 5%
where the time goes in v6:
time: 356 us; the launch traced here: 354 us
  waiting for transfers between devices  165 us (46%)
  starting transfers between devices  129 us (36%)
  Pallas kernels  46.2 us (13%)
  local copies, waits for them, and re-layouts  7.26 us (2%)
  other arithmetic  3.57 us (1%)
    ppermute x40, waiting for transfers between devices, send(): return lax.ppermute(piece, both, [(i, target(i)) for i in over])  163 us
    ppermute x40, starting transfers between devices, send(): return lax.ppermute(piece, both, [(i, target(i)) for i in over])  123 us
    pallas_call x1, Pallas kernels, unpack(): pl.pallas_call(functools.partial(unpack_kernel, plan=plan, sizes=sizes),...  13 us
    pallas_call x2, Pallas kernels, pack_pieces(): pl.pallas_call(functools.partial(pieces_kernel, plan=plan, inner=inner, c...  10.9 us
    pallas_call x1, Pallas kernels, advance(): pl.pallas_call(functools.partial(advance_kernel, width=width), grid=(node...  9.46 us
  transfers between devices with their start and end apart: 41, of which 21 were waited for; matrix products, arithmetic and copies ran while one was open for 1% of the time, Pallas kernels for 5%

profile of v6, /device:TPU:25, one launch (start us, length us, event | category | flops | bytes accessed | tf_op | source)
XLA Modules:
  0.0 353.8 jit_solution(10239153364928593106)
XLA Ops:
  1.4 6.2 %all-to-all-start = ((s32[32,1,32]{2,1,0:T(1,128)}), s32[32,1,32]{2,1,0:T(1,128)S(1)}, u32[]{:S(2)}, u32[]{:S(2)}) async-start(s32[32,1,32]{2,1,0:T(1,128)} %broadcast_in_dim.83), calls=%async_computation | async-start | bytes 32768 | tf_op jit(solution)/shard_map/all_to_all | solution.py:438
  14.0 339.7 %conditional.1 = (f32[41,32768]{1,0:T(8,128)}) conditional(s32[]{:T(128)} %clamp.3, (s32[256]{0:T(256)}, f32[5,40]{1,0:T(8,128)S(1)}, f32[41,32768]{1,0:T(8,128)}, s32[32,1,32]{2,1,0:T(1,128)S(1)}, s32[256,128]{1,0:T(8,128)}, /*index=5*/()) %tuple.17, (s32[256]{0:T(256)}, f32[5,40]{1,0:T(8,128)S(1)}, ...), branch_computations={%region_3.5_spmd, %region_5.7_spmd, %region_7.9_spmd, %region_9.11... | conditional | flops 54089800 | bytes 102263504 | solution.py:447
  15.0 9.5 %advance.6.adv_ref = f32[41,32768]{1,0:T(8,128)} custom-call(f32[5,41,128]{2,1,0:T(8,128)} %broadcast_in_dim.88.params_ref, f32[41,32768]{1,0:T(8,128)} %get-tuple-element.261.states_ref), custom_call_target="tpu_custom_call" | custom-call | flops 53739520 | bytes 10747904 | tf_op jit(solution)/shard_map/cond/branch_2_fun/advance/pallas_call | solution.py:117
  24.5 6.5 %branch_2_fun.2 = (f32[656,128]{1,0:T(8,128)}, f32[656,128]{1,0:T(8,128)}, f32[656,128]{1,0:T(8,128)}, f32[656,128]{1,0:T(8,128)}, f32[656,128]{1,0:T(8,128)}, /...) custom-call(s32[32,1,32]{2,1,0:T(1,128)S(1)} %get-tuple-element.146., ...), custom_call_target="tpu_custom_call" | custom-call | tf_op jit(solution)/shard_map/cond/branch_2_fun/pallas_call | solution.py:232
  39.6 10.6 %collective-permute-done.95.refs_16_ = f32[248,128]{1,0:T(8,128)S(1)} collective-permute-done((f32[248,128]{1,0:T(8,128)}, f32[248,128]{1,0:T(8,128)S(1)}, u32[]{:S(2)}, u32[]{:S(2)}) %collective-permute-start.95) | collective-permute-done | bytes 127008 | tf_op jit(solution)/shard_map/cond/branch_2_fun/ppermute | solution.py:402
  52.9 4.4 %collective-permute-start.101 = (f32[248,128]{1,0:T(8,128)}, f32[248,128]{1,0:T(8,128)S(1)}, u32[]{:S(2)}, u32[]{:S(2)}) collective-permute-start(f32[248,128]{1,0:T(8,128)} %get-tuple-element.171), channel_id=1, source_target_pairs={{0,14},{1,15},{2,12},{3,13},{4,10},{5,11},{6,8},{7,9},{8,6},{9,7},... | collective-permute-start | bytes 380936 | tf_op jit(solution)/shard_map/cond/branch_2_fun/ppermute | solution.py:402
  64.2 7.2 %collective-permute-done.99.refs_20_ = f32[248,128]{1,0:T(8,128)S(1)} collective-permute-done((f32[248,128]{1,0:T(8,128)}, f32[248,128]{1,0:T(8,128)S(1)}, u32[]{:S(2)}, u32[]{:S(2)}) %collective-permute-start.99) | collective-permute-done | bytes 127008 | tf_op jit(solution)/shard_map/cond/branch_2_fun/ppermute | solution.py:402
  71.8 6.0 %collective-permute-done.100.refs_21_ = f32[248,128]{1,0:T(8,128)S(1)} collective-permute-done((f32[248,128]{1,0:T(8,128)}, f32[248,128]{1,0:T(8,128)S(1)}, u32[]{:S(2)}, u32[]{:S(2)}) %collective-permute-start.100) | collective-permute-done | bytes 127008 | tf_op jit(solution)/shard_map/cond/branch_2_fun/ppermute | solution.py:402
  78.5 4.4 %collective-permute-start.106 = (f32[248,128]{1,0:T(8,128)}, f32[248,128]{1,0:T(8,128)S(1)}, u32[]{:S(2)}, u32[]{:S(2)}) collective-permute-start(f32[248,128]{1,0:T(8,128)} %get-tuple-element.176), channel_id=1, source_target_pairs={{0,23},{1,22},{2,21},{3,20},{4,19},{5,18},{6,17},{7,16},{8,31},{9,... | collective-permute-start | bytes 380936 | tf_op jit(solution)/shard_map/cond/branch_2_fun/ppermute | solution.py:402
  82.9 5.9 %pack_dense.6 = (f32[2056,128]{1,0:T(8,128)}, f32[2056,128]{1,0:T(8,128)}) custom-call(s32[32,1,32]{2,1,0:T(1,128)S(1)} %get-tuple-element.146.table_ref, f32[41,32768]{1,0:T(8,128)} %get-tuple-element.261.states_ref), custom_call_target="tpu_custom_call" | custom-call | tf_op jit(solution)/shard_map/cond/branch_2_fun/pack_dense/pallas_call | solution.py:192
  97.1 50.3 %collective-permute-start.108 = (f32[248,128]{1,0:T(8,128)}, f32[248,128]{1,0:T(8,128)S(1)}, u32[]{:S(2)}, u32[]{:S(2)}) collective-permute-start(f32[248,128]{1,0:T(8,128)} %get-tuple-element.178), channel_id=1, source_target_pairs={{0,29},{1,28},{2,31},{3,30},{4,25},{5,24},{6,27},{7,26},{8,21},{9,... | collective-permute-start | bytes 380936 | tf_op jit(solution)/shard_map/cond/branch_2_fun/ppermute | solution.py:402
  151.3 48.7 %collective-permute-done.107.refs_28_ = f32[248,128]{1,0:T(8,128)S(1)} collective-permute-done((f32[248,128]{1,0:T(8,128)S(1)}, f32[248,128]{1,0:T(8,128)S(1)}, u32[]{:S(2)}, u32[]{:S(2)}) %collective-permute-start.107) | collective-permute-done | bytes 127008 | tf_op jit(solution)/shard_map/cond/branch_2_fun/ppermute | solution.py:402
  206.7 4.4 %branch_2_fun.3 = (f32[656,128]{1,0:T(8,128)}, f32[656,128]{1,0:T(8,128)}, f32[656,128]{1,0:T(8,128)}, f32[656,128]{1,0:T(8,128)}) custom-call(s32[32,1,32]{2,1,0:T(1,128)S(1)} %get-tuple-element.146.table_ref, f32[41,32768]{1,0:T(8,128)} %advance.6.adv_ref), custom_call_target="tpu_custom_call" | custom-call | tf_op jit(solution)/shard_map/cond/branch_2_fun/pallas_call | solution.py:232
  215.9 4.8 %collective-permute-done.81.refs_2_ = f32[656,128]{1,0:T(8,128)S(1)} collective-permute-done((f32[656,128]{1,0:T(8,128)}, f32[656,128]{1,0:T(8,128)S(1)}, u32[]{:S(2)}, u32[]{:S(2)}) %collective-permute-start.81) | collective-permute-done | bytes 335904 | tf_op jit(solution)/shard_map/cond/branch_2_fun/ppermute | solution.py:402
  222.6 5.5 %collective-permute-done.82.refs_3_ = f32[656,128]{1,0:T(8,128)S(1)} collective-permute-done((f32[656,128]{1,0:T(8,128)}, f32[656,128]{1,0:T(8,128)S(1)}, u32[]{:S(2)}, u32[]{:S(2)}) %collective-permute-start.82) | collective-permute-done | bytes 335904 | tf_op jit(solution)/shard_map/cond/branch_2_fun/ppermute | solution.py:402
  230.6 5.2 %collective-permute-done.84.refs_5_ = f32[656,128]{1,0:T(8,128)S(1)} collective-permute-done((f32[656,128]{1,0:T(8,128)}, f32[656,128]{1,0:T(8,128)S(1)}, u32[]{:S(2)}, u32[]{:S(2)}) %collective-permute-start.84) | collective-permute-done | bytes 335904 | tf_op jit(solution)/shard_map/cond/branch_2_fun/ppermute | solution.py:402
  240.8 5.6 %collective-permute-done.86.refs_7_ = f32[656,128]{1,0:T(8,128)S(1)} collective-permute-done((f32[656,128]{1,0:T(8,128)}, f32[656,128]{1,0:T(8,128)S(1)}, u32[]{:S(2)}, u32[]{:S(2)}) %collective-permute-start.86) | collective-permute-done | bytes 335904 | tf_op jit(solution)/shard_map/cond/branch_2_fun/ppermute | solution.py:402
  251.9 7.0 %relay.6 = (f32[824,128]{1,0:T(8,128)}, f32[824,128]{1,0:T(8,128)}, f32[824,128]{1,0:T(8,128)}, f32[824,128]{1,0:T(8,128)}, f32[824,128]{1,0:T(8,128)}, /*index=...) custom-call(s32[32,1,32]{2,1,0:T(1,128)S(1)} %get-tuple-element.146.table_ref, ...), custom_call_target="tpu_custom_call" | custom-call | tf_op jit(solution)/shard_map/cond/branch_2_fun/relay/pallas_call | solution.py:291
  264.4 4.5 %collective-permute-done.90.refs_11_ = f32[656,128]{1,0:T(8,128)} collective-permute-done((f32[656,128]{1,0:T(8,128)}, f32[656,128]{1,0:T(8,128)}, u32[]{:S(2)}, u32[]{:S(2)}) %collective-permute-start.90) | collective-permute-done | bytes 335904 | tf_op jit(solution)/shard_map/cond/branch_2_fun/ppermute | solution.py:402
  270.2 21.1 %collective-permute-done.91.refs_12_ = f32[656,128]{1,0:T(8,128)} collective-permute-done((f32[656,128]{1,0:T(8,128)}, f32[656,128]{1,0:T(8,128)}, u32[]{:S(2)}, u32[]{:S(2)}) %collective-permute-start.91) | collective-permute-done | bytes 335904 | tf_op jit(solution)/shard_map/cond/branch_2_fun/ppermute | solution.py:402
  296.3 7.1 %collective-permute-done.94.refs_15_ = f32[656,128]{1,0:T(8,128)S(1)} collective-permute-done((f32[656,128]{1,0:T(8,128)}, f32[656,128]{1,0:T(8,128)S(1)}, u32[]{:S(2)}, u32[]{:S(2)}) %collective-permute-start.94) | collective-permute-done | bytes 335904 | tf_op jit(solution)/shard_map/cond/branch_2_fun/ppermute | solution.py:402
  312.7 9.0 %collective-permute-done.117.refs_37_ = f32[824,128]{1,0:T(8,128)S(1)} collective-permute-done((f32[824,128]{1,0:T(8,128)}, f32[824,128]{1,0:T(8,128)S(1)}, u32[]{:S(2)}, u32[]{:S(2)}) %collective-permute-start.117) | collective-permute-done | bytes 421920 | tf_op jit(solution)/shard_map/cond/branch_2_fun/ppermute | solution.py:402
  321.6 18.1 %collective-permute-done.118.refs_38_ = f32[824,128]{1,0:T(8,128)S(1)} collective-permute-done((f32[824,128]{1,0:T(8,128)}, f32[824,128]{1,0:T(8,128)S(1)}, u32[]{:S(2)}, u32[]{:S(2)}) %collective-permute-start.118) | collective-permute-done | bytes 421920 | tf_op jit(solution)/shard_map/cond/branch_2_fun/ppermute | solution.py:402
  340.7 13.0 %unpack.6 = f32[41,32768]{1,0:T(8,128)} custom-call(s32[256]{0:T(256)} %multiply_add_fusion.2.base_ref, s32[256]{0:T(256)} %get-tuple-element.275.tail_ref, s32[256]{0:T(256)} %get-tuple-element.276.step_ref, s32[256,128]{1,0:T(8,128)S(1)} %copy-done.2, f32[656,128]{1,0:T(8,128)} %get-tuple-element.149.refs_0_, f32[656,128]{1,0:T(8,128)} %copy-done.42, ...), custom_call_target="tpu_custom_call" | custom-call | tf_op jit(solution)/shard_map/cond/branch_2_fun/unpack/pallas_call | solution.py:343
  (153 shorter events, 86.3 us)
Async XLA Ops:
  33.5 23.9 %collective-permute-start.97 = (f32[248,128]{1,0:T(8,128)}, f32[248,128]{1,0:T(8,128)S(1)}, u32[]{:S(2)}, u32[]{:S(2)}) collective-permute-start(f32[248,128]{1,0:T(8,128)} %get-tuple-element.167), channel_id=1, source_target_pairs={{0,6},{1,7},{2,4},{3,5},{4,2},{5,3},{6,0},{7,1},{8,14},{9,15},{10,... | collective-permute-start | bytes 380936 | tf_op jit(solution)/shard_map/cond/branch_2_fun/ppermute | solution.py:402
  36.5 24.5 %collective-permute-start.98 = (f32[248,128]{1,0:T(8,128)}, f32[248,128]{1,0:T(8,128)S(1)}, u32[]{:S(2)}, u32[]{:S(2)}) collective-permute-start(f32[248,128]{1,0:T(8,128)} %get-tuple-element.168), channel_id=1, source_target_pairs={{0,7},{1,6},{2,5},{3,4},{4,3},{5,2},{6,1},{7,0},{8,15},{9,14},{10,... | collective-permute-start | bytes 380936 | tf_op jit(solution)/shard_map/cond/branch_2_fun/ppermute | solution.py:402
  37.6 33.7 %collective-permute-start.99 = (f32[248,128]{1,0:T(8,128)}, f32[248,128]{1,0:T(8,128)S(1)}, u32[]{:S(2)}, u32[]{:S(2)}) collective-permute-start(f32[248,128]{1,0:T(8,128)} %get-tuple-element.169), channel_id=1, source_target_pairs={{0,12},{1,13},{2,14},{3,15},{4,8},{5,9},{6,10},{7,11},{8,4},{9,5},... | collective-permute-start | bytes 380936 | tf_op jit(solution)/shard_map/cond/branch_2_fun/ppermute | solution.py:402
  50.2 27.7 %collective-permute-start.100 = (f32[248,128]{1,0:T(8,128)}, f32[248,128]{1,0:T(8,128)S(1)}, u32[]{:S(2)}, u32[]{:S(2)}) collective-permute-start(f32[248,128]{1,0:T(8,128)} %get-tuple-element.170), channel_id=1, source_target_pairs={{0,13},{1,12},{2,15},{3,14},{4,9},{5,8},{6,11},{7,10},{8,5},{9,4},... | collective-permute-start | bytes 380936 | tf_op jit(solution)/shard_map/cond/branch_2_fun/ppermute | solution.py:402
  52.9 24.9 %collective-permute-start.101 = (f32[248,128]{1,0:T(8,128)}, f32[248,128]{1,0:T(8,128)S(1)}, u32[]{:S(2)}, u32[]{:S(2)}) collective-permute-start(f32[248,128]{1,0:T(8,128)} %get-tuple-element.171), channel_id=1, source_target_pairs={{0,14},{1,15},{2,12},{3,13},{4,10},{5,11},{6,8},{7,9},{8,6},{9,7},... | collective-permute-start | bytes 380936 | tf_op jit(solution)/shard_map/cond/branch_2_fun/ppermute | solution.py:402
  57.4 31.5 %collective-permute-start.102 = (f32[248,128]{1,0:T(8,128)}, f32[248,128]{1,0:T(8,128)S(1)}, u32[]{:S(2)}, u32[]{:S(2)}) collective-permute-start(f32[248,128]{1,0:T(8,128)} %get-tuple-element.172), channel_id=1, source_target_pairs={{0,15},{1,14},{2,13},{3,12},{4,11},{5,10},{6,9},{7,8},{8,7},{9,6},... | collective-permute-start | bytes 380936 | tf_op jit(solution)/shard_map/cond/branch_2_fun/ppermute | solution.py:402
  61.0 32.1 %collective-permute-start.103 = (f32[248,128]{1,0:T(8,128)}, f32[248,128]{1,0:T(8,128)S(1)}, u32[]{:S(2)}, u32[]{:S(2)}) collective-permute-start(f32[248,128]{1,0:T(8,128)} %get-tuple-element.173), channel_id=1, source_target_pairs={{0,20},{1,21},{2,22},{3,23},{4,16},{5,17},{6,18},{7,19},{8,28},{9,... | collective-permute-start | bytes 380936 | tf_op jit(solution)/shard_map/cond/branch_2_fun/ppermute | solution.py:402
  71.4 25.1 %collective-permute-start.104 = (f32[248,128]{1,0:T(8,128)}, f32[248,128]{1,0:T(8,128)S(1)}, u32[]{:S(2)}, u32[]{:S(2)}) collective-permute-start(f32[248,128]{1,0:T(8,128)} %get-tuple-element.174), channel_id=1, source_target_pairs={{0,21},{1,20},{2,23},{3,22},{4,17},{5,16},{6,19},{7,18},{8,29},{9,... | collective-permute-start | bytes 380936 | tf_op jit(solution)/shard_map/cond/branch_2_fun/ppermute | solution.py:402
  78.5 68.9 %collective-permute-start.106 = (f32[248,128]{1,0:T(8,128)}, f32[248,128]{1,0:T(8,128)S(1)}, u32[]{:S(2)}, u32[]{:S(2)}) collective-permute-start(f32[248,128]{1,0:T(8,128)} %get-tuple-element.176), channel_id=1, source_target_pairs={{0,23},{1,22},{2,21},{3,20},{4,19},{5,18},{6,17},{7,16},{8,31},{9,... | collective-permute-start | bytes 380936 | tf_op jit(solution)/shard_map/cond/branch_2_fun/ppermute | solution.py:402
  89.5 159.3 %collective-permute-start.111 = (f32[2056,128]{1,0:T(8,128)}, f32[2056,128]{1,0:T(8,128)S(1)}, u32[]{:S(2)}, u32[]{:S(2)}) collective-permute-start(f32[2056,128]{1,0:T(8,128)} %get-tuple-element.181), channel_id=1, source_target_pairs={{0,4},{1,5},{2,6},{3,7},{4,0},{5,1},{6,2},{7,3},{8,12},{9,13},{10,... | collective-permute-start | bytes 3158024 | tf_op jit(solution)/shard_map/cond/branch_2_fun/ppermute | solution.py:402
  93.8 155.2 %collective-permute-start.112 = (f32[2056,128]{1,0:T(8,128)}, f32[2056,128]{1,0:T(8,128)S(1)}, u32[]{:S(2)}, u32[]{:S(2)}) collective-permute-start(f32[2056,128]{1,0:T(8,128)} %get-tuple-element.182), channel_id=1, source_target_pairs={{0,6},{1,7},{2,4},{3,5},{4,2},{5,3},{6,0},{7,1},{8,14},{9,15},{10,... | collective-permute-start | bytes 3158024 | tf_op jit(solution)/shard_map/cond/branch_2_fun/ppermute | solution.py:402
  96.5 103.5 %collective-permute-start.107 = (f32[248,128]{1,0:T(8,128)S(1)}, f32[248,128]{1,0:T(8,128)S(1)}, u32[]{:S(2)}, u32[]{:S(2)}) collective-permute-start(f32[248,128]{1,0:T(8,128)S(1)} %copy-done.130), channel_id=1, source_target_pairs={{0,28},{1,29},{2,30},{3,31},{4,24},{5,25},{6,26},{7,27},{8,20},{9,... | collective-permute-start | bytes 380936 | tf_op jit(solution)/shard_map/cond/branch_2_fun/ppermute | solution.py:402
  97.1 106.0 %collective-permute-start.108 = (f32[248,128]{1,0:T(8,128)}, f32[248,128]{1,0:T(8,128)S(1)}, u32[]{:S(2)}, u32[]{:S(2)}) collective-permute-start(f32[248,128]{1,0:T(8,128)} %get-tuple-element.178), channel_id=1, source_target_pairs={{0,29},{1,28},{2,31},{3,30},{4,25},{5,24},{6,27},{7,26},{8,21},{9,... | collective-permute-start | bytes 380936 | tf_op jit(solution)/shard_map/cond/branch_2_fun/ppermute | solution.py:402
  147.4 67.8 %collective-permute-start.80 = (f32[656,128]{1,0:T(8,128)}, f32[656,128]{1,0:T(8,128)S(1)}, u32[]{:S(2)}, u32[]{:S(2)}) collective-permute-start(f32[656,128]{1,0:T(8,128)} %get-tuple-element.150), channel_id=1, source_target_pairs={{0,1},{1,0},{2,3},{3,2},{4,5},{5,4},{6,7},{7,6},{8,9},{9,8},{10,11... | collective-permute-start | bytes 1007624 | tf_op jit(solution)/shard_map/cond/branch_2_fun/ppermute | solution.py:402
  235.7 23.1 %collective-permute-start.87 = (f32[656,128]{1,0:T(8,128)}, f32[656,128]{1,0:T(8,128)}, u32[]{:S(2)}, u32[]{:S(2)}) collective-permute-start(f32[656,128]{1,0:T(8,128)} %get-tuple-element.157), channel_id=1, source_target_pairs={{0,16},{1,17},{2,18},{3,19},{4,20},{5,21},{6,22},{7,23},{8,24},{9,... | collective-permute-start | bytes 1007624 | tf_op jit(solution)/shard_map/cond/branch_2_fun/ppermute | solution.py:402
  238.4 21.5 %collective-permute-start.88 = (f32[656,128]{1,0:T(8,128)}, f32[656,128]{1,0:T(8,128)}, u32[]{:S(2)}, u32[]{:S(2)}) collective-permute-start(f32[656,128]{1,0:T(8,128)} %get-tuple-element.158), channel_id=1, source_target_pairs={{0,17},{1,16},{2,19},{3,18},{4,21},{5,20},{6,23},{7,22},{8,25},{9,... | collective-permute-start | bytes 1007624 | tf_op jit(solution)/shard_map/cond/branch_2_fun/ppermute | solution.py:402
  248.9 20.0 %collective-permute-start.90 = (f32[656,128]{1,0:T(8,128)}, f32[656,128]{1,0:T(8,128)}, u32[]{:S(2)}, u32[]{:S(2)}) collective-permute-start(f32[656,128]{1,0:T(8,128)} %get-tuple-element.160), channel_id=1, source_target_pairs={{0,19},{1,18},{2,17},{3,16},{4,23},{5,22},{6,21},{7,20},{8,27},{9,... | collective-permute-start | bytes 1007624 | tf_op jit(solution)/shard_map/cond/branch_2_fun/ppermute | solution.py:402
  249.0 42.4 %collective-permute-start.91 = (f32[656,128]{1,0:T(8,128)}, f32[656,128]{1,0:T(8,128)}, u32[]{:S(2)}, u32[]{:S(2)}) collective-permute-start(f32[656,128]{1,0:T(8,128)} %get-tuple-element.161), channel_id=1, source_target_pairs={{0,24},{1,25},{2,26},{3,27},{4,28},{5,29},{6,30},{7,31},{8,16},{9,... | collective-permute-start | bytes 1007624 | tf_op jit(solution)/shard_map/cond/branch_2_fun/ppermute | solution.py:402
  258.9 45.4 %collective-permute-start.113 = (f32[824,128]{1,0:T(8,128)}, f32[824,128]{1,0:T(8,128)S(1)}, u32[]{:S(2)}, u32[]{:S(2)}) collective-permute-start(f32[824,128]{1,0:T(8,128)} %get-tuple-element.184), channel_id=1, source_target_pairs={{0,1},{1,0},{2,3},{3,2},{4,5},{5,4},{6,7},{7,6},{8,9},{9,8},{10,11... | collective-permute-start | bytes 1265672 | tf_op jit(solution)/shard_map/cond/branch_2_fun/ppermute | solution.py:402
  260.0 46.3 %collective-permute-start.114 = (f32[824,128]{1,0:T(8,128)}, f32[824,128]{1,0:T(8,128)S(1)}, u32[]{:S(2)}, u32[]{:S(2)}) collective-permute-start(f32[824,128]{1,0:T(8,128)} %get-tuple-element.185), channel_id=1, source_target_pairs={{0,8},{1,9},{2,10},{3,11},{4,12},{5,13},{6,14},{7,15},{8,0},{9,1},... | collective-permute-start | bytes 1265672 | tf_op jit(solution)/shard_map/cond/branch_2_fun/ppermute | solution.py:402
  261.6 30.4 %collective-permute-start.92 = (f32[656,128]{1,0:T(8,128)}, f32[656,128]{1,0:T(8,128)S(1)}, u32[]{:S(2)}, u32[]{:S(2)}) collective-permute-start(f32[656,128]{1,0:T(8,128)} %get-tuple-element.162), channel_id=1, source_target_pairs={{0,25},{1,24},{2,27},{3,26},{4,29},{5,28},{6,31},{7,30},{8,17},{9,... | collective-permute-start | bytes 1007624 | tf_op jit(solution)/shard_map/cond/branch_2_fun/ppermute | solution.py:402
  268.9 24.8 %collective-permute-start.93 = (f32[656,128]{1,0:T(8,128)}, f32[656,128]{1,0:T(8,128)S(1)}, u32[]{:S(2)}, u32[]{:S(2)}) collective-permute-start(f32[656,128]{1,0:T(8,128)} %get-tuple-element.163), channel_id=1, source_target_pairs={{0,26},{1,27},{2,24},{3,25},{4,30},{5,31},{6,28},{7,29},{8,18},{9,... | collective-permute-start | bytes 1007624 | tf_op jit(solution)/shard_map/cond/branch_2_fun/ppermute | solution.py:402
  304.3 35.5 %collective-permute-start.118 = (f32[824,128]{1,0:T(8,128)}, f32[824,128]{1,0:T(8,128)S(1)}, u32[]{:S(2)}, u32[]{:S(2)}) collective-permute-start(f32[824,128]{1,0:T(8,128)} %get-tuple-element.189), channel_id=1, source_target_pairs={{0,24},{1,25},{2,26},{3,27},{4,28},{5,29},{6,30},{7,31},{8,16},{9,... | collective-permute-start | bytes 1265672 | tf_op jit(solution)/shard_map/cond/branch_2_fun/ppermute | solution.py:402
  306.3 33.5 %collective-permute-start.119 = (f32[824,128]{1,0:T(8,128)}, f32[824,128]{1,0:T(8,128)S(1)}, u32[]{:S(2)}, u32[]{:S(2)}) collective-permute-start(f32[824,128]{1,0:T(8,128)} %get-tuple-element.190), channel_id=1, source_target_pairs={{0,25},{1,24},{2,27},{3,26},{4,29},{5,28},{6,31},{7,30},{8,17},{9,... | collective-permute-start | bytes 1265672 | tf_op jit(solution)/shard_map/cond/branch_2_fun/ppermute | solution.py:402
  (54 other events, 1689.5 us)
